TPU v7x, 256 devices: a whole 4x4x8 slice. The times are simulated.
256 devices in a mesh: cuts: 8 (over z_lo, core), tile: 2 (over z_hi), probe: 16 (over x, y).
Axes of the slice: x: 4, y: 4, z: 8 (z_hi: 2, z_lo: 4; z = z_hi * 4 + z_lo), core: 2. Of those that a mesh axis runs over, the one named last changes fastest.
Arguments:
- probe_wave: bfloat16 [2, 512, 512], replicated, may hold values from -6 to 6
- fresnel_rows: bfloat16 [2, 512, 512], replicated, may hold values from -0.1875 to 0.1875
- fresnel_cols: bfloat16 [2, 512, 512], replicated, may hold values from -0.1875 to 0.1875
- object_slices: float32 [8, 2, 1024, 768], P('cuts', None, 'tile'), may hold values from -1 to 1.9, as said below
- offsets: int32 [2, 32, 2], P('tile', 'probe'), may hold values from 0 to 256
- measured: float32 [2, 32, 512, 512], P('tile', 'probe'), may hold values from 0.2 to 2
Outputs:
- updated_object: float32 [8, 2, 1024, 768], P('cuts', None, ('tile', 'probe'))
Inputs may be any that keep to these rules, and one draw needn't show every extreme that they name: `object_slices`: real and imaginary parts of each slice's transmission.
All inputs are finite; a program needn't handle non-finite values.
Results may differ from a plain program's by a relative error of at most 0.02.
Values may be sent and summed in bfloat16 or wider, within the bound.
A program may use at most 128 MiB of HBM per device.

v0:
```python
import jax
import jax.numpy as jnp
from jax import lax
from jax.sharding import Mesh
from jax.sharding import PartitionSpec as P

MARGIN = 128
PROBE = ("probe_0", "probe_1")
TILE_PROBE = ("tile", "probe_0", "probe_1")


def extended_2(x, sides, width):
    for axis, dim in sides:
        count, length = (lax.axis_size(axis), x.shape[dim])
        up = [(i, (i + 1) % count) for i in range(count)]
        down = [(j, i) for i, j in up]
        last = lax.slice_in_dim(x, length - width, length, axis=dim)
        leading = lax.slice_in_dim(x, 0, width, axis=dim)
        before = lax.ppermute(last, axis, up)
        after = lax.ppermute(leading, axis, down)
        x = jnp.concatenate([before, x, after], axis=dim)
    return x


def passed_along(x, axis, by):
    count = lax.axis_size(axis)
    pairs = [(i, i + by) for i in range(count) if 0 <= i + by < count]
    return lax.ppermute(x, axis, pairs)


def sum_by_axis(x, axes, dim):
    for axis in axes:
        x = lax.psum_scatter(x, axis, scatter_dimension=dim, tiled=True)
    return x


def complex_mul(left_side, right_side):
    return jnp.stack(
        [
            left_side[:, 0] * right_side[:, 0] - left_side[:, 1] * right_side[:, 1],
            left_side[:, 0] * right_side[:, 1] + left_side[:, 1] * right_side[:, 0],
        ],
        axis=1,
    )


def conj_mul(left_side, right_side):
    return jnp.stack(
        [
            left_side[:, 0] * right_side[:, 0] + left_side[:, 1] * right_side[:, 1],
            left_side[:, 0] * right_side[:, 1] - left_side[:, 1] * right_side[:, 0],
        ],
        axis=1,
    )


def times_transposed(stacked, matrix):
    return lax.dot_general(
        stacked, matrix, (((1,), (1,)), ((), ())), preferred_element_type=jnp.float32
    )


def forward_apply(wave, col_real, col_imag, left_block):
    size = wave.shape[1]
    stacked = wave.reshape(2 * size, size)
    with_real = times_transposed(stacked, col_real)
    with_imag = times_transposed(stacked, col_imag)
    mid_real = with_real[:size] - with_imag[size:]
    mid_imag = with_imag[:size] + with_real[size:]
    middle = jnp.concatenate([mid_real, mid_imag], axis=0).astype(jnp.bfloat16)
    result = jnp.dot(left_block, middle, preferred_element_type=jnp.float32)
    return result.astype(jnp.bfloat16).reshape(2, size, size)


def adjoint_apply(wave, col_real, col_imag, left_block):
    size = wave.shape[1]
    stacked = wave.reshape(2 * size, size)
    with_real = jnp.dot(stacked, col_real, preferred_element_type=jnp.float32)
    with_imag = jnp.dot(stacked, col_imag, preferred_element_type=jnp.float32)
    mid_real = with_real[:size] + with_imag[size:]
    mid_imag = with_real[size:] - with_imag[:size]
    middle = jnp.concatenate([mid_real, mid_imag], axis=0).astype(jnp.bfloat16)
    result = jnp.dot(left_block, middle, preferred_element_type=jnp.float32)
    return result.astype(jnp.bfloat16).reshape(2, size, size)


def shards(probe_wave, fresnel_rows, fresnel_cols, object_slices, offsets, measured):
    cut_count = lax.axis_size("cuts")
    section_index = lax.axis_index("cuts")
    owned = object_slices[0]
    own_count = owned.shape[1]
    width_cols = owned.shape[2]
    window_size = probe_wave.shape[1]
    transmission = owned.astype(jnp.bfloat16)
    extended = extended_2(transmission, (("tile", 1),), MARGIN)
    starts = offsets[0]
    position_count = starts.shape[0]

    def cut_window(row_start, col_start):
        return lax.dynamic_slice(
            extended, (jnp.int32(0), row_start, col_start), (2, window_size, window_size)
        )

    windows = jax.vmap(cut_window)(starts[:, 0], starts[:, 1])
    row_real, row_imag = (fresnel_rows[0], fresnel_rows[1])
    col_real, col_imag = (fresnel_cols[0], fresnel_cols[1])
    forward_left = jnp.concatenate(
        [
            jnp.concatenate([row_real, -row_imag], axis=1),
            jnp.concatenate([row_imag, row_real], axis=1),
        ],
        axis=0,
    )
    adjoint_left = jnp.concatenate(
        [
            jnp.concatenate([row_real.T, row_imag.T], axis=1),
            jnp.concatenate([-row_imag.T, row_real.T], axis=1),
        ],
        axis=0,
    )
    wave_shape = (2, window_size, window_size)
    tick_count = cut_count + position_count - 1
    last_section = cut_count - 1

    def advance(wave, window):
        exits = complex_mul(
            wave[None].astype(jnp.float32), window[None].astype(jnp.float32)
        ).astype(jnp.bfloat16)
        return forward_apply(exits[0], col_real, col_imag, forward_left)

    def standby(wave, window):
        return jnp.zeros_like(wave)

    def forward_tick(tick, carry):
        incoming, saved, finals = carry
        position = tick - section_index
        valid = (position >= 0) & (position < position_count)
        slot = jnp.clip(position, 0, position_count - 1)
        wave_in = jnp.where(section_index == 0, probe_wave, incoming)
        window = lax.dynamic_index_in_dim(windows, slot, 0, keepdims=False)
        produced = lax.cond(valid, advance, standby, wave_in, window)
        previous = lax.dynamic_index_in_dim(saved, slot, 0, keepdims=False)
        saved = lax.dynamic_update_index_in_dim(saved, jnp.where(valid, wave_in, previous), slot, 0)
        earlier = lax.dynamic_index_in_dim(finals, slot, 0, keepdims=False)
        keep_final = valid & (section_index == last_section)
        finals = lax.dynamic_update_index_in_dim(
            finals, jnp.where(keep_final, produced, earlier), slot, 0
        )
        incoming = passed_along(produced, "cuts", 1)
        return (incoming, saved, finals)

    start_wave = jnp.zeros(wave_shape, jnp.bfloat16)
    stack_zeros = jnp.zeros((position_count,) + wave_shape, jnp.bfloat16)
    _, saved, finals = lax.fori_loop(
        0, tick_count, forward_tick, (start_wave, stack_zeros, stack_zeros)
    )
    psi_final = finals.astype(jnp.float32)
    amplitude = measured[0]
    factor = 1.0 - amplitude / jnp.sqrt(psi_final[:, 0] ** 2 + psi_final[:, 1] ** 2 + 1.0)
    final_cots = (psi_final * factor[:, None]).astype(jnp.bfloat16)

    def retreat(cotangent, window, wave_before):
        backed = adjoint_apply(cotangent, col_real, col_imag, adjoint_left)[None].astype(
            jnp.float32
        )
        incoming = wave_before[None].astype(jnp.float32)
        gradient_term = conj_mul(incoming, backed)[0]
        intensity = incoming[0, 0] ** 2 + incoming[0, 1] ** 2
        sending = conj_mul(window[None].astype(jnp.float32), backed).astype(jnp.bfloat16)[0]
        return (sending, gradient_term, intensity)

    def resting(cotangent, window, wave_before):
        zeros_wave = jnp.zeros(wave_shape, jnp.float32)
        zeros_light = jnp.zeros((window_size, window_size), jnp.float32)
        return (jnp.zeros_like(cotangent), zeros_wave, zeros_light)

    def backward_tick(tick, carry):
        incoming, gradient_total, light_total = carry
        position = tick - (last_section - section_index)
        valid = (position >= 0) & (position < position_count)
        slot = jnp.clip(position, 0, position_count - 1)
        own_cot = lax.dynamic_index_in_dim(final_cots, slot, 0, keepdims=False)
        cot_in = jnp.where(section_index == last_section, own_cot, incoming)
        window = lax.dynamic_index_in_dim(windows, slot, 0, keepdims=False)
        wave_before = lax.dynamic_index_in_dim(saved, slot, 0, keepdims=False)
        sending, gradient_term, intensity = lax.cond(
            valid, retreat, resting, cot_in, window, wave_before
        )
        gradient_old = lax.dynamic_index_in_dim(gradient_total, slot, 0, keepdims=False)
        gradient_total = lax.dynamic_update_index_in_dim(
            gradient_total, gradient_old + gradient_term, slot, 0
        )
        light_old = lax.dynamic_index_in_dim(light_total, slot, 0, keepdims=False)
        light_total = lax.dynamic_update_index_in_dim(light_total, light_old + intensity, slot, 0)
        incoming = passed_along(sending, "cuts", -1)
        return (incoming, gradient_total, light_total)

    gradient_start = jnp.zeros((position_count,) + wave_shape, jnp.float32)
    light_start = jnp.zeros((position_count, window_size, window_size), jnp.float32)
    _, gradient_total, light_total = lax.fori_loop(
        0, tick_count, backward_tick, (start_wave, gradient_start, light_start)
    )
    pieces = jnp.concatenate([gradient_total, light_total[:, None]], axis=1)
    accum_grid = jnp.zeros((3, own_count + 2 * MARGIN, width_cols), jnp.float32)
    for position in range(position_count):
        anchor = (jnp.int32(0), starts[position, 0], starts[position, 1])
        current_block = lax.dynamic_slice(accum_grid, anchor, (3, window_size, window_size))
        accum_grid = lax.dynamic_update_slice(accum_grid, current_block + pieces[position], anchor)
    edged = extended_2(accum_grid.astype(jnp.bfloat16), (("tile", 1),), MARGIN).astype(
        accum_grid.dtype
    )
    inside = accum_grid[:, MARGIN : MARGIN + own_count]
    upper_rows = inside[:, :MARGIN] + edged[:, :MARGIN]
    lower_rows = inside[:, own_count - MARGIN :] + edged[:, edged.shape[1] - MARGIN :]
    folded = jnp.concatenate(
        [upper_rows, inside[:, MARGIN : own_count - MARGIN], lower_rows], axis=1
    )
    summed = sum_by_axis(folded.astype(jnp.bfloat16), PROBE, 1).astype(jnp.float32)
    rows_each = summed.shape[1]
    own_part = lax.dynamic_slice_in_dim(owned, lax.axis_index(PROBE) * rows_each, rows_each, 1)
    updated = own_part - summed[:2] / (summed[2] + 1.0)
    return updated[None]


def solution(mesh):
    split = Mesh(
        mesh.devices.reshape(mesh.shape["cuts"], mesh.shape["tile"], 4, 4),
        ("cuts", "tile", "probe_0", "probe_1"),
    )
    return jax.shard_map(
        shards,
        mesh=split,
        in_specs=(
            P(),
            P(),
            P(),
            P("cuts", None, "tile", None),
            P("tile", PROBE, None),
            P("tile", PROBE, None, None),
        ),
        out_specs=P("cuts", None, TILE_PROBE, None),
        check_vma=False,
    )
```

profile of v0, /device:TPU:8, one launch (start us, length us, event | category | flops | bytes accessed | tf_op | source)
XLA Modules:
  0.0 743.1 jit_solution(7299210738483616082)
XLA Ops:
  38.2 12.1 %collective-permute-done.3 = bf16[2,128,768]{2,1,0:T(8,128)(2,1)} collective-permute-done((bf16[2,128,768]{2,1,0:T(8,128)(2,1)}, bf16[2,128,768]{2,1,0:T(8,128)(2,1)}, u32[]{:S(2)}, u32[]{:S(2)}) %collective-permute-start.3) | collective-permute-done | bytes 393248 | tf_op jit(solution)/shard_map/ppermute | solution.py:20
  64.8 232.0 %while.38 = (s32[]{:T(128)}, bf16[2,512,512]{1,0,2:T(2,128)(2,1)}, bf16[2,2,512,512]{3,2,1,0:T(8,128)(2,1)}, bf16[2,2,512,512]{3,2,1,0:T(8,128)(2,1)}, s32[]{:T(...) while((s32[]{:T(128)}, bf16[2,512,512]{1,0,2:T(2,128)(2,1)}, ...), condition=%wide.region_3.4_spmd, body=%wide.region_0.3_spmd.sunk | while | flops 2156396544 | bytes 72352600 | solution.py:154
  70.8 11.2 %conditional.4 = (bf16[2,512,512]{1,0,2:T(2,128)(2,1)S(1)}) conditional(s32[]{:T(128)} %convert_element_type.147, () %tuple.129, (bf16[2,512,512]{1,0,2:T(2,128)(2,1)S(1)}, bf16[2,2,512,512]{3,2,1,0:T(8,128)(2,1)}, s32[]{:T(128)}, bf16[512,512]{1,0:T(8,128)(2,1)}, bf16[512,512]{1,0:T(8,128)(2,1)}, /*index=5*/bf16[1024,1024]{1,0:T(8,128)(2,1)}) %tuple.130), branch_computations={%region_1.1_spmd, %region_2.2_spmd} | conditional | flops 2154823680 | bytes 42991656 | solution.py:141
  99.1 11.2 %conditional.4 = (bf16[2,512,512]{1,0,2:T(2,128)(2,1)S(1)}) conditional(s32[]{:T(128)} %convert_element_type.147, () %tuple.129, (bf16[2,512,512]{1,0,2:T(2,128)(2,1)S(1)}, bf16[2,2,512,512]{3,2,1,0:T(8,128)(2,1)}, s32[]{:T(128)}, bf16[512,512]{1,0:T(8,128)(2,1)}, bf16[512,512]{1,0:T(8,128)(2,1)}, /*index=5*/bf16[1024,1024]{1,0:T(8,128)(2,1)}) %tuple.130), branch_computations={%region_1.1_spmd, %region_2.2_spmd} | conditional | flops 2154823680 | bytes 42991656 | solution.py:141
  128.1 10.6 %collective-permute-start = (bf16[2,512,512]{1,0,2:T(2,128)(2,1)S(1)}, bf16[2,512,512]{1,0,2:T(2,128)(2,1)}, u32[]{:S(2)}, u32[]{:S(2)}) collective-permute-start(bf16[2,512,512]{1,0,2:T(2,128)(2,1)S(1)} %get-tuple-element.1083), channel_id=1, source_target_pairs={{0,32},{32,64},{64,96},{96,128},{128,160},{160,192},{192,224},{1,3... | collective-permute-start | bytes 3145736 | tf_op jit(solution)/shard_map/while/body/eval_jaxpr/ppermute | solution.py:28
  176.9 18.1 %collective-permute-start = (bf16[2,512,512]{1,0,2:T(2,128)(2,1)S(1)}, bf16[2,512,512]{1,0,2:T(2,128)(2,1)}, u32[]{:S(2)}, u32[]{:S(2)}) collective-permute-start(bf16[2,512,512]{1,0,2:T(2,128)(2,1)S(1)} %get-tuple-element.1083), channel_id=1, source_target_pairs={{0,32},{32,64},{64,96},{96,128},{128,160},{160,192},{192,224},{1,3... | collective-permute-start | bytes 3145736 | tf_op jit(solution)/shard_map/while/body/eval_jaxpr/ppermute | solution.py:28
  210.4 7.4 collective-permute-start
  278.8 9.2 %collective-permute-start = (bf16[2,512,512]{1,0,2:T(2,128)(2,1)S(1)}, bf16[2,512,512]{1,0,2:T(2,128)(2,1)}, u32[]{:S(2)}, u32[]{:S(2)}) collective-permute-start(bf16[2,512,512]{1,0,2:T(2,128)(2,1)S(1)} %get-tuple-element.1083), channel_id=1, source_target_pairs={{0,32},{32,64},{64,96},{96,128},{128,160},{160,192},{192,224},{1,3... | collective-permute-start | bytes 3145736 | tf_op jit(solution)/shard_map/while/body/eval_jaxpr/ppermute | solution.py:28
  307.7 266.0 %while.39 = (s32[]{:T(128)}, bf16[2,512,512]{2,1,0:T(8,128)(2,1)}, f32[2,2,512,512]{3,2,1,0:T(8,128)}, f32[2,512,512]{2,1,0:T(8,128)}, s32[]{:T(128)}, /*index=5...) while((s32[]{:T(128)}, bf16[2,512,512]{2,1,0:T(8,128)(2,1)}, ...), condition=%wide.region_7.8_spmd, body=%wide.region_4.7_spmd.sunk | while | flops 2159542272 | bytes 118489544 | solution.py:200
  330.9 8.5 %collective-permute-done.1 = bf16[2,512,512]{2,1,0:T(8,128)(2,1)} collective-permute-done((bf16[2,512,512]{2,1,0:T(8,128)(2,1)}, bf16[2,512,512]{2,1,0:T(8,128)(2,1)}, u32[]{:S(2)}, u32[]{:S(2)}) %collective-permute-start.1) | collective-permute-done | bytes 1048608 | tf_op jit(solution)/shard_map/while/body/eval_jaxpr/ppermute | solution.py:28
  350.1 8.6 %collective-permute-done.1 = bf16[2,512,512]{2,1,0:T(8,128)(2,1)} collective-permute-done((bf16[2,512,512]{2,1,0:T(8,128)(2,1)}, bf16[2,512,512]{2,1,0:T(8,128)(2,1)}, u32[]{:S(2)}, u32[]{:S(2)}) %collective-permute-start.1) | collective-permute-done | bytes 1048608 | tf_op jit(solution)/shard_map/while/body/eval_jaxpr/ppermute | solution.py:28
  369.3 8.6 %collective-permute-done.1 = bf16[2,512,512]{2,1,0:T(8,128)(2,1)} collective-permute-done((bf16[2,512,512]{2,1,0:T(8,128)(2,1)}, bf16[2,512,512]{2,1,0:T(8,128)(2,1)}, u32[]{:S(2)}, u32[]{:S(2)}) %collective-permute-start.1) | collective-permute-done | bytes 1048608 | tf_op jit(solution)/shard_map/while/body/eval_jaxpr/ppermute | solution.py:28
  388.5 8.6 %collective-permute-done.1 = bf16[2,512,512]{2,1,0:T(8,128)(2,1)} collective-permute-done((bf16[2,512,512]{2,1,0:T(8,128)(2,1)}, bf16[2,512,512]{2,1,0:T(8,128)(2,1)}, u32[]{:S(2)}, u32[]{:S(2)}) %collective-permute-start.1) | collective-permute-done | bytes 1048608 | tf_op jit(solution)/shard_map/while/body/eval_jaxpr/ppermute | solution.py:28
  407.8 8.6 %collective-permute-done.1 = bf16[2,512,512]{2,1,0:T(8,128)(2,1)} collective-permute-done((bf16[2,512,512]{2,1,0:T(8,128)(2,1)}, bf16[2,512,512]{2,1,0:T(8,128)(2,1)}, u32[]{:S(2)}, u32[]{:S(2)}) %collective-permute-start.1) | collective-permute-done | bytes 1048608 | tf_op jit(solution)/shard_map/while/body/eval_jaxpr/ppermute | solution.py:28
  427.0 85.4 %collective-permute-done.1 = bf16[2,512,512]{2,1,0:T(8,128)(2,1)} collective-permute-done((bf16[2,512,512]{2,1,0:T(8,128)(2,1)}, bf16[2,512,512]{2,1,0:T(8,128)(2,1)}, u32[]{:S(2)}, u32[]{:S(2)}) %collective-permute-start.1) | collective-permute-done | bytes 1048608 | tf_op jit(solution)/shard_map/while/body/eval_jaxpr/ppermute | solution.py:28
  512.4 17.5 %conditional.5 = (bf16[2,512,512]{2,1,0:T(8,128)(2,1)}, f32[2,512,512]{2,1,0:T(8,128)}, f32[512,512]{1,0:T(8,128)S(1)}) conditional(s32[]{:T(128)} %convert_element_type.148, () %tuple.132, (bf16[2,2,512,512]{3,2,1,0:T(8,128)(2,1)}, s32[]{:T(128)}, pred[]{:T(512)}, bf16[2,2,512,512]{3,2,1,0:T(8,128)(2,1)}, bf16[2,512,512]{2,1,0:T(8,128)(2,1)}, ...), branch_computations={%region_5.5_spmd, %region_6.6_spmd} | conditional | flops 2158755840 | bytes 48234528 | solution.py:186
  537.7 8.6 %collective-permute-done.1 = bf16[2,512,512]{2,1,0:T(8,128)(2,1)} collective-permute-done((bf16[2,512,512]{2,1,0:T(8,128)(2,1)}, bf16[2,512,512]{2,1,0:T(8,128)(2,1)}, u32[]{:S(2)}, u32[]{:S(2)}) %collective-permute-start.1) | collective-permute-done | bytes 1048608 | tf_op jit(solution)/shard_map/while/body/eval_jaxpr/ppermute | solution.py:28
  546.3 17.5 %conditional.5 = (bf16[2,512,512]{2,1,0:T(8,128)(2,1)}, f32[2,512,512]{2,1,0:T(8,128)}, f32[512,512]{1,0:T(8,128)S(1)}) conditional(s32[]{:T(128)} %convert_element_type.148, () %tuple.132, (bf16[2,2,512,512]{3,2,1,0:T(8,128)(2,1)}, s32[]{:T(128)}, pred[]{:T(512)}, bf16[2,2,512,512]{3,2,1,0:T(8,128)(2,1)}, bf16[2,512,512]{2,1,0:T(8,128)(2,1)}, ...), branch_computations={%region_5.5_spmd, %region_6.6_spmd} | conditional | flops 2158755840 | bytes 48234528 | solution.py:186
  580.9 21.9 %dynamic_update_slice.43 = f32[3,768,768]{2,1,0:T(8,128)} dynamic-update-slice(f32[3,768,768]{2,1,0:T(8,128)} %broadcast_in_dim.60, f32[3,512,512]{2,1,0:T(8,128)} %fusion.18, s32[]{:T(128)} %constant.155.clone.1, s32[]{:T(128)S(6)} %select_n.122, s32[]{:T(128)S(6)} %select_n.123) | dynamic-update-slice | bytes 6291460 | tf_op jit(solution)/shard_map/dynamic_update_slice | solution.py:208
  608.1 21.6 %dynamic_update_slice.44 = f32[3,768,768]{2,1,0:T(8,128)} dynamic-update-slice(f32[3,768,768]{2,1,0:T(8,128)} %dynamic_update_slice.43, f32[3,512,512]{2,1,0:T(8,128)} %fusion.20, s32[]{:T(128)} %constant.155.clone.1, s32[]{:T(128)S(6)} %select_n.124, s32[]{:T(128)S(6)} %select_n.125) | dynamic-update-slice | bytes 6291460 | tf_op jit(solution)/shard_map/dynamic_update_slice | solution.py:208
  639.3 22.7 %collective-permute-done.4 = bf16[3,128,768]{2,1,0:T(8,128)(2,1)S(1)} collective-permute-done((bf16[3,128,768]{2,1,0:T(8,128)(2,1)S(1)}, bf16[3,128,768]{2,1,0:T(8,128)(2,1)S(1)}, u32[]{:S(2)}, u32[]{:S(2)}) %collective-permute-start.4) | collective-permute-done | bytes 589856 | tf_op jit(solution)/shard_map/ppermute | solution.py:19
  661.9 12.6 %collective-permute-done.5 = bf16[3,128,768]{2,1,0:T(8,128)(2,1)S(1)} collective-permute-done((bf16[3,128,768]{2,1,0:T(8,128)(2,1)S(1)}, bf16[3,128,768]{2,1,0:T(8,128)(2,1)S(1)}, u32[]{:S(2)}, u32[]{:S(2)}) %collective-permute-start.5) | collective-permute-done | bytes 589856 | tf_op jit(solution)/shard_map/ppermute | solution.py:20
  678.1 30.9 %reduce-scatter.3.cloned.1.call-done = bf16[3,128,768]{2,1,0:T(8,128)(2,1)} async-done(((bf16[3,512,768]{2,1,0:T(8,128)(2,1)}), bf16[3,128,768]{2,1,0:T(8,128)(2,1)}) %reduce-scatter.3.cloned.1.call-update) | async-done | bytes 589840 | tf_op jit(solution)/shard_map/reduce_scatter | solution.py:33
  709.1 24.6 %reduce-scatter.5.cloned.1.call-done = bf16[3,32,768]{2,1,0:T(8,128)(2,1)} async-done(((bf16[3,128,768]{2,1,0:T(8,128)(2,1)}), bf16[3,32,768]{2,1,0:T(8,128)(2,1)}) %reduce-scatter.5.cloned.1.call-update) | async-done | bytes 147472 | tf_op jit(solution)/shard_map/reduce_scatter | solution.py:33
  (370 shorter events, 421.9 us)
Async XLA Ops:
  6.5 702.5 %reduce-scatter.3.cloned.1.call-start = ((), (), s32[]{:S(2)}) async-start(), calls=%async_computation.2 | async-start | bytes 2949120 | tf_op jit(solution)/shard_map/reduce_scatter | solution.py:33
  9.7 28.5 %collective-permute-start.2 = (bf16[2,128,768]{2,1,0:T(8,128)(2,1)}, bf16[2,128,768]{2,1,0:T(8,128)(2,1)S(1)}, u32[]{:S(2)}, u32[]{:S(2)}) collective-permute-start(bf16[2,128,768]{2,1,0:T(8,128)(2,1)} %get-tuple-element.771), channel_id=1, source_target_pairs={{0,16},{16,0},{1,17},{17,1},{2,18},{18,2},{3,19},{19,3},{4,20},{20... | collective-permute-start | bytes 1179656 | tf_op jit(solution)/shard_map/ppermute | solution.py:19
  16.9 33.4 %collective-permute-start.3 = (bf16[2,128,768]{2,1,0:T(8,128)(2,1)}, bf16[2,128,768]{2,1,0:T(8,128)(2,1)}, u32[]{:S(2)}, u32[]{:S(2)}) collective-permute-start(bf16[2,128,768]{2,1,0:T(8,128)(2,1)} %get-tuple-element.772), channel_id=1, source_target_pairs={{16,0},{0,16},{17,1},{1,17},{18,2},{2,18},{19,3},{3,19},{20,4},{4,... | collective-permute-start | bytes 1179656 | tf_op jit(solution)/shard_map/ppermute | solution.py:20
  82.1 11.1 %collective-permute-start = (bf16[2,512,512]{1,0,2:T(2,128)(2,1)S(1)}, bf16[2,512,512]{1,0,2:T(2,128)(2,1)}, u32[]{:S(2)}, u32[]{:S(2)}) collective-permute-start(bf16[2,512,512]{1,0,2:T(2,128)(2,1)S(1)} %get-tuple-element.1083), channel_id=1, source_target_pairs={{0,32},{32,64},{64,96},{96,128},{128,160},{160,192},{192,224},{1,3... | collective-permute-start | bytes 3145736 | tf_op jit(solution)/shard_map/while/body/eval_jaxpr/ppermute | solution.py:28
  110.4 11.1 %collective-permute-start = (bf16[2,512,512]{1,0,2:T(2,128)(2,1)S(1)}, bf16[2,512,512]{1,0,2:T(2,128)(2,1)}, u32[]{:S(2)}, u32[]{:S(2)}) collective-permute-start(bf16[2,512,512]{1,0,2:T(2,128)(2,1)S(1)} %get-tuple-element.1083), channel_id=1, source_target_pairs={{0,32},{32,64},{64,96},{96,128},{128,160},{160,192},{192,224},{1,3... | collective-permute-start | bytes 3145736 | tf_op jit(solution)/shard_map/while/body/eval_jaxpr/ppermute | solution.py:28
  128.1 19.5 %collective-permute-start = (bf16[2,512,512]{1,0,2:T(2,128)(2,1)S(1)}, bf16[2,512,512]{1,0,2:T(2,128)(2,1)}, u32[]{:S(2)}, u32[]{:S(2)}) collective-permute-start(bf16[2,512,512]{1,0,2:T(2,128)(2,1)S(1)} %get-tuple-element.1083), channel_id=1, source_target_pairs={{0,32},{32,64},{64,96},{96,128},{128,160},{160,192},{192,224},{1,3... | collective-permute-start | bytes 3145736 | tf_op jit(solution)/shard_map/while/body/eval_jaxpr/ppermute | solution.py:28
  154.1 16.2 %collective-permute-start = (bf16[2,512,512]{1,0,2:T(2,128)(2,1)S(1)}, bf16[2,512,512]{1,0,2:T(2,128)(2,1)}, u32[]{:S(2)}, u32[]{:S(2)}) collective-permute-start(bf16[2,512,512]{1,0,2:T(2,128)(2,1)S(1)} %get-tuple-element.1083), channel_id=1, source_target_pairs={{0,32},{32,64},{64,96},{96,128},{128,160},{160,192},{192,224},{1,3... | collective-permute-start | bytes 3145736 | tf_op jit(solution)/shard_map/while/body/eval_jaxpr/ppermute | solution.py:28
  176.9 26.9 %collective-permute-start = (bf16[2,512,512]{1,0,2:T(2,128)(2,1)S(1)}, bf16[2,512,512]{1,0,2:T(2,128)(2,1)}, u32[]{:S(2)}, u32[]{:S(2)}) collective-permute-start(bf16[2,512,512]{1,0,2:T(2,128)(2,1)S(1)} %get-tuple-element.1083), channel_id=1, source_target_pairs={{0,32},{32,64},{64,96},{96,128},{128,160},{160,192},{192,224},{1,3... | collective-permute-start | bytes 3145736 | tf_op jit(solution)/shard_map/while/body/eval_jaxpr/ppermute | solution.py:28
  210.4 16.2 %collective-permute-start = (bf16[2,512,512]{1,0,2:T(2,128)(2,1)S(1)}, bf16[2,512,512]{1,0,2:T(2,128)(2,1)}, u32[]{:S(2)}, u32[]{:S(2)}) collective-permute-start(bf16[2,512,512]{1,0,2:T(2,128)(2,1)S(1)} %get-tuple-element.1083), channel_id=1, source_target_pairs={{0,32},{32,64},{64,96},{96,128},{128,160},{160,192},{192,224},{1,3... | collective-permute-start | bytes 3145736 | tf_op jit(solution)/shard_map/while/body/eval_jaxpr/ppermute | solution.py:28
  233.2 16.2 %collective-permute-start = (bf16[2,512,512]{1,0,2:T(2,128)(2,1)S(1)}, bf16[2,512,512]{1,0,2:T(2,128)(2,1)}, u32[]{:S(2)}, u32[]{:S(2)}) collective-permute-start(bf16[2,512,512]{1,0,2:T(2,128)(2,1)S(1)} %get-tuple-element.1083), channel_id=1, source_target_pairs={{0,32},{32,64},{64,96},{96,128},{128,160},{160,192},{192,224},{1,3... | collective-permute-start | bytes 3145736 | tf_op jit(solution)/shard_map/while/body/eval_jaxpr/ppermute | solution.py:28
  256.0 16.2 %collective-permute-start = (bf16[2,512,512]{1,0,2:T(2,128)(2,1)S(1)}, bf16[2,512,512]{1,0,2:T(2,128)(2,1)}, u32[]{:S(2)}, u32[]{:S(2)}) collective-permute-start(bf16[2,512,512]{1,0,2:T(2,128)(2,1)S(1)} %get-tuple-element.1083), channel_id=1, source_target_pairs={{0,32},{32,64},{64,96},{96,128},{128,160},{160,192},{192,224},{1,3... | collective-permute-start | bytes 3145736 | tf_op jit(solution)/shard_map/while/body/eval_jaxpr/ppermute | solution.py:28
  278.8 18.0 %collective-permute-start = (bf16[2,512,512]{1,0,2:T(2,128)(2,1)S(1)}, bf16[2,512,512]{1,0,2:T(2,128)(2,1)}, u32[]{:S(2)}, u32[]{:S(2)}) collective-permute-start(bf16[2,512,512]{1,0,2:T(2,128)(2,1)S(1)} %get-tuple-element.1083), channel_id=1, source_target_pairs={{0,32},{32,64},{64,96},{96,128},{128,160},{160,192},{192,224},{1,3... | collective-permute-start | bytes 3145736 | tf_op jit(solution)/shard_map/while/body/eval_jaxpr/ppermute | solution.py:28
  310.5 8.9 %collective-permute-start.1 = (bf16[2,512,512]{2,1,0:T(8,128)(2,1)}, bf16[2,512,512]{2,1,0:T(8,128)(2,1)}, u32[]{:S(2)}, u32[]{:S(2)}) collective-permute-start(bf16[2,512,512]{2,1,0:T(8,128)(2,1)} %get-tuple-element.963), channel_id=1, source_target_pairs={{32,0},{64,32},{96,64},{128,96},{160,128},{192,160},{224,192},{33,... | collective-permute-start | bytes 3145736 | tf_op jit(solution)/shard_map/while/body/eval_jaxpr/ppermute | solution.py:28
  323.1 16.4 %collective-permute-start.1 = (bf16[2,512,512]{2,1,0:T(8,128)(2,1)}, bf16[2,512,512]{2,1,0:T(8,128)(2,1)}, u32[]{:S(2)}, u32[]{:S(2)}) collective-permute-start(bf16[2,512,512]{2,1,0:T(8,128)(2,1)} %get-tuple-element.963), channel_id=1, source_target_pairs={{32,0},{64,32},{96,64},{128,96},{160,128},{192,160},{224,192},{33,... | collective-permute-start | bytes 3145736 | tf_op jit(solution)/shard_map/while/body/eval_jaxpr/ppermute | solution.py:28
  342.2 16.4 %collective-permute-start.1 = (bf16[2,512,512]{2,1,0:T(8,128)(2,1)}, bf16[2,512,512]{2,1,0:T(8,128)(2,1)}, u32[]{:S(2)}, u32[]{:S(2)}) collective-permute-start(bf16[2,512,512]{2,1,0:T(8,128)(2,1)} %get-tuple-element.963), channel_id=1, source_target_pairs={{32,0},{64,32},{96,64},{128,96},{160,128},{192,160},{224,192},{33,... | collective-permute-start | bytes 3145736 | tf_op jit(solution)/shard_map/while/body/eval_jaxpr/ppermute | solution.py:28
  361.5 16.4 %collective-permute-start.1 = (bf16[2,512,512]{2,1,0:T(8,128)(2,1)}, bf16[2,512,512]{2,1,0:T(8,128)(2,1)}, u32[]{:S(2)}, u32[]{:S(2)}) collective-permute-start(bf16[2,512,512]{2,1,0:T(8,128)(2,1)} %get-tuple-element.963), channel_id=1, source_target_pairs={{32,0},{64,32},{96,64},{128,96},{160,128},{192,160},{224,192},{33,... | collective-permute-start | bytes 3145736 | tf_op jit(solution)/shard_map/while/body/eval_jaxpr/ppermute | solution.py:28
  380.7 16.4 %collective-permute-start.1 = (bf16[2,512,512]{2,1,0:T(8,128)(2,1)}, bf16[2,512,512]{2,1,0:T(8,128)(2,1)}, u32[]{:S(2)}, u32[]{:S(2)}) collective-permute-start(bf16[2,512,512]{2,1,0:T(8,128)(2,1)} %get-tuple-element.963), channel_id=1, source_target_pairs={{32,0},{64,32},{96,64},{128,96},{160,128},{192,160},{224,192},{33,... | collective-permute-start | bytes 3145736 | tf_op jit(solution)/shard_map/while/body/eval_jaxpr/ppermute | solution.py:28
  399.9 16.4 %collective-permute-start.1 = (bf16[2,512,512]{2,1,0:T(8,128)(2,1)}, bf16[2,512,512]{2,1,0:T(8,128)(2,1)}, u32[]{:S(2)}, u32[]{:S(2)}) collective-permute-start(bf16[2,512,512]{2,1,0:T(8,128)(2,1)} %get-tuple-element.963), channel_id=1, source_target_pairs={{32,0},{64,32},{96,64},{128,96},{160,128},{192,160},{224,192},{33,... | collective-permute-start | bytes 3145736 | tf_op jit(solution)/shard_map/while/body/eval_jaxpr/ppermute | solution.py:28
  419.1 93.3 %collective-permute-start.1 = (bf16[2,512,512]{2,1,0:T(8,128)(2,1)}, bf16[2,512,512]{2,1,0:T(8,128)(2,1)}, u32[]{:S(2)}, u32[]{:S(2)}) collective-permute-start(bf16[2,512,512]{2,1,0:T(8,128)(2,1)} %get-tuple-element.963), channel_id=1, source_target_pairs={{32,0},{64,32},{96,64},{128,96},{160,128},{192,160},{224,192},{33,... | collective-permute-start | bytes 3145736 | tf_op jit(solution)/shard_map/while/body/eval_jaxpr/ppermute | solution.py:28
  529.9 16.4 %collective-permute-start.1 = (bf16[2,512,512]{2,1,0:T(8,128)(2,1)}, bf16[2,512,512]{2,1,0:T(8,128)(2,1)}, u32[]{:S(2)}, u32[]{:S(2)}) collective-permute-start(bf16[2,512,512]{2,1,0:T(8,128)(2,1)} %get-tuple-element.963), channel_id=1, source_target_pairs={{32,0},{64,32},{96,64},{128,96},{160,128},{192,160},{224,192},{33,... | collective-permute-start | bytes 3145736 | tf_op jit(solution)/shard_map/while/body/eval_jaxpr/ppermute | solution.py:28
  563.8 7.8 %collective-permute-start.1 = (bf16[2,512,512]{2,1,0:T(8,128)(2,1)}, bf16[2,512,512]{2,1,0:T(8,128)(2,1)}, u32[]{:S(2)}, u32[]{:S(2)}) collective-permute-start(bf16[2,512,512]{2,1,0:T(8,128)(2,1)} %get-tuple-element.963), channel_id=1, source_target_pairs={{32,0},{64,32},{96,64},{128,96},{160,128},{192,160},{224,192},{33,... | collective-permute-start | bytes 3145736 | tf_op jit(solution)/shard_map/while/body/eval_jaxpr/ppermute | solution.py:28
  633.2 28.8 %collective-permute-start.4 = (bf16[3,128,768]{2,1,0:T(8,128)(2,1)S(1)}, bf16[3,128,768]{2,1,0:T(8,128)(2,1)S(1)}, u32[]{:S(2)}, u32[]{:S(2)}) collective-permute-start(bf16[3,128,768]{2,1,0:T(8,128)(2,1)S(1)} %get-tuple-element.769), channel_id=1, source_target_pairs={{0,16},{16,0},{1,17},{17,1},{2,18},{18,2},{3,19},{19,3},{4,20},{20... | collective-permute-start | bytes 1769480 | tf_op jit(solution)/shard_map/ppermute | solution.py:19
  638.8 35.7 %collective-permute-start.5 = (bf16[3,128,768]{2,1,0:T(8,128)(2,1)S(1)}, bf16[3,128,768]{2,1,0:T(8,128)(2,1)S(1)}, u32[]{:S(2)}, u32[]{:S(2)}) collective-permute-start(bf16[3,128,768]{2,1,0:T(8,128)(2,1)S(1)} %get-tuple-element.770), channel_id=1, source_target_pairs={{16,0},{0,16},{17,1},{1,17},{18,2},{2,18},{19,3},{3,19},{20,4},{4,... | collective-permute-start | bytes 1769480 | tf_op jit(solution)/shard_map/ppermute | solution.py:20
  678.1 55.6 %reduce-scatter.5.cloned.1.call-start = ((), (), s32[]{:S(2)}) async-start(), calls=%async_computation.3 | async-start | bytes 737280 | tf_op jit(solution)/shard_map/reduce_scatter | solution.py:33
  (46 other events, 281.5 us)
Sparse Core Ops, SparseCore 0:
  678.2 30.7 reduce-scatter.2
  711.6 22.0 reduce-scatter.4
where the time goes:
time: 750 us; the launch traced here: 743 us
  waiting for transfers between devices  241 us (32%)
  local copies, waits for them, and re-layouts  239 us (32%)
  other arithmetic  118 us (16%)
  starting transfers between devices  96.9 us (13%)
  matrix products  25.2 us (3%)
  between operations  21 us (3%)
    ppermute x18, waiting for transfers between devices, passed_along(): return lax.ppermute(x, axis, pairs)  138 us
    ppermute x18, starting transfers between devices, passed_along(): return lax.ppermute(x, axis, pairs)  83.6 us
    reduce_scatter x2, waiting for transfers between devices, sum_by_axis(): x = lax.psum_scatter(x, axis, scatter_dimension=dim, tiled=True)  55.5 us
    dynamic_update_slice x2, local copies, waits for them, and re-layouts, shards(): lax.dynamic_update_slice(accum_grid, current_block + pieces[position], an...  43.5 us
    broadcast_in_dim x9, other arithmetic, forward_tick(): lax.dynamic_update_index_in_dim(saved, jnp.where(valid, wave_in, previous...  33.5 us
    another operation x34, local copies, waits for them, and re-layouts  30.2 us
    dynamic_update_slice x18, local copies, waits for them, and re-layouts, forward_tick(): lax.dynamic_update_index_in_dim(finals, jnp.where(keep_final, produced, e...  26.8 us
    ppermute x2, waiting for transfers between devices, extended_2(): after = lax.ppermute(leading, axis, down)  24.7 us
  transfers between devices with their start and end apart: 24, of which 13 were waited for; matrix products, arithmetic and copies ran while one was open for 19% of the time, Pallas kernels for 0%

commit v1 on v0

v1 whole, which is shorter than its diff:
```python
import jax
import jax.numpy as jnp
from jax import lax
from jax.experimental import pallas as pl
from jax.experimental.pallas import tpu as pltpu
from jax.sharding import Mesh
from jax.sharding import PartitionSpec as P

MARGIN = 128
LANES = 128
SUB = 8
PROBE = ("probe_0", "probe_1")
TILE_PROBE = ("tile", "probe_0", "probe_1")
MESH_ID = pl.DeviceIdType.MESH
BF = jnp.bfloat16
F32 = jnp.float32
VMEM = pltpu.VMEM


def cut_kernel(starts, slab, out):
    positions, chunks, size, _ = out.shape
    width = slab.shape[2]
    block = 64
    for position in range(positions):
        row = starts[position, 0]
        col = starts[position, 1]
        shift = lax.rem(width - col, width)
        base = row // SUB * SUB
        drop = lax.rem(block + SUB - lax.rem(row, SUB), block + SUB)

        def rows(step, carry):
            at = pl.multiple_of(step * block, block)
            for part in range(2):
                values = slab[part, pl.ds(pl.multiple_of(base + at, SUB), block + SUB), :]
                turned = pltpu.roll(values, shift, 1)[:, :size]
                turned = pltpu.roll(turned, drop, 0)[:block]
                for chunk in range(chunks):
                    out[position, chunk, pl.ds(at, block), part * LANES : (part + 1) * LANES] = turned[
                        :, chunk * LANES : (chunk + 1) * LANES
                    ].astype(BF)
            return carry

        lax.fori_loop(0, size // block, rows, 0)


def place_kernel(starts, grads, lights, out, total):
    positions, chunks, size, _ = grads.shape
    blocks, _, each, width = out.shape
    block = 64
    total[...] = jnp.zeros_like(total)
    for position in range(positions):
        row = starts[position, 0]
        col = starts[position, 1]
        base = row // SUB * SUB
        drop = lax.rem(row, SUB)

        def rows(step, carry):
            at = pl.multiple_of(step * block, block)
            for part in range(3):
                pieces = []
                for chunk in range(chunks):
                    if part < 2:
                        piece = grads[position, chunk, pl.ds(at, block), part * LANES : (part + 1) * LANES]
                    else:
                        piece = lights[position, chunk, pl.ds(at, block), :]
                    pieces.append(piece.astype(F32))
                lines = jnp.concatenate(pieces, axis=1)
                lines = pltpu.roll(jnp.concatenate([lines, jnp.zeros((SUB, size), F32)], axis=0), drop, 0)
                lines = jnp.concatenate([lines, jnp.zeros((block + SUB, width - size), F32)], axis=1)
                turned = pltpu.roll(lines, col, 1)
                where = pl.ds(pl.multiple_of(base + at, SUB), block + SUB)
                total[part, where, :] = total[part, where, :] + turned
            return carry

        lax.fori_loop(0, size // block, rows, 0)
    own = 2 * each // 3
    edge = each - own
    half = blocks // 2
    for index in range(blocks):
        first = MARGIN + index * own
        out[index, :, 0:own, :] = total[:, first : first + own, :].astype(BF)
        first = index * edge
        if index >= half:
            first += blocks * own
        out[index, :, own:each, :] = total[:, first : first + edge, :].astype(BF)


def chain_kernel(
    probe, windows, forward_cols, adjoint_cols, forward_rows, adjoint_rows, measured,
    grads, lights,
    waves, cots, wave_out, cot_out, total, middle, backs,
    send_f, recv_f, send_b, recv_b,
):
    me = lax.axis_index("cuts")
    count = lax.axis_size("cuts")
    last = count - 1
    right = lax.rem(me + 1, count)
    left = lax.rem(me + count - 1, count)
    positions, chunks, size, pair = windows.shape
    half = pair // 2

    barrier = pltpu.get_barrier_semaphore()
    for other in (left, right):
        pl.semaphore_signal(barrier, inc=1, device_id={"cuts": other}, device_id_type=MESH_ID)

    total[...] = jnp.zeros_like(total)

    @pl.when(me == 0)
    def _():
        for position in range(positions):
            waves[position] = probe[...]

    pl.semaphore_wait(barrier, 2)

    def forward_copy(position, chunk):
        return pltpu.make_async_remote_copy(
            src_ref=wave_out.at[position, chunk],
            dst_ref=waves.at[position, chunk],
            send_sem=send_f.at[position, chunk],
            recv_sem=recv_f.at[position, chunk],
            device_id={"cuts": right},
            device_id_type=MESH_ID,
        )

    def adjoint_copy(position, chunk):
        return pltpu.make_async_remote_copy(
            src_ref=cot_out.at[position, chunk],
            dst_ref=cots.at[position, chunk],
            send_sem=send_b.at[position, chunk],
            recv_sem=recv_b.at[position, chunk],
            device_id={"cuts": left},
            device_id_type=MESH_ID,
        )

    def parts_of(value):
        value = value.astype(F32)
        return value[:, :half], value[:, half:]

    def both(real, imag):
        return jnp.concatenate([real, imag], axis=1)

    def to_middle():
        for chunk in range(chunks):
            columns = slice(chunk * pair, (chunk + 1) * pair)
            middle[chunk] = total[:, columns].astype(BF)
        total[...] = jnp.zeros_like(total)

    def forward(position):
        def gather(chunk, carry):
            @pl.when(me > 0)
            def _():
                forward_copy(position, chunk).wait_recv()

            wave_r, wave_i = parts_of(waves[position, chunk])
            win_r, win_i = parts_of(windows[position, chunk])
            out = both(wave_r * win_r - wave_i * win_i, wave_r * win_i + wave_i * win_r).astype(BF)
            total[...] += jnp.dot(out, forward_cols[chunk], preferred_element_type=F32)
            return carry

        lax.fori_loop(0, chunks, gather, 0)
        to_middle()

        def produce(chunk, carry):
            result = jnp.dot(forward_rows[...], middle[chunk], preferred_element_type=F32)
            real = result[:size, :half] - result[size:, half:]
            imag = result[size:, :half] + result[:size, half:]
            wave_out[position, chunk] = both(real, imag).astype(BF)

            @pl.when(me < last)
            def _():
                forward_copy(position, chunk).start()

            @pl.when(me == last)
            def _():
                psi_r, psi_i = parts_of(wave_out[position, chunk])
                amplitude = measured[position, chunk]
                factor = 1.0 - amplitude * lax.rsqrt(psi_r * psi_r + psi_i * psi_i + 1.0)
                cots[position, chunk] = both(psi_r * factor, psi_i * factor).astype(BF)

            return carry

        lax.fori_loop(0, chunks, produce, 0)

        def brighten(chunk, carry):
            wave_r, wave_i = parts_of(waves[position, chunk])
            lights[position, chunk] = (wave_r * wave_r + wave_i * wave_i).astype(BF)
            return carry

        lax.fori_loop(0, chunks, brighten, 0)

    def adjoint(position):
        def gather(chunk, carry):
            @pl.when(me < last)
            def _():
                adjoint_copy(position, chunk).wait_recv()

            total[...] += jnp.dot(cots[position, chunk], adjoint_cols[chunk], preferred_element_type=F32)
            return carry

        lax.fori_loop(0, chunks, gather, 0)
        to_middle()

        def produce(chunk, carry):
            result = jnp.dot(adjoint_rows[...], middle[chunk], preferred_element_type=F32)
            real = result[:size, :half] + result[size:, half:]
            imag = result[:size, half:] - result[size:, :half]
            back = both(real, imag).astype(BF)
            backs[chunk] = back

            @pl.when(me > 0)
            def _():
                back_r, back_i = parts_of(back)
                win_r, win_i = parts_of(windows[position, chunk])
                cot_out[position, chunk] = both(
                    win_r * back_r + win_i * back_i, win_r * back_i - win_i * back_r
                ).astype(BF)
                adjoint_copy(position, chunk).start()

            return carry

        lax.fori_loop(0, chunks, produce, 0)

        def grade(chunk, carry):
            wave_r, wave_i = parts_of(waves[position, chunk])
            back_r, back_i = parts_of(backs[chunk])
            grads[position, chunk] = both(
                wave_r * back_r + wave_i * back_i, wave_r * back_i - wave_i * back_r
            ).astype(BF)
            return carry

        lax.fori_loop(0, chunks, grade, 0)

    late = me // (count - 2)

    def phase(step, carry):
        is_back = late * (step % positions) + (1 - late) * (step // positions)
        position = late * (step // positions) + (1 - late) * (step % positions)

        @pl.when(is_back == 0)
        def _():
            forward(position)

        @pl.when(is_back == 1)
        def _():
            adjoint(position)

        return carry

    lax.fori_loop(0, 2 * positions, phase, 0)

    def finish(index, carry):
        position = index // chunks
        chunk = index % chunks

        @pl.when(me < last)
        def _():
            forward_copy(position, chunk).wait_send()

        @pl.when(me > 0)
        def _():
            adjoint_copy(position, chunk).wait_send()

        return carry

    lax.fori_loop(0, positions * chunks, finish, 0)


def column_blocks(matrix, chunks):
    _, _, depth, width = matrix.shape
    cut = matrix.reshape(2, 2, chunks, depth // chunks, chunks, width // chunks)
    return cut.transpose(2, 0, 3, 4, 1, 5).reshape(chunks, 2 * depth // chunks, 2 * width)


def in_vmem(count):
    return [pl.BlockSpec(memory_space=pltpu.VMEM)] * count


def shards(probe_wave, fresnel_rows, fresnel_cols, object_slices, offsets, measured):
    owned = object_slices[0]
    starts = offsets[0]
    size = probe_wave.shape[1]
    positions = starts.shape[0]
    rows, width = owned.shape[1:]
    chunks = size // LANES
    pair = 2 * LANES
    probe_index = lax.axis_index(PROBE)
    probe_count = lax.axis_size(PROBE)

    transmission = owned.astype(BF)
    edges = jnp.concatenate([transmission[:, rows - MARGIN :], transmission[:, :MARGIN]], axis=1)
    share = edges.shape[1] // probe_count
    mine = lax.dynamic_slice_in_dim(edges, probe_index * share, share, 1)
    swapped = lax.ppermute(mine, "tile", [(0, 1), (1, 0)])
    theirs = lax.all_gather(swapped, PROBE, axis=1, tiled=True)
    slab = jnp.concatenate([theirs[:, :MARGIN], transmission, theirs[:, MARGIN:]], axis=1).astype(F32)
    slab = jnp.pad(slab, ((0, 0), (0, SUB), (0, 0)))

    windows = pl.pallas_call(
        cut_kernel,
        out_shape=jax.ShapeDtypeStruct((positions, chunks, size, pair), BF),
        in_specs=[pl.BlockSpec(memory_space=pltpu.SMEM)] + in_vmem(1),
        out_specs=pl.BlockSpec(memory_space=pltpu.VMEM),
        name="cut",
    )(starts, slab)

    col_r, col_i = fresnel_cols[0], fresnel_cols[1]
    forward_cols = column_blocks(jnp.stack([jnp.stack([col_r.T, col_i.T]), jnp.stack([-col_i.T, col_r.T])]), chunks)
    adjoint_cols = column_blocks(jnp.stack([jnp.stack([col_r, -col_i]), jnp.stack([col_i, col_r])]), chunks)
    forward_rows = fresnel_rows.reshape(2 * size, size)
    adjoint_rows = fresnel_rows.swapaxes(1, 2).reshape(2 * size, size)
    probe = probe_wave.reshape(2, size, chunks, LANES).transpose(2, 1, 0, 3).reshape(chunks, size, pair)
    amplitude = measured[0].reshape(positions, size, chunks, LANES).transpose(0, 2, 1, 3)

    wave_stack = pltpu.VMEM((positions, chunks, size, pair), BF)
    grads, lights = pl.pallas_call(
        chain_kernel,
        out_shape=[
            jax.ShapeDtypeStruct((positions, chunks, size, pair), BF),
            jax.ShapeDtypeStruct((positions, chunks, size, LANES), BF),
        ],
        in_specs=in_vmem(7),
        out_specs=in_vmem(2),
        scratch_shapes=[
            wave_stack,
            wave_stack,
            wave_stack,
            wave_stack,
            pltpu.VMEM((size, 2 * size), F32),
            pltpu.VMEM((chunks, size, pair), BF),
            pltpu.VMEM((chunks, size, pair), BF),
            pltpu.SemaphoreType.DMA((positions, chunks)),
            pltpu.SemaphoreType.DMA((positions, chunks)),
            pltpu.SemaphoreType.DMA((positions, chunks)),
            pltpu.SemaphoreType.DMA((positions, chunks)),
        ],
        compiler_params=pltpu.CompilerParams(collective_id=0, has_side_effects=True, vmem_limit_bytes=60 * 2**20),
        name="chain",
    )(probe, windows, forward_cols, adjoint_cols, forward_rows, adjoint_rows, amplitude)

    own = rows // probe_count
    edge = 2 * MARGIN // probe_count
    grid = pl.pallas_call(
        place_kernel,
        out_shape=jax.ShapeDtypeStruct((probe_count, 3, own + edge, width), BF),
        in_specs=[pl.BlockSpec(memory_space=pltpu.SMEM)] + in_vmem(2),
        out_specs=pl.BlockSpec(memory_space=pltpu.VMEM),
        scratch_shapes=[pltpu.VMEM((3, rows + 2 * MARGIN + SUB, width), F32)],
        name="place",
    )(starts, grads, lights)

    summed = grid
    for axis in PROBE:
        summed = lax.psum_scatter(summed, axis, scatter_dimension=0, tiled=True)
    summed = summed[0]
    inside = summed[:, :own].astype(F32)
    margin = summed[:, own:]
    per_own = own // edge
    half = probe_count // 2
    received = []
    for which in range(per_own):
        pairs = []
        for tile in range(2):
            for index in range(which, probe_count, per_own):
                if index < half:
                    target = probe_count - half // per_own + index // per_own
                else:
                    target = (index - half) // per_own
                pairs.append((tile * probe_count + index, (1 - tile) * probe_count + target))
        received.append(lax.ppermute(margin, TILE_PROBE, pairs))
    full = inside + jnp.concatenate(received, axis=1).astype(F32)
    own_part = lax.dynamic_slice_in_dim(owned, probe_index * own, own, 1)
    updated = own_part - full[:2] / (full[2] + 1.0)
    return updated[None]


def solution(mesh):
    split = Mesh(
        mesh.devices.reshape(mesh.shape["cuts"], mesh.shape["tile"], 4, 4),
        ("cuts", "tile", "probe_0", "probe_1"),
    )
    return jax.shard_map(
        shards,
        mesh=split,
        in_specs=(
            P(),
            P(),
            P(),
            P("cuts", None, "tile", None),
            P("tile", PROBE, None),
            P("tile", PROBE, None, None),
        ),
        out_specs=P("cuts", None, TILE_PROBE, None),
        check_vma=False,
    )
```

time: 750 us -> 377 us (0.50)
  local copies, waits for them, and re-layouts: 239 us -> 50.5 us
  Pallas kernels: 0 us -> 167 us
  waiting for transfers between devices: 241 us -> 77.6 us
  other arithmetic: 118 us -> 22.5 us
  starting transfers between devices: 96.9 us -> 20.6 us
  matrix products: 25.2 us -> 0 us
  blocking collectives: 0 us -> 24.2 us
  between operations: 21 us -> 13.5 us
    ppermute x22 -> x3, waiting for transfers between devices: 185 us -> 12.9 us  [the longest x2 12.9 us: shards(): received.append(lax.ppermute(margin, TILE_PROBE, pairs))]
    pallas_call x0 -> x3, Pallas kernels: none -> 167 us  [the longest x1 151 us: shards(): pl.pallas_call(chain_kernel, out_shape=[jax.ShapeDtypeStruct((positions,...]
    dynamic_update_slice x29 -> x0, local copies, waits for them, and re-layouts: 92.4 us -> none  [the longest x2 43.5 us: shards(): lax.dynamic_update_slice(accum_grid, current_block + pieces[position], an...]
    ppermute x22 -> x3, starting transfers between devices: 96.9 us -> 20.6 us  [the longest x2 13.3 us: shards(): received.append(lax.ppermute(margin, TILE_PROBE, pairs))]
    dynamic_slice x54 -> x0, local copies, waits for them, and re-layouts: 71.3 us -> none  [the longest x18 20.5 us: forward_tick(): previous = lax.dynamic_index_in_dim(saved, slot, 0, keepdims=False)]
    broadcast_in_dim x18 -> x0, other arithmetic: 43.3 us -> none  [the longest x9 33.5 us: forward_tick(): lax.dynamic_update_index_in_dim(saved, jnp.where(valid, wave_in, previous...]
    dot_general x12 -> x0, matrix products: 25.2 us -> none  [the longest x2 8.5 us: adjoint_apply(): result = jnp.dot(left_block, middle, preferred_element_type=jnp.float32)]
    all_gather x0 -> x1, blocking collectives: none -> 24.2 us  [shards(): theirs = lax.all_gather(swapped, PROBE, axis=1, tiled=True)]
  transfers between devices with their start and end apart: 24 -> 5, of which waited for: 13 -> 4; matrix products, arithmetic and copies ran while one was open for 19% -> 17% of each run, Pallas kernels for 0% -> 0%
where the time goes in v1:
time: 377 us; the launch traced here: 376 us
  Pallas kernels  167 us (44%)
  waiting for transfers between devices  77.6 us (21%)
  local copies, waits for them, and re-layouts  50.5 us (13%)
  blocking collectives  24.2 us (6%)
  other arithmetic  22.5 us (6%)
  starting transfers between devices  20.6 us (5%)
  between operations  13.5 us (4%)
    pallas_call x1, Pallas kernels, shards(): pl.pallas_call(chain_kernel, out_shape=[jax.ShapeDtypeStruct((positions,...  151 us
    reduce_scatter x2, waiting for transfers between devices, shards(): summed = lax.psum_scatter(summed, axis, scatter_dimension=0, tiled=True)  64.7 us
    all_gather x1, blocking collectives, shards(): theirs = lax.all_gather(swapped, PROBE, axis=1, tiled=True)  24.2 us
    ppermute x2, starting transfers between devices, shards(): received.append(lax.ppermute(margin, TILE_PROBE, pairs))  13.3 us
    ppermute x2, waiting for transfers between devices, shards(): received.append(lax.ppermute(margin, TILE_PROBE, pairs))  12.9 us
    another operation x4, local copies, waits for them, and re-layouts, shards(): jnp.stack([col_r.T, col_i.T])  11.6 us
    another operation x4, local copies, waits for them, and re-layouts, shards(): jnp.stack([jnp.stack([col_r, -col_i]), jnp.stack([col_i, col_r])])  11.1 us
    transpose x2, other arithmetic, column_blocks(): cut.transpose(2, 0, 3, 4, 1, 5)  10 us
  transfers between devices with their start and end apart: 5, of which 4 were waited for; matrix products, arithmetic and copies ran while one was open for 17% of the time, Pallas kernels for 0%

profile of v1, /device:TPU:8, one launch (start us, length us, event | category | flops | bytes accessed | tf_op | source)
XLA Modules:
  0.0 375.8 jit_solution(3090354356561662293)
XLA Ops:
  8.7 7.3 %collective-permute-start = (bf16[2,16,768]{2,1,0:T(8,128)(2,1)S(1)}, bf16[2,16,768]{2,1,0:T(8,128)(2,1)S(1)}, u32[]{:S(2)}, u32[]{:S(2)}) collective-permute-start(bf16[2,16,768]{2,1,0:T(8,128)(2,1)S(1)} %fusion.9), channel_id=1, source_target_pairs={{0,16},{16,0},{1,17},{17,1},{2,18},{18,2},{3,19},{19,3},{4,20},{20... | collective-permute-start | bytes 147464 | tf_op jit(solution)/shard_map/ppermute | solution.py:293
  20.2 2.9 copy.18
  25.1 3.8 %copy.17 = bf16[1,1,4,128,4,128]{5,1,4,3,0,2:T(2,128)(2,1)} copy(bf16[1,1,4,128,4,128]{3,2,5,4,1,0:T(4,128)(2,1)} %stack.38) | data formatting | bytes 1048576 | tf_op jit(solution)/shard_map/stack | solution.py:307
  30.9 3.8 %copy.16 = bf16[1,1,4,128,4,128]{5,1,4,3,0,2:T(2,128)(2,1)} copy(bf16[1,1,4,128,4,128]{3,2,5,4,1,0:T(4,128)(2,1)} %stack.37) | data formatting | bytes 1048576 | tf_op jit(solution)/shard_map/stack | solution.py:307
  34.7 2.9 pad_maximum_fusion
  39.8 3.8 %copy.20 = bf16[1,2,4,128,4,128]{5,1,4,3,0,2:T(2,128)(2,1)} copy(bf16[1,2,4,128,4,128]{5,4,3,2,1,0:T(4,128)(2,1)} %stack.44) | data formatting | bytes 2097152 | tf_op jit(solution)/shard_map/stack | solution.py:308
  45.8 3.0 copy.21
  48.8 5.6 %maximum_bitcast_fusion = bf16[4,2,128,4,2,128]{5,4,3,2,1,0:T(2,128)(2,1)} fusion(bf16[1,1,4,128,4,128]{5,1,4,3,0,2:T(2,128)(2,1)S(1)} %copy-done.1, bf16[1,1,4,128,4,128]{5,1,4,3,0,2:T(2,128)(2,1)S(1)} %copy.18, bf16[1,1,4,128,4,128]{5,1,4,3,0,2:T(2,128)(2,1)S(1)} %copy-done), kind=kLoop, calls=%fused_computation.7 | loop fusion | flops 8388608 | bytes 3670016 | tf_op jit(solution)/shard_map/transpose | solution.py:271
  54.5 4.4 %maximum_bitcast_fusion.1 = bf16[4,2,128,4,2,128]{5,4,3,2,1,0:T(2,128)(2,1)} fusion(bf16[1,2,4,128,4,128]{5,1,4,3,0,2:T(2,128)(2,1)S(1)} %copy.21, bf16[1,2,4,128,4,128]{5,1,4,3,0,2:T(2,128)(2,1)S(1)} %copy-done.2), kind=kLoop, calls=%fused_computation.8 | loop fusion | flops 1048576 | bytes 4194304 | tf_op jit(solution)/shard_map/transpose | solution.py:271
  59.9 2.3 copy.26
  63.7 2.3 copy.22
  66.0 2.9 copy.23
  68.9 2.9 copy.24
  71.8 4.4 %reshape.40.forward_cols = bf16[4,256,1024]{2,1,0:T(8,128)(2,1)} reshape(bf16[4,2,128,4,2,128]{5,4,3,2,1,0:T(2,128)(2,1)} %maximum_bitcast_fusion) | data formatting | bytes 4194304 | tf_op jit(solution)/shard_map/reshape | solution.py:271
  76.3 4.5 %reshape.41.adjoint_cols = bf16[4,256,1024]{2,1,0:T(8,128)(2,1)} reshape(bf16[4,2,128,4,2,128]{5,4,3,2,1,0:T(2,128)(2,1)} %maximum_bitcast_fusion.1) | data formatting | bytes 4194304 | tf_op jit(solution)/shard_map/reshape | solution.py:271
  80.7 24.2 %all_gather.3 = bf16[2,256,768]{2,1,0:T(8,128)(2,1)S(1)} all-gather(bf16[2,16,768]{2,1,0:T(8,128)(2,1)S(1)} %collective-permute-done), channel_id=1, replica_groups=mesh['cuts'=8,'tile'=2,'probe_0'=4,'probe_1'=4] {'probe_0','probe_1'}, dimensions={1}, use_global_device_ids=true | all-gather | bytes 835584 | tf_op jit(solution)/shard_map/all_gather | solution.py:294
  105.0 2.6 fusion.5.slab
  107.6 7.4 %cut.1.windows = bf16[2,4,512,256]{3,2,1,0:T(8,128)(2,1)} custom-call(s32[2,2]{1,0:T(2,128)} %bitcast.45, f32[2,776,768]{2,1,0:T(8,128)} %fusion.5.slab), custom_call_target="tpu_custom_call" | custom-call | tf_op jit(solution)/shard_map/cut/pallas_call | solution.py:298
  115.0 151.0 %chain.1 = (bf16[2,4,512,256]{3,2,1,0:T(8,128)(2,1)}, bf16[2,4,512,128]{3,2,1,0:T(8,128)(2,1)}) custom-call(bf16[4,512,256]{2,1,0:T(8,128)(2,1)} %reshape.39.probe, bf16[2,4,512,256]{3,2,1,0:T(8,128)(2,1)} %cut.1.windows, bf16[4,256,1024]{2,1,0:T(8,128)(2,1)} %reshape.40.forward_cols, bf16[4,256,1024]{2,1,0:T(8,128)(2,1)} %reshape.41.adjoint_cols, ...), custom_call_target="tpu_custom_call" | custom-call | tf_op jit(solution)/shard_map/chain/pallas_call | solution.py:315
  266.0 8.4 %place.1 = bf16[16,3,48,768]{3,2,1,0:T(8,128)(2,1)} custom-call(s32[2,2]{1,0:T(2,128)} %bitcast.46, bf16[2,4,512,256]{3,2,1,0:T(8,128)(2,1)} %get-tuple-element.7.grads, bf16[2,4,512,128]{3,2,1,0:T(8,128)(2,1)} %get-tuple-element.8.lights), custom_call_target="tpu_custom_call" | custom-call | tf_op jit(solution)/shard_map/place/pallas_call | solution.py:342
  274.5 39.1 %reduce-scatter.3.cloned.1.call-done = bf16[4,3,48,768]{3,2,1,0:T(8,128)(2,1)} async-done(((bf16[16,3,48,768]{3,2,1,0:T(8,128)(2,1)}), bf16[4,3,48,768]{3,2,1,0:T(8,128)(2,1)}) %reduce-scatter.3.cloned.1.call-update) | async-done | bytes 884752 | tf_op jit(solution)/shard_map/reduce_scatter | solution.py:353
  313.6 25.6 %reduce-scatter.5.cloned.1.call-done = bf16[1,3,48,768]{3,2,1,0:T(8,128)(2,1)} async-done(((bf16[4,3,48,768]{3,2,1,0:T(8,128)(2,1)}), bf16[1,3,48,768]{3,2,1,0:T(8,128)(2,1)}) %reduce-scatter.5.cloned.1.call-update) | async-done | bytes 221200 | tf_op jit(solution)/shard_map/reduce_scatter | solution.py:353
  340.1 12.0 %collective-permute-start.2 = (bf16[3,16,768]{2,1,0:T(8,128)(2,1)S(1)}, bf16[3,16,768]{2,1,0:T(8,128)(2,1)S(1)}, u32[]{:S(2)}, u32[]{:S(2)}) collective-permute-start(bf16[3,16,768]{2,1,0:T(8,128)(2,1)S(1)} %slice.45), channel_id=1, source_target_pairs={{1,28},{3,29},{5,30},{7,31},{9,16},{11,17},{13,18},{15,19},{17,12}... | collective-permute-start | bytes 221192 | tf_op jit(solution)/shard_map/ppermute | solution.py:369
  355.1 11.3 %collective-permute-done.1 = bf16[3,16,768]{2,1,0:T(8,128)(2,1)S(1)} collective-permute-done((bf16[3,16,768]{2,1,0:T(8,128)(2,1)S(1)}, bf16[3,16,768]{2,1,0:T(8,128)(2,1)S(1)}, u32[]{:S(2)}, u32[]{:S(2)}) %collective-permute-start.1) | collective-permute-done | bytes 73760 | tf_op jit(solution)/shard_map/ppermute | solution.py:369
  (34 shorter events, 23.8 us)
Async XLA Ops:
  6.5 307.1 %reduce-scatter.3.cloned.1.call-start = ((), (), s32[]{:S(2)}) async-start(), calls=%async_computation.2 | async-start | bytes 4423680 | tf_op jit(solution)/shard_map/reduce_scatter | solution.py:353
  8.6 7.4 %copy-start.3 = (bf16[2,512,512]{2,1,0:T(8,128)(2,1)S(1)}, bf16[2,512,512]{2,1,0:T(8,128)(2,1)}, u32[]{:S(2)}) copy-start(bf16[2,512,512]{2,1,0:T(8,128)(2,1)} %param.8) | copy-start | bytes 3145732
  8.7 72.0 %collective-permute-start = (bf16[2,16,768]{2,1,0:T(8,128)(2,1)S(1)}, bf16[2,16,768]{2,1,0:T(8,128)(2,1)S(1)}, u32[]{:S(2)}, u32[]{:S(2)}) collective-permute-start(bf16[2,16,768]{2,1,0:T(8,128)(2,1)S(1)} %fusion.9), channel_id=1, source_target_pairs={{0,16},{16,0},{1,17},{17,1},{2,18},{18,2},{3,19},{19,3},{4,20},{20... | collective-permute-start | bytes 147464 | tf_op jit(solution)/shard_map/ppermute | solution.py:293
  45.8 3.0 copy-start
  45.8 3.0 copy-start.1
  48.8 5.7 %copy-start.2 = (bf16[1,2,4,128,4,128]{5,1,4,3,0,2:T(2,128)(2,1)S(1)}, bf16[1,2,4,128,4,128]{5,1,4,3,0,2:T(2,128)(2,1)}, u32[]{:S(2)}) copy-start(bf16[1,2,4,128,4,128]{5,1,4,3,0,2:T(2,128)(2,1)} %copy.20) | copy-start | bytes 3145732
  54.5 4.4 %copy-start.4 = (bf16[2,512,512]{2,1,0:T(8,128)(2,1)S(1)}, bf16[2,512,512]{2,1,0:T(8,128)(2,1)}, u32[]{:S(2)}) copy-start(bf16[2,512,512]{2,1,0:T(8,128)(2,1)} %param.6) | copy-start | bytes 3145732
  274.5 64.7 %reduce-scatter.5.cloned.1.call-start = ((), (), s32[]{:S(2)}) async-start(), calls=%async_computation.3 | async-start | bytes 1105920 | tf_op jit(solution)/shard_map/reduce_scatter | solution.py:353
  340.1 15.0 %collective-permute-start.2 = (bf16[3,16,768]{2,1,0:T(8,128)(2,1)S(1)}, bf16[3,16,768]{2,1,0:T(8,128)(2,1)S(1)}, u32[]{:S(2)}, u32[]{:S(2)}) collective-permute-start(bf16[3,16,768]{2,1,0:T(8,128)(2,1)S(1)} %slice.45), channel_id=1, source_target_pairs={{1,28},{3,29},{5,30},{7,31},{9,16},{11,17},{13,18},{15,19},{17,12}... | collective-permute-start | bytes 221192 | tf_op jit(solution)/shard_map/ppermute | solution.py:369
  352.1 14.2 %collective-permute-start.1 = (bf16[3,16,768]{2,1,0:T(8,128)(2,1)S(1)}, bf16[3,16,768]{2,1,0:T(8,128)(2,1)S(1)}, u32[]{:S(2)}, u32[]{:S(2)}) collective-permute-start(bf16[3,16,768]{2,1,0:T(8,128)(2,1)S(1)} %slice.45), channel_id=1, source_target_pairs={{0,28},{2,29},{4,30},{6,31},{8,16},{10,17},{12,18},{14,19},{16,12}... | collective-permute-start | bytes 221192 | tf_op jit(solution)/shard_map/ppermute | solution.py:369
Sparse Core Ops, SparseCore 0:
  274.6 38.9 reduce-scatter.2
  316.2 22.9 reduce-scatter.4

commit v2 on v1

--- a/solution.py
+++ b/solution.py
@@ -17,10 +17,79 @@
 VMEM = pltpu.VMEM
 
 
-def cut_kernel(starts, slab, out):
+def edge_kernel(owned, out, mine, got, gathered, send_z, recv_z, send_sem, recv_sem):
+    tile, x, y = lax.axis_index("tile"), lax.axis_index("probe_0"), lax.axis_index("probe_1")
+    nx, ny = lax.axis_size("probe_0"), lax.axis_size("probe_1")
+    count = nx * ny
+    me = x * ny + y
+    rows = owned.shape[1]
+    share = mine.shape[1]
+    half = count // 2
+    mate = {"tile": 1 - tile}
+
+    def peer(step):
+        other = lax.rem(me + step, count)
+        return {"probe_0": other // ny, "probe_1": lax.rem(other, ny)}
+
+    barrier = pltpu.get_barrier_semaphore()
+    pl.semaphore_signal(barrier, inc=1, device_id=mate, device_id_type=MESH_ID)
+    for step in range(1, count):
+        pl.semaphore_signal(barrier, inc=1, device_id=peer(step), device_id_type=MESH_ID)
+
+    lower = me // half
+    first = (1 - lower) * (rows - MARGIN + me * share) + lower * (me - half) * share
+    mine[...] = owned[:, pl.ds(pl.multiple_of(first, share), share), :].astype(BF)
+    pl.semaphore_wait(barrier, count)
+
+    swap = pltpu.make_async_remote_copy(
+        src_ref=mine, dst_ref=got, send_sem=send_z, recv_sem=recv_z, device_id=mate, device_id_type=MESH_ID
+    )
+    swap.start()
+    swap.wait_recv()
+
+    def share_copy(step):
+        return pltpu.make_async_remote_copy(
+            src_ref=got,
+            dst_ref=gathered.at[me],
+            send_sem=send_sem.at[step],
+            recv_sem=recv_sem.at[me],
+            device_id=peer(step),
+            device_id_type=MESH_ID,
+        )
+
+    def arrival(step):
+        sender = lax.rem(me + count - step, count)
+        return pltpu.make_async_remote_copy(
+            src_ref=got,
+            dst_ref=gathered.at[sender],
+            send_sem=send_sem.at[step],
+            recv_sem=recv_sem.at[sender],
+            device_id=peer(step),
+            device_id_type=MESH_ID,
+        )
+
+    for step in range(1, count):
+        share_copy(step).start()
+    out[me] = got[...]
+    for step in range(1, count):
+        arrival(step).wait_recv()
+        sender = lax.rem(me + count - step, count)
+        out[sender] = gathered[sender]
+    swap.wait_send()
+    for step in range(1, count):
+        share_copy(step).wait_send()
+
+
+def cut_kernel(starts, owned, edges, out, slab):
     positions, chunks, size, _ = out.shape
-    width = slab.shape[2]
+    rows, width = owned.shape[1:]
+    count, _, share, _ = edges.shape
     block = 64
+    for index in range(count):
+        first = index * share + (rows if index >= count // 2 else 0)
+        slab[:, first : first + share, :] = edges[index].astype(F32)
+    slab[:, MARGIN : MARGIN + rows, :] = owned[...].astype(BF).astype(F32)
+    slab[:, rows + 2 * MARGIN :, :] = jnp.zeros((2, SUB, width), F32)
     for position in range(positions):
         row = starts[position, 0]
         col = starts[position, 1]
@@ -28,7 +97,7 @@
         base = row // SUB * SUB
         drop = lax.rem(block + SUB - lax.rem(row, SUB), block + SUB)
 
-        def rows(step, carry):
+        def lines(step, carry):
             at = pl.multiple_of(step * block, block)
             for part in range(2):
                 values = slab[part, pl.ds(pl.multiple_of(base + at, SUB), block + SUB), :]
@@ -40,12 +109,14 @@
                     ].astype(BF)
             return carry
 
-        lax.fori_loop(0, size // block, rows, 0)
+        lax.fori_loop(0, size // block, lines, 0)
 
 
 def place_kernel(starts, grads, lights, out, total):
     positions, chunks, size, _ = grads.shape
-    blocks, _, each, width = out.shape
+    _, nx, ny, each, width = out.shape
+    ny //= 3
+    width *= 2
     block = 64
     total[...] = jnp.zeros_like(total)
     for position in range(positions):
@@ -75,19 +146,176 @@
         lax.fori_loop(0, size // block, rows, 0)
     own = 2 * each // 3
     edge = each - own
-    half = blocks // 2
-    for index in range(blocks):
-        first = MARGIN + index * own
-        out[index, :, 0:own, :] = total[:, first : first + own, :].astype(BF)
-        first = index * edge
-        if index >= half:
-            first += blocks * own
-        out[index, :, own:each, :] = total[:, first : first + edge, :].astype(BF)
+    for x in range(nx):
+        for y in range(ny):
+            index = x * ny + y
+            first = MARGIN + index * own
+            second = index * edge + (nx * ny * own if 2 * index >= nx * ny else 0)
+            for side in range(2):
+                major, minor = (x, y) if side == 0 else (y, x)
+                lanes = slice(side * width // 2, (side + 1) * width // 2)
+                place = slice(3 * minor, 3 * minor + 3)
+                out[side, major, place, 0:own, :] = total[:, first : first + own, lanes].astype(BF)
+                out[side, major, place, own:each, :] = total[:, second : second + edge, lanes].astype(BF)
+
+
+def reduce_kernel(
+    grid, owned, out,
+    pre_up, pre_down, staged_up, staged_down, got_up, got_down, partial,
+    pre_up2, pre_down2, staged_up2, staged_down2, got_up2, got_down2,
+    final, extra, rows_here, send_sem, recv_sem, send_m, recv_m, local_sem,
+):
+    tile = lax.axis_index("tile")
+    where = {"probe_0": lax.axis_index("probe_0"), "probe_1": lax.axis_index("probe_1")}
+    sizes = {"probe_0": lax.axis_size("probe_0"), "probe_1": lax.axis_size("probe_1")}
+    nx, ny = sizes["probe_0"], sizes["probe_1"]
+    count = nx * ny
+    me = where["probe_0"] * ny + where["probe_1"]
+    each = grid.shape[3]
+    own = 2 * each // 3
+    edge = each - own
+    lanes = grid.shape[4]
+    half = count // 2
+    order = (("probe_0", "probe_1"), ("probe_1", "probe_0"))
+
+    def device(index):
+        return {"tile": 1 - tile, "probe_0": index // ny, "probe_1": lax.rem(index, ny)}
+
+    lower = me // half
+    target = (1 - lower) * (count - half // 2 + me // 2) + lower * ((me - half) // 2)
+    outer = where["probe_0"] // (nx - 1) + (nx - 1 - where["probe_0"]) // (nx - 1)
+    source = where["probe_0"] // (nx - 1) * (2 * (me - count + half // 2)) + (
+        nx - 1 - where["probe_0"]
+    ) // (nx - 1) * (half + 2 * me)
+
+    fetch = pltpu.make_async_copy(owned.at[:, pl.ds(pl.multiple_of(me * own, own), own), :], rows_here, local_sem)
+    fetch.start()
+
+    barrier = pltpu.get_barrier_semaphore()
+    for axis in ("probe_0", "probe_1"):
+        for step in (1, sizes[axis] - 1):
+            other = {axis: lax.rem(where[axis] + step, sizes[axis])}
+            pl.semaphore_signal(barrier, inc=1, device_id=other, device_id_type=MESH_ID)
+
+    @pl.when(outer == 1)
+    def _():
+        for which in range(2):
+            pl.semaphore_signal(barrier, inc=1, device_id=device(source + which), device_id_type=MESH_ID)
+
+    pl.semaphore_wait(barrier, 5)
+
+    def copies(stage, side, src, bufs):
+        axis = order[side][stage]
+        size = sizes[axis]
+        here = where[axis]
+        plus, minus = lax.rem(here + 1, size), lax.rem(here + size - 1, size)
+        opposite = lax.rem(here + 2, size)
+        up_pre, down_pre, up_staged, down_staged, up_got, down_got = bufs
+        depth = src.shape[1]
+        cut = (depth + 1) // 2
+        low, high = pl.ds(0, cut), pl.ds(cut, depth - cut)
+
+        def copy(index, source_ref, target_ref, to):
+            return pltpu.make_async_remote_copy(
+                src_ref=source_ref,
+                dst_ref=target_ref,
+                send_sem=send_sem.at[stage, side, index],
+                recv_sem=recv_sem.at[stage, side, index],
+                device_id={axis: to},
+                device_id_type=MESH_ID,
+            )
+
+        return (
+            copy(0, src.at[opposite, low], up_pre.at[side], plus),
+            copy(1, src.at[opposite, high], down_pre.at[side], minus),
+            copy(2, src.at[plus, high], up_got.at[side, high], plus),
+            copy(3, src.at[minus, low], down_got.at[side, low], minus),
+            copy(4, up_staged.at[side], up_got.at[side, low], plus),
+            copy(5, down_staged.at[side], down_got.at[side, high], minus),
+        ), (here, plus, minus, low, high)
+
+    def begin(stage, side, src, bufs):
+        made, _ = copies(stage, side, src, bufs)
+        for index in range(4):
+            made[index].start()
+
+    def relay(stage, side, src, bufs):
+        made, (_, plus, minus, low, high) = copies(stage, side, src, bufs)
+        up_pre, down_pre, up_staged, down_staged, _, _ = bufs
+        made[0].wait_recv()
+        up_staged[side] = (up_pre[side].astype(F32) + src[plus, low].astype(F32)).astype(BF)
+        made[4].start()
+        made[1].wait_recv()
+        down_staged[side] = (down_pre[side].astype(F32) + src[minus, high].astype(F32)).astype(BF)
+        made[5].start()
+
+    def settle(stage, side, src, bufs):
+        made, (here, _, _, _, _) = copies(stage, side, src, bufs)
+        for index in range(2, 6):
+            made[index].wait_recv()
+        up_got, down_got = bufs[4], bufs[5]
+        return src[here].astype(F32) + up_got[side].astype(F32) + down_got[side].astype(F32)
+
+    def drain(stage, side, src, bufs):
+        for copy in copies(stage, side, src, bufs)[0]:
+            copy.wait_send()
+
+    one = (pre_up, pre_down, staged_up, staged_down, got_up, got_down)
+    two = (pre_up2, pre_down2, staged_up2, staged_down2, got_up2, got_down2)
+    for side in range(2):
+        begin(0, side, grid.at[side], one)
+    for side in range(2):
+        relay(0, side, grid.at[side], one)
+    for side in range(2):
+        summed = settle(0, side, grid.at[side], one).astype(BF)
+        for index in range(partial.shape[1]):
+            partial[side, index] = summed[3 * index : 3 * index + 3]
+        begin(1, side, partial.at[side], two)
+    for side in range(2):
+        relay(1, side, partial.at[side], two)
+    for side in range(2):
+        final[side] = settle(1, side, partial.at[side], two).astype(BF)
+
+    def margin_copy(slot):
+        return pltpu.make_async_remote_copy(
+            src_ref=final.at[:, :, pl.ds(own, edge), :],
+            dst_ref=extra.at[slot],
+            send_sem=send_m,
+            recv_sem=recv_m.at[slot],
+            device_id=device(target),
+            device_id_type=MESH_ID,
+        )
+
+    margin_copy(lax.rem(me, 2)).start()
+    fetch.wait()
+
+    @pl.when(outer == 0)
+    def _():
+        extra[...] = jnp.zeros_like(extra)
+
+    @pl.when(outer == 1)
+    def _():
+        for slot in range(2):
+            margin_copy(slot).wait_recv()
+
+    for side in range(2):
+        columns = slice(side * lanes, (side + 1) * lanes)
+        for slot in range(2):
+            lines = slice(slot * edge, (slot + 1) * edge)
+            full = final[side, :, lines, :].astype(F32) + extra[slot, side].astype(F32)
+            scale = 1.0 / (full[2] + 1.0)
+            for part in range(2):
+                out[part, lines, columns] = rows_here[part, lines, columns] - full[part] * scale
+    margin_copy(lax.rem(me, 2)).wait_send()
+    for side in range(2):
+        drain(0, side, grid.at[side], one)
+        drain(1, side, partial.at[side], two)
 
 
 def chain_kernel(
-    probe, windows, forward_cols, adjoint_cols, forward_rows, adjoint_rows, measured,
+    probe, windows, fresnel_cols, forward_rows, measured,
     grads, lights,
+    forward_cols, adjoint_cols, adjoint_rows,
     waves, cots, wave_out, cot_out, total, middle, backs,
     send_f, recv_f, send_b, recv_b,
 ):
@@ -104,11 +332,49 @@
         pl.semaphore_signal(barrier, inc=1, device_id={"cuts": other}, device_id_type=MESH_ID)
 
     total[...] = jnp.zeros_like(total)
+    first_half, second_half = slice(0, half), slice(half, pair)
 
     @pl.when(me == 0)
     def _():
         for position in range(positions):
-            waves[position] = probe[...]
+            for chunk in range(chunks):
+                lanes = slice(chunk * half, (chunk + 1) * half)
+                waves[position, chunk, :, first_half] = probe[0, :, lanes]
+                waves[position, chunk, :, second_half] = probe[1, :, lanes]
+
+    def turned(value):
+        return value.astype(F32).T.astype(BF)
+
+    def prepare_forward(chunk, carry):
+        lanes = pl.ds(pl.multiple_of(chunk * half, half), half)
+        for other in range(chunks):
+            lines = slice(other * half, (other + 1) * half)
+            real, imag = turned(fresnel_cols[0, lines, lanes]), turned(fresnel_cols[1, lines, lanes])
+            left_lanes = slice(other * pair, other * pair + half)
+            right_lanes = slice(other * pair + half, (other + 1) * pair)
+            forward_cols[chunk, first_half, left_lanes] = real
+            forward_cols[chunk, first_half, right_lanes] = imag
+            forward_cols[chunk, second_half, left_lanes] = -imag
+            forward_cols[chunk, second_half, right_lanes] = real
+        return carry
+
+    lax.fori_loop(0, chunks, prepare_forward, 0)
+
+    def prepare_adjoint(chunk, carry):
+        lines = pl.ds(pl.multiple_of(chunk * half, half), half)
+        for other in range(chunks):
+            lanes = slice(other * half, (other + 1) * half)
+            real, imag = fresnel_cols[0, lines, lanes], fresnel_cols[1, lines, lanes]
+            left_lanes = slice(other * pair, other * pair + half)
+            right_lanes = slice(other * pair + half, (other + 1) * pair)
+            adjoint_cols[chunk, first_half, left_lanes] = real
+            adjoint_cols[chunk, first_half, right_lanes] = -imag
+            adjoint_cols[chunk, second_half, left_lanes] = imag
+            adjoint_cols[chunk, second_half, right_lanes] = real
+            for part in range(2):
+                block = forward_rows[pl.ds(pl.multiple_of(part * size + chunk * half, half), half), lanes]
+                adjoint_rows[part * size + other * half : part * size + (other + 1) * half, lines] = turned(block)
+        return carry
 
     pl.semaphore_wait(barrier, 2)
 
@@ -173,7 +439,7 @@
             @pl.when(me == last)
             def _():
                 psi_r, psi_i = parts_of(wave_out[position, chunk])
-                amplitude = measured[position, chunk]
+                amplitude = measured[position, :, pl.ds(pl.multiple_of(chunk * half, half), half)]
                 factor = 1.0 - amplitude * lax.rsqrt(psi_r * psi_r + psi_i * psi_i + 1.0)
                 cots[position, chunk] = both(psi_r * factor, psi_i * factor).astype(BF)
 
@@ -236,6 +502,10 @@
         is_back = late * (step % positions) + (1 - late) * (step // positions)
         position = late * (step // positions) + (1 - late) * (step % positions)
 
+        @pl.when(step == positions * (1 - late))
+        def _():
+            lax.fori_loop(0, chunks, prepare_adjoint, 0)
+
         @pl.when(is_back == 0)
         def _():
             forward(position)
@@ -265,14 +535,16 @@
     lax.fori_loop(0, positions * chunks, finish, 0)
 
 
-def column_blocks(matrix, chunks):
-    _, _, depth, width = matrix.shape
-    cut = matrix.reshape(2, 2, chunks, depth // chunks, chunks, width // chunks)
-    return cut.transpose(2, 0, 3, 4, 1, 5).reshape(chunks, 2 * depth // chunks, 2 * width)
-
-
 def in_vmem(count):
     return [pl.BlockSpec(memory_space=pltpu.VMEM)] * count
+
+
+def in_smem():
+    return [pl.BlockSpec(memory_space=pltpu.SMEM)]
+
+
+def on_chip(limit, **more):
+    return pltpu.CompilerParams(vmem_limit_bytes=limit * 2**20, **more)
 
 
 def shards(probe_wave, fresnel_rows, fresnel_cols, object_slices, offsets, measured):
@@ -283,93 +555,109 @@
     rows, width = owned.shape[1:]
     chunks = size // LANES
     pair = 2 * LANES
-    probe_index = lax.axis_index(PROBE)
-    probe_count = lax.axis_size(PROBE)
-
-    transmission = owned.astype(BF)
-    edges = jnp.concatenate([transmission[:, rows - MARGIN :], transmission[:, :MARGIN]], axis=1)
-    share = edges.shape[1] // probe_count
-    mine = lax.dynamic_slice_in_dim(edges, probe_index * share, share, 1)
-    swapped = lax.ppermute(mine, "tile", [(0, 1), (1, 0)])
-    theirs = lax.all_gather(swapped, PROBE, axis=1, tiled=True)
-    slab = jnp.concatenate([theirs[:, :MARGIN], transmission, theirs[:, MARGIN:]], axis=1).astype(F32)
-    slab = jnp.pad(slab, ((0, 0), (0, SUB), (0, 0)))
+    nx, ny = lax.axis_size("probe_0"), lax.axis_size("probe_1")
+    count = nx * ny
+    share = 2 * MARGIN // count
+    own = rows // count
+    each = own + share
+    dma = pltpu.SemaphoreType.DMA
+
+    edges = pl.pallas_call(
+        edge_kernel,
+        out_shape=jax.ShapeDtypeStruct((count, 2, share, width), BF),
+        in_specs=in_vmem(1),
+        out_specs=pl.BlockSpec(memory_space=pltpu.VMEM),
+        scratch_shapes=[
+            VMEM((2, share, width), BF),
+            VMEM((2, share, width), BF),
+            VMEM((count, 2, share, width), BF),
+            dma,
+            dma,
+            dma((count,)),
+            dma((count,)),
+        ],
+        compiler_params=on_chip(24, collective_id=1, has_side_effects=True),
+        name="edge",
+    )(owned)
 
     windows = pl.pallas_call(
         cut_kernel,
         out_shape=jax.ShapeDtypeStruct((positions, chunks, size, pair), BF),
-        in_specs=[pl.BlockSpec(memory_space=pltpu.SMEM)] + in_vmem(1),
+        in_specs=in_smem() + in_vmem(2),
         out_specs=pl.BlockSpec(memory_space=pltpu.VMEM),
+        scratch_shapes=[VMEM((2, rows + 2 * MARGIN + SUB, width), F32)],
+        compiler_params=on_chip(40),
         name="cut",
-    )(starts, slab)
-
-    col_r, col_i = fresnel_cols[0], fresnel_cols[1]
-    forward_cols = column_blocks(jnp.stack([jnp.stack([col_r.T, col_i.T]), jnp.stack([-col_i.T, col_r.T])]), chunks)
-    adjoint_cols = column_blocks(jnp.stack([jnp.stack([col_r, -col_i]), jnp.stack([col_i, col_r])]), chunks)
-    forward_rows = fresnel_rows.reshape(2 * size, size)
-    adjoint_rows = fresnel_rows.swapaxes(1, 2).reshape(2 * size, size)
-    probe = probe_wave.reshape(2, size, chunks, LANES).transpose(2, 1, 0, 3).reshape(chunks, size, pair)
-    amplitude = measured[0].reshape(positions, size, chunks, LANES).transpose(0, 2, 1, 3)
-
-    wave_stack = pltpu.VMEM((positions, chunks, size, pair), BF)
+    )(starts, owned, edges)
+
+    wave_stack = VMEM((positions, chunks, size, pair), BF)
+    columns = VMEM((chunks, pair, 2 * size), BF)
     grads, lights = pl.pallas_call(
         chain_kernel,
         out_shape=[
             jax.ShapeDtypeStruct((positions, chunks, size, pair), BF),
             jax.ShapeDtypeStruct((positions, chunks, size, LANES), BF),
         ],
-        in_specs=in_vmem(7),
+        in_specs=in_vmem(5),
         out_specs=in_vmem(2),
         scratch_shapes=[
+            columns,
+            columns,
+            VMEM((2 * size, size), BF),
             wave_stack,
             wave_stack,
             wave_stack,
             wave_stack,
-            pltpu.VMEM((size, 2 * size), F32),
-            pltpu.VMEM((chunks, size, pair), BF),
-            pltpu.VMEM((chunks, size, pair), BF),
-            pltpu.SemaphoreType.DMA((positions, chunks)),
-            pltpu.SemaphoreType.DMA((positions, chunks)),
-            pltpu.SemaphoreType.DMA((positions, chunks)),
-            pltpu.SemaphoreType.DMA((positions, chunks)),
+            VMEM((size, 2 * size), F32),
+            VMEM((chunks, size, pair), BF),
+            VMEM((chunks, size, pair), BF),
+            dma((positions, chunks)),
+            dma((positions, chunks)),
+            dma((positions, chunks)),
+            dma((positions, chunks)),
         ],
-        compiler_params=pltpu.CompilerParams(collective_id=0, has_side_effects=True, vmem_limit_bytes=60 * 2**20),
+        compiler_params=on_chip(60, collective_id=0, has_side_effects=True),
         name="chain",
-    )(probe, windows, forward_cols, adjoint_cols, forward_rows, adjoint_rows, amplitude)
-
-    own = rows // probe_count
-    edge = 2 * MARGIN // probe_count
+    )(probe_wave, windows, fresnel_cols, fresnel_rows.reshape(2 * size, size), measured[0])
+
     grid = pl.pallas_call(
         place_kernel,
-        out_shape=jax.ShapeDtypeStruct((probe_count, 3, own + edge, width), BF),
-        in_specs=[pl.BlockSpec(memory_space=pltpu.SMEM)] + in_vmem(2),
+        out_shape=jax.ShapeDtypeStruct((2, nx, 3 * ny, each, width // 2), BF),
+        in_specs=in_smem() + in_vmem(2),
         out_specs=pl.BlockSpec(memory_space=pltpu.VMEM),
-        scratch_shapes=[pltpu.VMEM((3, rows + 2 * MARGIN + SUB, width), F32)],
+        scratch_shapes=[VMEM((3, rows + 2 * MARGIN + SUB, width), F32)],
+        compiler_params=on_chip(40),
         name="place",
     )(starts, grads, lights)
 
-    summed = grid
-    for axis in PROBE:
-        summed = lax.psum_scatter(summed, axis, scatter_dimension=0, tiled=True)
-    summed = summed[0]
-    inside = summed[:, :own].astype(F32)
-    margin = summed[:, own:]
-    per_own = own // edge
-    half = probe_count // 2
-    received = []
-    for which in range(per_own):
-        pairs = []
-        for tile in range(2):
-            for index in range(which, probe_count, per_own):
-                if index < half:
-                    target = probe_count - half // per_own + index // per_own
-                else:
-                    target = (index - half) // per_own
-                pairs.append((tile * probe_count + index, (1 - tile) * probe_count + target))
-        received.append(lax.ppermute(margin, TILE_PROBE, pairs))
-    full = inside + jnp.concatenate(received, axis=1).astype(F32)
-    own_part = lax.dynamic_slice_in_dim(owned, probe_index * own, own, 1)
-    updated = own_part - full[:2] / (full[2] + 1.0)
+    def slots(depth):
+        return VMEM((2, depth, each, width // 2), BF)
+
+    def ring(depth):
+        cut = (depth + 1) // 2
+        return [slots(cut), slots(depth - cut), slots(cut), slots(depth - cut), slots(depth), slots(depth)]
+
+    updated = pl.pallas_call(
+        reduce_kernel,
+        out_shape=jax.ShapeDtypeStruct((2, own, width), F32),
+        in_specs=in_vmem(1) + [pl.BlockSpec(memory_space=pl.ANY)],
+        out_specs=pl.BlockSpec(memory_space=pltpu.VMEM),
+        scratch_shapes=ring(3 * ny)
+        + [VMEM((2, ny, 3, each, width // 2), BF)]
+        + ring(3)
+        + [
+            slots(3),
+            VMEM((2, 2, 3, share, width // 2), BF),
+            VMEM((2, own, width), F32),
+            dma((2, 2, 6)),
+            dma((2, 2, 6)),
+            dma,
+            dma((2,)),
+            dma,
+        ],
+        compiler_params=on_chip(40, collective_id=2, has_side_effects=True),
+        name="reduce",
+    )(grid, owned)
     return updated[None]
 
 

time: 377 us -> 231 us (0.61)
  waiting for transfers between devices: 77.6 us -> 0 us
  Pallas kernels: 167 us -> 224 us
  local copies, waits for them, and re-layouts: 50.5 us -> 6.74 us
  blocking collectives: 24.2 us -> 0 us
  other arithmetic: 22.5 us -> 0 us
  starting transfers between devices: 20.6 us -> 0 us
  between operations: 13.5 us -> 0.07 us
    reduce_scatter x2 -> x0, waiting for transfers between devices: 64.7 us -> none  [shards(): summed = lax.psum_scatter(summed, axis, scatter_dimension=0, tiled=True)]
    pallas_call x1 -> x3, Pallas kernels: 8.42 us -> 69.1 us  [the longest x1 39.8 us: shards(): pl.pallas_call(reduce_kernel, out_shape=jax.ShapeDtypeStruct((2, own, wid...]
    another operation x11 -> x0, local copies, waits for them, and re-layouts: 30.5 us -> none  [the longest x4 11.6 us: shards(): jnp.stack([col_r.T, col_i.T])]
    all_gather x1 -> x0, blocking collectives: 24.2 us -> none  [shards(): theirs = lax.all_gather(swapped, PROBE, axis=1, tiled=True)]
    ppermute x3 -> x0, starting transfers between devices: 20.6 us -> none  [the longest x2 13.3 us: shards(): received.append(lax.ppermute(margin, TILE_PROBE, pairs))]
    reshape x5 -> x0, local copies, waits for them, and re-layouts: 13.8 us -> none  [the longest x2 8.9 us: column_blocks(): cut.transpose(2, 0, 3, 4, 1, 5)]
    ppermute x3 -> x0, waiting for transfers between devices: 12.9 us -> none  [the longest x2 12.9 us: shards(): received.append(lax.ppermute(margin, TILE_PROBE, pairs))]
    transpose x2 -> x0, other arithmetic: 10 us -> none  [column_blocks(): cut.transpose(2, 0, 3, 4, 1, 5)]
  transfers between devices with their start and end apart: 5 -> 0, of which waited for: 4 -> 0; matrix products, arithmetic and copies ran while one was open for 17% -> 0% of each run, Pallas kernels for 0% -> 0%
where the time goes in v2:
time: 231 us
  Pallas kernels  224 us (97%)
  local copies, waits for them, and re-layouts  6.74 us (3%)
    pallas_call x1, Pallas kernels, shards(): pl.pallas_call(chain_kernel, out_shape=[jax.ShapeDtypeStruct((positions,...  150 us
    pallas_call x1, Pallas kernels, shards(): pl.pallas_call(reduce_kernel, out_shape=jax.ShapeDtypeStruct((2, own, wid...  39.8 us
    pallas_call x1, Pallas kernels, shards(): pl.pallas_call(edge_kernel, out_shape=jax.ShapeDtypeStruct((count, 2, sha...  23.9 us
    unnamed x13, local copies, waits for them, and re-layouts  6.74 us
    pallas_call x1, Pallas kernels, shards(): pl.pallas_call(place_kernel, out_shape=jax.ShapeDtypeStruct((2, nx, 3 * n...  5.38 us

profile of v2, /device:TPU:8, one launch (start us, length us, event | category | flops | bytes accessed | tf_op | source)
XLA Modules:
  0.0 230.8 jit_solution(5964152113363614473)
XLA Ops:
  0.0 0.0 copy-start.5
  0.0 0.0 copy-start
  0.0 1.9 copy-done
  1.9 0.0 copy-start.1
  1.9 23.9 %edge.1.edges = bf16[16,2,16,768]{3,2,1,0:T(8,128)(2,1)S(1)} custom-call(f32[2,512,768]{2,1,0:T(8,128)S(1)} %bitcast.5), custom_call_target="tpu_custom_call" | custom-call | tf_op jit(solution)/shard_map/edge/pallas_call | solution.py:565
  25.8 0.0 copy-done.5
  25.8 0.0 copy-done.1
  25.8 4.5 %cut.1.windows = bf16[2,4,512,256]{3,2,1,0:T(8,128)(2,1)S(1)} custom-call(s32[2,2]{1,0:T(2,128)S(1)} %bitcast.9, f32[2,512,768]{2,1,0:T(8,128)S(1)} %bitcast.6, bf16[16,2,16,768]{3,2,1,0:T(8,128)(2,1)S(1)} %edge.1.edges), custom_call_target="tpu_custom_call" | custom-call | tf_op jit(solution)/shard_map/cut/pallas_call | solution.py:583
  30.3 0.0 copy-start.2
  30.3 1.3 copy-done.2
  31.7 150.4 %chain.1 = (bf16[2,4,512,256]{3,2,1,0:T(8,128)(2,1)}, bf16[2,4,512,128]{3,2,1,0:T(8,128)(2,1)}) custom-call(bf16[2,512,512]{2,1,0:T(8,128)(2,1)} %probe.1, bf16[2,4,512,256]{3,2,1,0:T(8,128)(2,1)} %copy-done.2, bf16[2,512,512]{2,1,0:T(8,128)(2,1)} %fresnel_cols.1, bf16[1024,512]{1,0:T(8,128)(2,1)} %bitcast.12, f32[2,512,512]{2,1,0:T(8,128)} %bitcast.11), custom_call_target="tpu_custom_call" | custom-call | tf_op jit(solution)/shard_map/chain/pallas_call | solution.py:595
  182.1 0.0 copy-start.3
  182.1 1.6 copy-done.3
  183.7 0.0 copy-start.4
  183.7 1.2 copy-done.4
  184.9 5.4 %place.1.grid = bf16[2,4,12,48,384]{4,3,2,1,0:T(8,128)(2,1)S(1)} custom-call(s32[2,2]{1,0:T(2,128)S(1)} %bitcast.10, bf16[2,4,512,256]{3,2,1,0:T(8,128)(2,1)S(1)} %copy-done.3, bf16[2,4,512,128]{3,2,1,0:T(8,128)(2,1)S(1)} %copy-done.4), custom_call_target="tpu_custom_call" | custom-call | tf_op jit(solution)/shard_map/place/pallas_call | solution.py:623
  190.3 39.8 %reduce.1 = f32[2,32,768]{2,1,0:T(8,128)S(1)} custom-call(bf16[2,4,12,48,384]{4,3,2,1,0:T(8,128)(2,1)S(1)} %place.1.grid, f32[2,512,768]{2,1,0:T(8,128)S(1)} %bitcast.7), custom_call_target="tpu_custom_call" | custom-call | tf_op jit(solution)/shard_map/reduce/pallas_call | solution.py:640
  230.1 0.7 copy.8
Async XLA Ops:
  0.0 25.8 %copy-start.5 = (s32[1,2,2]{2,1,0:T(2,128)S(1)}, s32[1,2,2]{2,1,0:T(2,128)}, u32[]{:S(2)}) copy-start(s32[1,2,2]{2,1,0:T(2,128)} %param.10) | copy-start | bytes 52
  0.0 1.9 copy-start
  1.9 23.9 %copy-start.1 = (f32[1,2,512,768]{3,2,1,0:T(8,128)S(1)}, f32[1,2,512,768]{3,2,1,0:T(8,128)}, u32[]{:S(2)}) copy-start(f32[1,2,512,768]{3,2,1,0:T(8,128)} %param.9) | copy-start | bytes 9437188
  30.3 1.4 copy-start.2
  182.1 1.6 copy-start.3
  183.7 1.2 copy-start.4

commit v3 on v2

v3 whole, which is shorter than its diff:
```python
import jax
import jax.numpy as jnp
from jax import lax
from jax.experimental import pallas as pl
from jax.experimental.pallas import tpu as pltpu
from jax.sharding import Mesh
from jax.sharding import PartitionSpec as P

MARGIN = 128
LANES = 128
SUB = 8
HOSTED = 2
PROBE = ("probe_0", "probe_1")
TILE_PROBE = ("tile", "probe_0", "probe_1")
MESH_ID = pl.DeviceIdType.MESH
BF = jnp.bfloat16
F32 = jnp.float32
VMEM = pltpu.VMEM


def edge_kernel(owned, out, mine, got, gathered, send_z, recv_z, send_sem, recv_sem):
    tile, x, y = lax.axis_index("tile"), lax.axis_index("probe_0"), lax.axis_index("probe_1")
    nx, ny = lax.axis_size("probe_0"), lax.axis_size("probe_1")
    count = nx * ny
    me = x * ny + y
    rows = owned.shape[1]
    share = mine.shape[1]
    half = count // 2
    mate = {"tile": 1 - tile}

    def peer(step):
        other = lax.rem(me + step, count)
        return {"probe_0": other // ny, "probe_1": lax.rem(other, ny)}

    barrier = pltpu.get_barrier_semaphore()
    pl.semaphore_signal(barrier, inc=1, device_id=mate, device_id_type=MESH_ID)
    for step in range(1, count):
        pl.semaphore_signal(barrier, inc=1, device_id=peer(step), device_id_type=MESH_ID)

    lower = me // half
    first = (1 - lower) * (rows - MARGIN + me * share) + lower * (me - half) * share
    mine[...] = owned[:, pl.ds(pl.multiple_of(first, share), share), :].astype(BF)
    pl.semaphore_wait(barrier, count)

    swap = pltpu.make_async_remote_copy(
        src_ref=mine, dst_ref=got, send_sem=send_z, recv_sem=recv_z, device_id=mate, device_id_type=MESH_ID
    )
    swap.start()
    swap.wait_recv()

    def share_copy(step):
        return pltpu.make_async_remote_copy(
            src_ref=got,
            dst_ref=gathered.at[me],
            send_sem=send_sem.at[step],
            recv_sem=recv_sem.at[me],
            device_id=peer(step),
            device_id_type=MESH_ID,
        )

    def arrival(step):
        sender = lax.rem(me + count - step, count)
        return pltpu.make_async_remote_copy(
            src_ref=got,
            dst_ref=gathered.at[sender],
            send_sem=send_sem.at[step],
            recv_sem=recv_sem.at[sender],
            device_id=peer(step),
            device_id_type=MESH_ID,
        )

    for step in range(1, count):
        share_copy(step).start()
    out[me] = got[...]
    for step in range(1, count):
        arrival(step).wait_recv()
        sender = lax.rem(me + count - step, count)
        out[sender] = gathered[sender]
    swap.wait_send()
    for step in range(1, count):
        share_copy(step).wait_send()


def cut_kernel(starts, owned, edges, out, slab):
    positions, chunks, size, _ = out.shape
    rows, width = owned.shape[1:]
    count, _, share, _ = edges.shape
    block = 64
    for index in range(count):
        first = index * share + (rows if index >= count // 2 else 0)
        slab[:, first : first + share, :] = edges[index].astype(F32)
    slab[:, MARGIN : MARGIN + rows, :] = owned[...].astype(BF).astype(F32)
    slab[:, rows + 2 * MARGIN :, :] = jnp.zeros((2, SUB, width), F32)
    for position in range(positions):
        row = starts[position, 0]
        col = starts[position, 1]
        shift = lax.rem(width - col, width)
        base = row // SUB * SUB
        drop = lax.rem(block + SUB - lax.rem(row, SUB), block + SUB)

        def lines(step, carry):
            at = pl.multiple_of(step * block, block)
            for part in range(2):
                values = slab[part, pl.ds(pl.multiple_of(base + at, SUB), block + SUB), :]
                turned = pltpu.roll(values, shift, 1)[:, :size]
                turned = pltpu.roll(turned, drop, 0)[:block]
                for chunk in range(chunks):
                    out[position, chunk, pl.ds(at, block), part * LANES : (part + 1) * LANES] = turned[
                        :, chunk * LANES : (chunk + 1) * LANES
                    ].astype(BF)
            return carry

        lax.fori_loop(0, size // block, lines, 0)


def active_slots(me, count):
    return (1 + me // (count - 4)) * (1 - me // (count - 2))


def place_kernel(starts, grads, lights, out, total):
    _, positions, chunks, size, _ = grads.shape
    _, _, nx, ny, each, width = out.shape
    ny //= 3
    width *= 2
    block = 64
    own = 2 * each // 3
    edge = each - own

    def one_slot(slot, carry):
        total[...] = jnp.zeros_like(total)
        for position in range(positions):
            row = starts[position, 0]
            col = starts[position, 1]
            base = row // SUB * SUB
            drop = lax.rem(row, SUB)

            def rows(step, inner):
                at = pl.multiple_of(step * block, block)
                for part in range(3):
                    pieces = []
                    for chunk in range(chunks):
                        if part < 2:
                            piece = grads[slot, position, chunk, pl.ds(at, block), part * LANES : (part + 1) * LANES]
                        else:
                            piece = lights[slot, position, chunk, pl.ds(at, block), :]
                        pieces.append(piece.astype(F32))
                    lines = jnp.concatenate(pieces, axis=1)
                    lines = pltpu.roll(jnp.concatenate([lines, jnp.zeros((SUB, size), F32)], axis=0), drop, 0)
                    lines = jnp.concatenate([lines, jnp.zeros((block + SUB, width - size), F32)], axis=1)
                    turned = pltpu.roll(lines, col, 1)
                    where = pl.ds(pl.multiple_of(base + at, SUB), block + SUB)
                    total[part, where, :] = total[part, where, :] + turned
                return inner

            lax.fori_loop(0, size // block, rows, 0)
        for x in range(nx):
            for y in range(ny):
                index = x * ny + y
                first = MARGIN + index * own
                second = index * edge + (nx * ny * own if 2 * index >= nx * ny else 0)
                for side in range(2):
                    major, minor = (x, y) if side == 0 else (y, x)
                    lanes = slice(side * width // 2, (side + 1) * width // 2)
                    place = slice(3 * minor, 3 * minor + 3)
                    out[slot, side, major, place, 0:own, :] = total[:, first : first + own, lanes].astype(BF)
                    out[slot, side, major, place, own:each, :] = total[:, second : second + edge, lanes].astype(BF)
        return carry

    lax.fori_loop(0, active_slots(lax.axis_index("cuts"), lax.axis_size("cuts")), one_slot, 0)


def reduce_kernel(
    grids, owned, out,
    held, pre_up, pre_down, staged_up, staged_down, got_up, got_down, partial,
    pre_up2, pre_down2, staged_up2, staged_down2, got_up2, got_down2,
    final, extra, rows_here, ratio, incoming,
    send_sem, recv_sem, send_m, recv_m, send_d, recv_d, local_sem, held_sem,
):
    tile = lax.axis_index("tile")
    where = {"probe_0": lax.axis_index("probe_0"), "probe_1": lax.axis_index("probe_1")}
    sizes = {"probe_0": lax.axis_size("probe_0"), "probe_1": lax.axis_size("probe_1")}
    nx, ny = sizes["probe_0"], sizes["probe_1"]
    count = nx * ny
    me = where["probe_0"] * ny + where["probe_1"]
    cut = lax.axis_index("cuts")
    cuts = lax.axis_size("cuts")
    last = cuts - 3
    slots = active_slots(cut, cuts)
    each = grids.shape[4]
    own = 2 * each // 3
    edge = each - own
    lanes = grids.shape[5]
    half = count // 2
    order = (("probe_0", "probe_1"), ("probe_1", "probe_0"))

    def device(index):
        return {"tile": 1 - tile, "probe_0": index // ny, "probe_1": lax.rem(index, ny)}

    lower = me // half
    target = (1 - lower) * (count - half // 2 + me // 2) + lower * ((me - half) // 2)
    outer = where["probe_0"] // (nx - 1) + (nx - 1 - where["probe_0"]) // (nx - 1)
    source = where["probe_0"] // (nx - 1) * (2 * (me - count + half // 2)) + (
        nx - 1 - where["probe_0"]
    ) // (nx - 1) * (half + 2 * me)

    fetch = pltpu.make_async_copy(owned.at[:, pl.ds(pl.multiple_of(me * own, own), own), :], rows_here, local_sem)
    fetch.start()

    def load(slot):
        return pltpu.make_async_copy(grids.at[slot], held.at[slot], held_sem.at[slot])

    def start_load(slot, carry):
        load(slot).start()
        return carry

    lax.fori_loop(0, slots, start_load, 0)

    barrier = pltpu.get_barrier_semaphore()

    @pl.when(cut >= last)
    def _():
        host = last - 1 + cut // (last + 1)
        pl.semaphore_signal(barrier, inc=1, device_id={"cuts": host}, device_id_type=MESH_ID)

    @pl.when(cut <= last)
    def _():
        for axis in ("probe_0", "probe_1"):
            for step in (1, sizes[axis] - 1):
                other = {axis: lax.rem(where[axis] + step, sizes[axis])}
                pl.semaphore_signal(barrier, inc=1, device_id=other, device_id_type=MESH_ID)

        @pl.when(outer == 1)
        def _():
            for which in range(2):
                pl.semaphore_signal(barrier, inc=1, device_id=device(source + which), device_id_type=MESH_ID)

        pl.semaphore_wait(barrier, 5 + cut // (last - 1) + cut // last)

    def copies(slot, stage, side, src, bufs):
        axis = order[side][stage]
        size = sizes[axis]
        here = where[axis]
        plus, minus = lax.rem(here + 1, size), lax.rem(here + size - 1, size)
        opposite = lax.rem(here + 2, size)
        up_pre, down_pre, up_staged, down_staged, up_got, down_got = bufs
        depth = src.shape[1]
        cut = (depth + 1) // 2
        low, high = pl.ds(0, cut), pl.ds(cut, depth - cut)

        def copy(index, source_ref, target_ref, to):
            return pltpu.make_async_remote_copy(
                src_ref=source_ref,
                dst_ref=target_ref,
                send_sem=send_sem.at[slot, stage, side, index],
                recv_sem=recv_sem.at[slot, stage, side, index],
                device_id={axis: to},
                device_id_type=MESH_ID,
            )

        return (
            copy(0, src.at[opposite, low], up_pre.at[side], plus),
            copy(1, src.at[opposite, high], down_pre.at[side], minus),
            copy(2, src.at[plus, high], up_got.at[side, high], plus),
            copy(3, src.at[minus, low], down_got.at[side, low], minus),
            copy(4, up_staged.at[side], up_got.at[side, low], plus),
            copy(5, down_staged.at[side], down_got.at[side, high], minus),
        ), (here, plus, minus, low, high)

    def begin(slot, stage, side, src, bufs):
        made, _ = copies(slot, stage, side, src, bufs)
        for index in range(4):
            made[index].start()

    def relay(slot, stage, side, src, bufs):
        made, (_, plus, minus, low, high) = copies(slot, stage, side, src, bufs)
        up_pre, down_pre, up_staged, down_staged, _, _ = bufs
        made[0].wait_recv()
        up_staged[side] = (up_pre[side].astype(F32) + src[plus, low].astype(F32)).astype(BF)
        made[4].start()
        made[1].wait_recv()
        down_staged[side] = (down_pre[side].astype(F32) + src[minus, high].astype(F32)).astype(BF)
        made[5].start()

    def settle(slot, stage, side, src, bufs):
        made, (here, _, _, _, _) = copies(slot, stage, side, src, bufs)
        for index in range(2, 6):
            made[index].wait_recv()
        up_got, down_got = bufs[4], bufs[5]
        return src[here].astype(F32) + up_got[side].astype(F32) + down_got[side].astype(F32)

    def drain(slot, stage, side, src, bufs):
        for copy in copies(slot, stage, side, src, bufs)[0]:
            copy.wait_send()

    def ring_of(slot, buffers):
        return tuple(buffer.at[slot] for buffer in buffers)

    def margin_copy(slot, piece):
        return pltpu.make_async_remote_copy(
            src_ref=final.at[slot, :, :, pl.ds(own, edge), :],
            dst_ref=extra.at[slot, piece],
            send_sem=send_m.at[slot],
            recv_sem=recv_m.at[slot, piece],
            device_id=device(target),
            device_id_type=MESH_ID,
        )

    def deliver(slot):
        return pltpu.make_async_remote_copy(
            src_ref=ratio.at[slot],
            dst_ref=incoming,
            send_sem=send_d.at[slot],
            recv_sem=recv_d,
            device_id={"cuts": lax.rem(cut + 1 + slot * (cut - last + 1), cuts)},
            device_id_type=MESH_ID,
        )

    def one_slot(slot, carry):
        load(slot).wait()
        grid = held.at[slot]
        part_sums = partial.at[slot]
        one = ring_of(slot, (pre_up, pre_down, staged_up, staged_down, got_up, got_down))
        two = ring_of(slot, (pre_up2, pre_down2, staged_up2, staged_down2, got_up2, got_down2))
        for side in range(2):
            begin(slot, 0, side, grid.at[side], one)
        for side in range(2):
            relay(slot, 0, side, grid.at[side], one)
        for side in range(2):
            summed = settle(slot, 0, side, grid.at[side], one).astype(BF)
            for index in range(ny):
                part_sums[side, index] = summed[3 * index : 3 * index + 3]
            begin(slot, 1, side, part_sums.at[side], two)
        for side in range(2):
            relay(slot, 1, side, part_sums.at[side], two)
        for side in range(2):
            final[slot, side] = settle(slot, 1, side, part_sums.at[side], two).astype(BF)
        margin_copy(slot, lax.rem(me, 2)).start()

        @pl.when(outer == 0)
        def _():
            extra[slot] = jnp.zeros(extra.shape[1:], extra.dtype)

        @pl.when(outer == 1)
        def _():
            for piece in range(2):
                margin_copy(slot, piece).wait_recv()

        for side in range(2):
            columns = slice(side * lanes, (side + 1) * lanes)
            for piece in range(2):
                lines = slice(piece * edge, (piece + 1) * edge)
                full = final[slot, side, :, lines, :].astype(F32) + extra[slot, piece, side].astype(F32)
                scale = 1.0 / (full[2] + 1.0)
                for part in range(2):
                    ratio[slot, part, lines, columns] = full[part] * scale

        @pl.when((cut == last) | (slot > 0))
        def _():
            deliver(slot).start()

        return carry

    lax.fori_loop(0, slots, one_slot, 0)
    fetch.wait()

    @pl.when(cut < last)
    def _():
        out[...] = rows_here[...] - ratio[0]

    @pl.when(cut >= last)
    def _():
        deliver(0).wait_recv()
        out[...] = rows_here[...] - incoming[...]

    def finish(slot, carry):
        one = ring_of(slot, (pre_up, pre_down, staged_up, staged_down, got_up, got_down))
        two = ring_of(slot, (pre_up2, pre_down2, staged_up2, staged_down2, got_up2, got_down2))
        for side in range(2):
            drain(slot, 0, side, held.at[slot].at[side], one)
            drain(slot, 1, side, partial.at[slot].at[side], two)
        margin_copy(slot, lax.rem(me, 2)).wait_send()

        @pl.when((cut == last) | (slot > 0))
        def _():
            deliver(slot).wait_send()

        return carry

    lax.fori_loop(0, slots, finish, 0)


def chain_kernel(
    probe, windows, fresnel_cols, forward_rows, measured,
    grads, lights,
    cuts, forward_cols, adjoint_cols, adjoint_rows,
    waves, cots, wave_out, cot_out, total, middle, backs,
    send_f, recv_f, send_b, recv_b, send_w, recv_w,
):
    me = lax.axis_index("cuts")
    count = lax.axis_size("cuts")
    last = count - 3
    right = lax.rem(me + 1, count)
    left = lax.rem(me + count - 1, count)
    positions, chunks, size, pair = windows.shape
    half = pair // 2
    hosted = 1 + me // (last - 1)

    barrier = pltpu.get_barrier_semaphore()
    for other in (left, right):
        pl.semaphore_signal(barrier, inc=1, device_id={"cuts": other}, device_id_type=MESH_ID)

    @pl.when(me == last)
    def _():
        pl.semaphore_signal(barrier, inc=1, device_id={"cuts": count - 1}, device_id_type=MESH_ID)

    first_half, second_half = slice(0, half), slice(half, pair)

    @pl.when(me == 0)
    def _():
        for position in range(positions):
            for chunk in range(chunks):
                lanes = slice(chunk * half, (chunk + 1) * half)
                waves[0, position, chunk, :, first_half] = probe[0, :, lanes]
                waves[0, position, chunk, :, second_half] = probe[1, :, lanes]

    pl.semaphore_wait(barrier, 2 + me // (count - 1))

    def window_copy(position, slot, target):
        return pltpu.make_async_remote_copy(
            src_ref=windows.at[position],
            dst_ref=cuts.at[slot, position],
            send_sem=send_w.at[position],
            recv_sem=recv_w.at[slot, position],
            device_id={"cuts": target},
            device_id_type=MESH_ID,
        )

    give_slot = 1 - lax.rem(me + 1, 2) * (me // (last + 1))
    give_to = last - 1 + me // (last + 1)

    @pl.when(me >= last)
    def _():
        for position in range(positions):
            window_copy(position, give_slot, give_to).start()

    @pl.when(me < last)
    def _():
        cuts[0] = windows[...]

    def turned(value):
        return value.astype(F32).T.astype(BF)

    def prepare_forward(chunk, carry):
        lanes = pl.ds(pl.multiple_of(chunk * half, half), half)
        for other in range(chunks):
            lines = slice(other * half, (other + 1) * half)
            real, imag = turned(fresnel_cols[0, lines, lanes]), turned(fresnel_cols[1, lines, lanes])
            left_lanes = slice(other * pair, other * pair + half)
            right_lanes = slice(other * pair + half, (other + 1) * pair)
            forward_cols[chunk, first_half, left_lanes] = real
            forward_cols[chunk, first_half, right_lanes] = imag
            forward_cols[chunk, second_half, left_lanes] = -imag
            forward_cols[chunk, second_half, right_lanes] = real
        return carry

    def prepare_adjoint(chunk, carry):
        lines = pl.ds(pl.multiple_of(chunk * half, half), half)
        for other in range(chunks):
            lanes = slice(other * half, (other + 1) * half)
            real, imag = fresnel_cols[0, lines, lanes], fresnel_cols[1, lines, lanes]
            left_lanes = slice(other * pair, other * pair + half)
            right_lanes = slice(other * pair + half, (other + 1) * pair)
            adjoint_cols[chunk, first_half, left_lanes] = real
            adjoint_cols[chunk, first_half, right_lanes] = -imag
            adjoint_cols[chunk, second_half, left_lanes] = imag
            adjoint_cols[chunk, second_half, right_lanes] = real
            for part in range(2):
                block = forward_rows[pl.ds(pl.multiple_of(part * size + chunk * half, half), half), lanes]
                adjoint_rows[part * size + other * half : part * size + (other + 1) * half, lines] = turned(block)
        return carry

    def forward_copy(position, chunk):
        return pltpu.make_async_remote_copy(
            src_ref=wave_out.at[position, chunk],
            dst_ref=waves.at[0, position, chunk],
            send_sem=send_f.at[position, chunk],
            recv_sem=recv_f.at[position, chunk],
            device_id={"cuts": right},
            device_id_type=MESH_ID,
        )

    def adjoint_copy(position, chunk):
        return pltpu.make_async_remote_copy(
            src_ref=cot_out.at[position, chunk],
            dst_ref=cots.at[position, chunk],
            send_sem=send_b.at[position, chunk],
            recv_sem=recv_b.at[position, chunk],
            device_id={"cuts": left},
            device_id_type=MESH_ID,
        )

    def parts_of(value):
        value = value.astype(F32)
        return value[:, :half], value[:, half:]

    def both(real, imag):
        return jnp.concatenate([real, imag], axis=1)

    def add_product(chunk, value, matrix):
        product = jnp.dot(value, matrix, preferred_element_type=F32)
        if chunk == 0:
            total[...] = product
        elif chunk < chunks - 1:
            total[...] += product
        else:
            product = (total[...] + product).astype(BF)
            for other in range(chunks):
                middle[other] = product[:, other * pair : (other + 1) * pair]

    def forward(position):
        def hosted_slice(slot, carry):
            @pl.when((me >= last) | (slot > 0))
            def _():
                window_copy(position, slot, give_to).wait_recv()

            for chunk in range(chunks):
                @pl.when((me > 0) & (slot == 0))
                def _():
                    forward_copy(position, chunk).wait_recv()

                wave_r, wave_i = parts_of(waves[slot, position, chunk])
                win_r, win_i = parts_of(cuts[slot, position, chunk])
                out = both(wave_r * win_r - wave_i * win_i, wave_r * win_i + wave_i * win_r).astype(BF)
                add_product(chunk, out, forward_cols[chunk])

            def produce(chunk, inner):
                result = jnp.dot(forward_rows[...], middle[chunk], preferred_element_type=F32)
                real = result[:size, :half] - result[size:, half:]
                imag = result[size:, :half] + result[:size, half:]
                value = both(real, imag).astype(BF)

                @pl.when(slot < hosted - 1)
                def _():
                    waves[1, position, chunk] = value

                @pl.when(slot == hosted - 1)
                def _():
                    wave_out[position, chunk] = value

                    @pl.when(me < last)
                    def _():
                        forward_copy(position, chunk).start()

                    @pl.when(me == last)
                    def _():
                        psi_r, psi_i = parts_of(value)
                        amplitude = measured[position, :, pl.ds(pl.multiple_of(chunk * half, half), half)]
                        factor = 1.0 - amplitude * lax.rsqrt(psi_r * psi_r + psi_i * psi_i + 1.0)
                        cots[position, chunk] = both(psi_r * factor, psi_i * factor).astype(BF)

                return inner

            lax.fori_loop(0, chunks, produce, 0)

            def brighten(chunk, inner):
                wave_r, wave_i = parts_of(waves[slot, position, chunk])
                lights[slot, position, chunk] = (wave_r * wave_r + wave_i * wave_i).astype(BF)
                return inner

            lax.fori_loop(0, chunks, brighten, 0)
            return carry

        lax.fori_loop(0, hosted, hosted_slice, 0)

    def adjoint(position):
        def hosted_slice(step, carry):
            slot = hosted - 1 - step
            for chunk in range(chunks):
                @pl.when((me < last) & (step == 0))
                def _():
                    adjoint_copy(position, chunk).wait_recv()

                add_product(chunk, cots[position, chunk], adjoint_cols[chunk])

            def produce(chunk, inner):
                result = jnp.dot(adjoint_rows[...], middle[chunk], preferred_element_type=F32)
                real = result[:size, :half] + result[size:, half:]
                imag = result[:size, half:] - result[size:, :half]
                back = both(real, imag).astype(BF)
                backs[chunk] = back

                @pl.when(me > 0)
                def _():
                    back_r, back_i = parts_of(back)
                    win_r, win_i = parts_of(cuts[slot, position, chunk])
                    value = both(win_r * back_r + win_i * back_i, win_r * back_i - win_i * back_r).astype(BF)

                    @pl.when(slot > 0)
                    def _():
                        cots[position, chunk] = value

                    @pl.when(slot == 0)
                    def _():
                        cot_out[position, chunk] = value
                        adjoint_copy(position, chunk).start()

                return inner

            lax.fori_loop(0, chunks, produce, 0)

            def grade(chunk, inner):
                wave_r, wave_i = parts_of(waves[slot, position, chunk])
                back_r, back_i = parts_of(backs[chunk])
                grads[slot, position, chunk] = both(
                    wave_r * back_r + wave_i * back_i, wave_r * back_i - wave_i * back_r
                ).astype(BF)
                return inner

            lax.fori_loop(0, chunks, grade, 0)
            return carry

        lax.fori_loop(0, hosted, hosted_slice, 0)

    late = me // last

    @pl.when(me <= last)
    def _():
        lax.fori_loop(0, chunks, prepare_forward, 0)

        def phase(step, carry):
            is_back = late * (step % positions) + (1 - late) * (step // positions)
            position = late * (step // positions) + (1 - late) * (step % positions)

            @pl.when(step == positions * (1 - late))
            def _():
                lax.fori_loop(0, chunks, prepare_adjoint, 0)

            @pl.when(is_back == 0)
            def _():
                forward(position)

            @pl.when(is_back == 1)
            def _():
                adjoint(position)

            return carry

        lax.fori_loop(0, 2 * positions, phase, 0)

    def finish(index, carry):
        position = index // chunks
        chunk = index % chunks

        @pl.when(me < last)
        def _():
            forward_copy(position, chunk).wait_send()

        @pl.when((me > 0) & (me <= last))
        def _():
            adjoint_copy(position, chunk).wait_send()

        return carry

    lax.fori_loop(0, positions * chunks, finish, 0)

    @pl.when(me >= last)
    def _():
        for position in range(positions):
            window_copy(position, give_slot, give_to).wait_send()


def in_vmem(count):
    return [pl.BlockSpec(memory_space=pltpu.VMEM)] * count


def in_smem():
    return [pl.BlockSpec(memory_space=pltpu.SMEM)]


def on_chip(limit, **more):
    return pltpu.CompilerParams(vmem_limit_bytes=limit * 2**20, **more)


def run_chain(probe_wave, windows, fresnel_cols, fresnel_rows, amplitude):
    positions, chunks, size, pair = windows.shape
    dma = pltpu.SemaphoreType.DMA
    wave_stack = VMEM((positions, chunks, size, pair), BF)
    hosted_stack = VMEM((HOSTED, positions, chunks, size, pair), BF)
    columns = VMEM((chunks, pair, 2 * size), BF)
    return pl.pallas_call(
        chain_kernel,
        out_shape=[
            jax.ShapeDtypeStruct((HOSTED, positions, chunks, size, pair), BF),
            jax.ShapeDtypeStruct((HOSTED, positions, chunks, size, LANES), BF),
        ],
        in_specs=in_vmem(5),
        out_specs=in_vmem(2),
        scratch_shapes=[
            hosted_stack,
            columns,
            columns,
            VMEM((2 * size, size), BF),
            hosted_stack,
            wave_stack,
            wave_stack,
            wave_stack,
            VMEM((size, 2 * size), F32),
            VMEM((chunks, size, pair), BF),
            VMEM((chunks, size, pair), BF),
            dma((positions, chunks)),
            dma((positions, chunks)),
            dma((positions, chunks)),
            dma((positions, chunks)),
            dma((positions,)),
            dma((HOSTED, positions)),
        ],
        compiler_params=on_chip(60, collective_id=0, has_side_effects=True),
        name="chain",
    )(probe_wave, windows, fresnel_cols, fresnel_rows.reshape(2 * size, size), amplitude)


def shards(probe_wave, fresnel_rows, fresnel_cols, object_slices, offsets, measured):
    owned = object_slices[0]
    starts = offsets[0]
    size = probe_wave.shape[1]
    positions = starts.shape[0]
    rows, width = owned.shape[1:]
    chunks = size // LANES
    pair = 2 * LANES
    nx, ny = lax.axis_size("probe_0"), lax.axis_size("probe_1")
    count = nx * ny
    share = 2 * MARGIN // count
    own = rows // count
    each = own + share
    dma = pltpu.SemaphoreType.DMA

    edges = pl.pallas_call(
        edge_kernel,
        out_shape=jax.ShapeDtypeStruct((count, 2, share, width), BF),
        in_specs=in_vmem(1),
        out_specs=pl.BlockSpec(memory_space=pltpu.VMEM),
        scratch_shapes=[
            VMEM((2, share, width), BF),
            VMEM((2, share, width), BF),
            VMEM((count, 2, share, width), BF),
            dma,
            dma,
            dma((count,)),
            dma((count,)),
        ],
        compiler_params=on_chip(24, collective_id=1, has_side_effects=True),
        name="edge",
    )(owned)

    windows = pl.pallas_call(
        cut_kernel,
        out_shape=jax.ShapeDtypeStruct((positions, chunks, size, pair), BF),
        in_specs=in_smem() + in_vmem(2),
        out_specs=pl.BlockSpec(memory_space=pltpu.VMEM),
        scratch_shapes=[VMEM((2, rows + 2 * MARGIN + SUB, width), F32)],
        compiler_params=on_chip(40),
        name="cut",
    )(starts, owned, edges)

    grads, lights = run_chain(probe_wave, windows, fresnel_cols, fresnel_rows, measured[0])

    grid = pl.pallas_call(
        place_kernel,
        out_shape=jax.ShapeDtypeStruct((HOSTED, 2, nx, 3 * ny, each, width // 2), BF),
        in_specs=in_smem() + in_vmem(2),
        out_specs=pl.BlockSpec(memory_space=pltpu.VMEM),
        scratch_shapes=[VMEM((3, rows + 2 * MARGIN + SUB, width), F32)],
        compiler_params=on_chip(48),
        name="place",
    )(starts, grads, lights)

    def slots(depth):
        return VMEM((HOSTED, 2, depth, each, width // 2), BF)

    def ring(depth):
        cut = (depth + 1) // 2
        return [slots(cut), slots(depth - cut), slots(cut), slots(depth - cut), slots(depth), slots(depth)]

    updated = pl.pallas_call(
        reduce_kernel,
        out_shape=jax.ShapeDtypeStruct((2, own, width), F32),
        in_specs=[pl.BlockSpec(memory_space=pl.ANY)] * 2,
        out_specs=pl.BlockSpec(memory_space=pltpu.VMEM),
        scratch_shapes=[VMEM((HOSTED, 2, nx, 3 * ny, each, width // 2), BF)]
        + ring(3 * ny)
        + [VMEM((HOSTED, 2, ny, 3, each, width // 2), BF)]
        + ring(3)
        + [
            slots(3),
            VMEM((HOSTED, 2, 2, 3, share, width // 2), BF),
            VMEM((2, own, width), F32),
            VMEM((HOSTED, 2, own, width), F32),
            VMEM((2, own, width), F32),
            dma((HOSTED, 2, 2, 6)),
            dma((HOSTED, 2, 2, 6)),
            dma((HOSTED,)),
            dma((HOSTED, 2)),
            dma((HOSTED,)),
            dma,
            dma,
            dma((HOSTED,)),
        ],
        compiler_params=on_chip(56, collective_id=2, has_side_effects=True),
        name="reduce",
    )(grid, owned)
    return updated[None]


def solution(mesh):
    split = Mesh(
        mesh.devices.reshape(mesh.shape["cuts"], mesh.shape["tile"], 4, 4),
        ("cuts", "tile", "probe_0", "probe_1"),
    )
    return jax.shard_map(
        shards,
        mesh=split,
        in_specs=(
            P(),
            P(),
            P(),
            P("cuts", None, "tile", None),
            P("tile", PROBE, None),
            P("tile", PROBE, None, None),
        ),
        out_specs=P("cuts", None, TILE_PROBE, None),
        check_vma=False,
    )
```

time: 231 us -> 218 us (0.944)
  the two profiles are of different devices: /device:TPU:8 before, /device:TPU:65 now
where the time goes in v3:
time: 218 us
  Pallas kernels  212 us (97%)
  local copies, waits for them, and re-layouts  6.44 us (3%)
    pallas_call x1, Pallas kernels, run_chain(): pl.pallas_call(chain_kernel, out_shape=[jax.ShapeDtypeStruct((HOSTED, pos...  87.3 us
    pallas_call x1, Pallas kernels, shards(): pl.pallas_call(reduce_kernel, out_shape=jax.ShapeDtypeStruct((2, own, wid...  83.9 us
    pallas_call x1, Pallas kernels, shards(): pl.pallas_call(edge_kernel, out_shape=jax.ShapeDtypeStruct((count, 2, sha...  21.1 us
    pallas_call x1, Pallas kernels, shards(): pl.pallas_call(place_kernel, out_shape=jax.ShapeDtypeStruct((HOSTED, 2, n...  14.8 us
    unnamed x11, local copies, waits for them, and re-layouts  6.44 us
    pallas_call x1, Pallas kernels, shards(): pl.pallas_call(cut_kernel, out_shape=jax.ShapeDtypeStruct((positions, chu...  4.52 us

profile of v3, /device:TPU:65, one launch (start us, length us, event | category | flops | bytes accessed | tf_op | source)
XLA Modules:
  0.0 218.1 jit_solution(16155864299712608499)
XLA Ops:
  0.0 0.0 copy-start.4
  0.0 0.0 copy-start
  0.0 1.9 copy-done
  1.9 0.0 copy-start.1
  1.9 21.1 %edge.1.edges = bf16[16,2,16,768]{3,2,1,0:T(8,128)(2,1)S(1)} custom-call(f32[2,512,768]{2,1,0:T(8,128)S(1)} %bitcast.6), custom_call_target="tpu_custom_call" | custom-call | tf_op jit(solution)/shard_map/edge/pallas_call | solution.py:737
  23.0 0.0 copy-done.4
  23.0 0.0 copy-done.1
  23.0 4.5 %cut.1.windows = bf16[2,4,512,256]{3,2,1,0:T(8,128)(2,1)S(1)} custom-call(s32[2,2]{1,0:T(2,128)S(1)} %bitcast.8, f32[2,512,768]{2,1,0:T(8,128)S(1)} %bitcast.7, bf16[16,2,16,768]{3,2,1,0:T(8,128)(2,1)S(1)} %edge.1.edges), custom_call_target="tpu_custom_call" | custom-call | tf_op jit(solution)/shard_map/cut/pallas_call | solution.py:755
  27.5 0.0 copy-start.2
  27.6 1.3 copy-done.2
  28.9 87.3 %chain.1 = (bf16[2,2,4,512,256]{4,3,2,1,0:T(8,128)(2,1)}, bf16[2,2,4,512,128]{4,3,2,1,0:T(8,128)(2,1)}) custom-call(bf16[2,512,512]{2,1,0:T(8,128)(2,1)} %probe.1, bf16[2,4,512,256]{3,2,1,0:T(8,128)(2,1)} %copy-done.2, bf16[2,512,512]{2,1,0:T(8,128)(2,1)} %fresnel_cols.1, bf16[1024,512]{1,0:T(8,128)(2,1)} %bitcast.11, f32[2,512,512]{2,1,0:T(8,128)} %bitcast.10), custom_call_target="tpu_custom_call" | custom-call | tf_op jit(solution)/shard_map/chain/pallas_call | solution.py:690
  116.2 0.0 copy-start.3
  116.2 1.6 copy-done.3
  117.8 14.8 %place.1.grids = bf16[2,2,4,12,48,384]{5,4,3,2,1,0:T(8,128)(2,1)} custom-call(s32[2,2]{1,0:T(2,128)S(1)} %bitcast.9, bf16[2,2,4,512,256]{4,3,2,1,0:T(8,128)(2,1)} %get-tuple-element.7.grads, bf16[2,2,4,512,128]{4,3,2,1,0:T(8,128)(2,1)S(1)} %copy-done.3), custom_call_target="tpu_custom_call" | custom-call | tf_op jit(solution)/shard_map/place/pallas_call | solution.py:767
  132.6 83.9 %reduce.1 = f32[2,32,768]{2,1,0:T(8,128)} custom-call(bf16[2,2,4,12,48,384]{5,4,3,2,1,0:T(8,128)(2,1)} %place.1.grids, f32[2,512,768]{2,1,0:T(8,128)} %bitcast.5), custom_call_target="tpu_custom_call" | custom-call | tf_op jit(solution)/shard_map/reduce/pallas_call | solution.py:784
  216.5 1.6 copy.8
Async XLA Ops:
  0.0 23.0 %copy-start.4 = (s32[1,2,2]{2,1,0:T(2,128)S(1)}, s32[1,2,2]{2,1,0:T(2,128)}, u32[]{:S(2)}) copy-start(s32[1,2,2]{2,1,0:T(2,128)} %param.10) | copy-start | bytes 52
  0.0 1.9 copy-start
  1.9 21.1 %copy-start.1 = (f32[1,2,512,768]{3,2,1,0:T(8,128)S(1)}, f32[1,2,512,768]{3,2,1,0:T(8,128)}, u32[]{:S(2)}) copy-start(f32[1,2,512,768]{3,2,1,0:T(8,128)} %param.9) | copy-start | bytes 9437188
  27.5 1.3 copy-start.2
  116.2 1.6 copy-start.3

commit v4 on v1

v4 whole, which is shorter than its diff:
```python
import jax
import jax.numpy as jnp
from jax import lax
from jax.experimental import pallas as pl
from jax.experimental.pallas import tpu as pltpu
from jax.sharding import Mesh
from jax.sharding import PartitionSpec as P

MARGIN = 128
LANES = 128
HOSTED = 2
LIGHT, GRADE = 0, 1
PROBE = ("probe_0", "probe_1")
TILE_PROBE = ("tile", "probe_0", "probe_1")
MESH_ID = pl.DeviceIdType.MESH
BF = jnp.bfloat16
F32 = jnp.float32
VMEM = pltpu.VMEM


def active_slots(me, count):
    return (1 + me // (count - 4)) * (1 - me // (count - 2))


def step_kernel(
    starts, owned, probe, fresnel_cols, forward_rows, measured,
    out,
    rows_here, edge_rows, mine, swapped, gathered, slab, tall, wide, amplitude_here,
    cuts, forward_cols, adjoint_cols, adjoint_rows,
    waves, cots, wave_out, cot_out, total, middle, backs,
    pieces, grids, pre, staged, got_up, got_down, partial, pre2, staged2, got_up2, got_down2,
    final, extra, ratio, incoming,
    send_z, recv_z, send_e, recv_e,
    send_f, recv_f, send_b, recv_b, send_w, recv_w,
    send_r, recv_r, send_m, recv_m, send_d, recv_d, local_sem,
):
    tile = lax.axis_index("tile")
    where = {"probe_0": lax.axis_index("probe_0"), "probe_1": lax.axis_index("probe_1")}
    sizes = {"probe_0": lax.axis_size("probe_0"), "probe_1": lax.axis_size("probe_1")}
    nx, ny = sizes["probe_0"], sizes["probe_1"]
    members = nx * ny
    spot = where["probe_0"] * ny + where["probe_1"]
    me = lax.axis_index("cuts")
    count = lax.axis_size("cuts")
    last = count - 3
    right = lax.rem(me + 1, count)
    left = lax.rem(me + count - 1, count)
    _, positions, chunks, size, pair = cuts.shape
    half = pair // 2
    hosted = 1 + me // (last - 1)
    slots = active_slots(me, count)
    _, rows, width = owned.shape
    share = mine.shape[1]
    own = rows // members
    each = own + share
    lanes_side = width // 2

    def plane_peer(step):
        other = lax.rem(spot + step, members)
        return {"probe_0": other // ny, "probe_1": lax.rem(other, ny)}

    def across(index):
        return {"tile": 1 - tile, "probe_0": index // ny, "probe_1": lax.rem(index, ny)}

    lower = spot // (members // 2)
    edge_first = (1 - lower) * (rows - MARGIN + spot * share) + lower * (spot - members // 2) * share
    target = (1 - lower) * (members - members // 4 + spot // 2) + lower * ((spot - members // 2) // 2)
    at_end = where["probe_0"] // (nx - 1)
    at_start = (nx - 1 - where["probe_0"]) // (nx - 1)
    outer = at_end + at_start
    source = at_end * (2 * (spot - members + members // 4)) + at_start * (members // 2 + 2 * spot)

    barrier = pltpu.get_barrier_semaphore()

    def greet(device_id):
        pl.semaphore_signal(barrier, inc=1, device_id=device_id, device_id_type=MESH_ID)

    greet({"tile": 1 - tile})
    for step in range(1, members):
        greet(plane_peer(step))
    for other in (left, right):
        greet({"cuts": other})

    @pl.when(me == last)
    def _():
        greet({"cuts": count - 1})

    @pl.when(me == count - 1)
    def _():
        greet({"cuts": last})

    @pl.when(outer == 1)
    def _():
        for which in range(2):
            greet(across(source + which))

    fetch_edge = pltpu.make_async_copy(
        owned.at[:, pl.ds(pl.multiple_of(edge_first, share), share), :], edge_rows, local_sem.at[0]
    )
    fetch_edge.start()
    fetch_rows = pltpu.make_async_copy(
        owned.at[:, pl.ds(pl.multiple_of(spot * own, own), own), :], rows_here, local_sem.at[1]
    )
    fetch_rows.start()

    def fetch_slab(part):
        return pltpu.make_async_copy(owned.at[part], total.at[:, pl.ds(0, width)], local_sem.at[2])

    fetch_slab(0).start()

    def fetch_measured():
        return pltpu.make_async_copy(measured, amplitude_here, local_sem.at[3])

    @pl.when(me == last)
    def _():
        fetch_measured().start()

    fetch_edge.wait()
    mine[...] = edge_rows[...].astype(BF)
    pl.semaphore_wait(barrier, members + 3 + (me + 1) // count + (me // last) * (1 - me // (last + 1)))

    swap = pltpu.make_async_remote_copy(
        src_ref=mine, dst_ref=swapped, send_sem=send_z, recv_sem=recv_z, device_id={"tile": 1 - tile}, device_id_type=MESH_ID
    )
    swap.start()

    first_half, second_half = slice(0, half), slice(half, pair)

    @pl.when(me == 0)
    def _():
        for position in range(positions):
            for chunk in range(chunks):
                lanes = slice(chunk * half, (chunk + 1) * half)
                waves[0, position, chunk, :, first_half] = probe[0, :, lanes]
                waves[0, position, chunk, :, second_half] = probe[1, :, lanes]

    def turned(value):
        return value.astype(F32).T.astype(BF)

    def prepare_forward(chunk, carry):
        lanes = pl.ds(pl.multiple_of(chunk * half, half), half)
        for other in range(chunks):
            lines = slice(other * half, (other + 1) * half)
            real, imag = turned(fresnel_cols[0, lines, lanes]), turned(fresnel_cols[1, lines, lanes])
            left_lanes = slice(other * pair, other * pair + half)
            right_lanes = slice(other * pair + half, (other + 1) * pair)
            forward_cols[chunk, first_half, left_lanes] = real
            forward_cols[chunk, first_half, right_lanes] = imag
            forward_cols[chunk, second_half, left_lanes] = -imag
            forward_cols[chunk, second_half, right_lanes] = real
        return carry

    def prepare_adjoint(chunk, carry):
        lines = pl.ds(pl.multiple_of(chunk * half, half), half)
        for other in range(chunks):
            lanes = slice(other * half, (other + 1) * half)
            real, imag = fresnel_cols[0, lines, lanes], fresnel_cols[1, lines, lanes]
            left_lanes = slice(other * pair, other * pair + half)
            right_lanes = slice(other * pair + half, (other + 1) * pair)
            adjoint_cols[chunk, first_half, left_lanes] = real
            adjoint_cols[chunk, first_half, right_lanes] = -imag
            adjoint_cols[chunk, second_half, left_lanes] = imag
            adjoint_cols[chunk, second_half, right_lanes] = real
            for part in range(2):
                block = forward_rows[pl.ds(pl.multiple_of(part * size + chunk * half, half), half), lanes]
                adjoint_rows[part * size + other * half : part * size + (other + 1) * half, lines] = turned(block)
        return carry


    for part in range(2):
        fetch_slab(part).wait()
        slab[part, MARGIN : MARGIN + rows, :] = total[:, :width].astype(BF)
        if part == 0:
            fetch_slab(1).start()

    def edge_copy(step, slot):
        return pltpu.make_async_remote_copy(
            src_ref=swapped,
            dst_ref=gathered.at[slot],
            send_sem=send_e.at[step],
            recv_sem=recv_e.at[slot],
            device_id=plane_peer(step),
            device_id_type=MESH_ID,
        )

    swap.wait_recv()
    for step in range(1, members):
        edge_copy(step, spot).start()
    gathered[spot] = swapped[...]

    lax.fori_loop(0, chunks, prepare_forward, 0)
    lax.fori_loop(0, chunks, prepare_adjoint, 0)

    def select(index, carry):
        position, which = index // 2, lax.rem(index, 2)
        start = starts[position, which]
        far = lax.broadcasted_iota(jnp.int32, (width, size), 0) - lax.broadcasted_iota(jnp.int32, (width, size), 1)
        tall[position, which] = jnp.where(far == start, 1.0, 0.0).astype(BF)
        far = lax.broadcasted_iota(jnp.int32, (size, width), 1) - lax.broadcasted_iota(jnp.int32, (size, width), 0)
        wide[position, which] = jnp.where(far == start, 1.0, 0.0).astype(BF)
        return carry

    lax.fori_loop(0, 2 * positions, select, 0)

    for step in range(1, members):
        edge_copy(step, lax.rem(spot + members - step, members)).wait_recv()
    for index in range(members):
        first = index * share + (rows if index >= members // 2 else 0)
        slab[:, first : first + share, :] = gathered[index]

    def cut_window(position):
        def columns(index, carry):
            part, where_to = index // 2, lax.rem(index, 2)
            lanes = pl.ds(pl.multiple_of(where_to * pair, pair), pair)
            values = jnp.dot(slab[part], tall[position, 1, :, lanes], preferred_element_type=F32).astype(BF)
            values = jnp.dot(wide[position, 0], values, preferred_element_type=F32).astype(BF)
            here = pl.ds(pl.multiple_of(part * half, half), half)
            wave_out[position, 2 * where_to, :, here] = values[:, :half]
            wave_out[position, 2 * where_to + 1, :, here] = values[:, half:]
            return carry

        lax.fori_loop(0, 4, columns, 0)

    def window_copy(position, slot, to):
        return pltpu.make_async_remote_copy(
            src_ref=wave_out.at[position],
            dst_ref=cuts.at[slot, position],
            send_sem=send_w.at[position],
            recv_sem=recv_w.at[slot, position],
            device_id={"cuts": to},
            device_id_type=MESH_ID,
        )

    give_slot = 1 - lax.rem(me + 1, 2) * (me // (last + 1))
    give_to = last - 1 + me // (last + 1)

    @pl.when(me >= last)
    def _():
        for position in range(positions):
            cut_window(position)
            window_copy(position, give_slot, give_to).start()

    @pl.when(me == last)
    def _():
        fetch_measured().wait()

    def forward_copy(position, chunk):
        return pltpu.make_async_remote_copy(
            src_ref=wave_out.at[position, chunk],
            dst_ref=waves.at[0, position, chunk],
            send_sem=send_f.at[position, chunk],
            recv_sem=recv_f.at[position, chunk],
            device_id={"cuts": right},
            device_id_type=MESH_ID,
        )

    def adjoint_copy(position, chunk):
        return pltpu.make_async_remote_copy(
            src_ref=cot_out.at[position, chunk],
            dst_ref=cots.at[position, chunk],
            send_sem=send_b.at[position, chunk],
            recv_sem=recv_b.at[position, chunk],
            device_id={"cuts": left},
            device_id_type=MESH_ID,
        )

    def parts_of(value):
        value = value.astype(F32)
        return value[:, :half], value[:, half:]

    def both(real, imag):
        return jnp.concatenate([real, imag], axis=1)

    def add_product(chunk, value, matrix):
        product = jnp.dot(value, matrix, preferred_element_type=F32)
        if chunk == 0:
            total[...] = product
        elif chunk < chunks - 1:
            total[...] += product
        else:
            product = (total[...] + product).astype(BF)
            for other in range(chunks):
                middle[other] = product[:, other * pair : (other + 1) * pair]

    def forward(position):
        @pl.when(me < last)
        def _():
            cut_window(position)
            cuts[0, position] = wave_out[position]

        def hosted_slice(slot, carry):
            @pl.when((me >= last) | (slot > 0))
            def _():
                window_copy(position, slot, give_to).wait_recv()

            for chunk in range(chunks):
                @pl.when((me > 0) & (slot == 0))
                def _():
                    forward_copy(position, chunk).wait_recv()

                wave_r, wave_i = parts_of(waves[slot, position, chunk])
                win_r, win_i = parts_of(cuts[slot, position, chunk])
                out = both(wave_r * win_r - wave_i * win_i, wave_r * win_i + wave_i * win_r).astype(BF)
                add_product(chunk, out, forward_cols[chunk])

            def produce(chunk, inner):
                result = jnp.dot(forward_rows[...], middle[chunk], preferred_element_type=F32)
                real = result[:size, :half] - result[size:, half:]
                imag = result[size:, :half] + result[:size, half:]
                value = both(real, imag).astype(BF)

                @pl.when(slot < hosted - 1)
                def _():
                    waves[1, position, chunk] = value

                @pl.when(slot == hosted - 1)
                def _():
                    @pl.when(me < last)
                    def _():
                        wave_out[position, chunk] = value
                        forward_copy(position, chunk).start()

                    @pl.when(me == last)
                    def _():
                        psi_r, psi_i = parts_of(value)
                        amplitude = amplitude_here[position, :, pl.ds(pl.multiple_of(chunk * half, half), half)]
                        factor = 1.0 - amplitude * lax.rsqrt(psi_r * psi_r + psi_i * psi_i + 1.0)
                        cots[position, chunk] = both(psi_r * factor, psi_i * factor).astype(BF)

                return inner

            lax.fori_loop(0, chunks, produce, 0)

            def brighten(chunk, inner):
                wave_r, wave_i = parts_of(waves[slot, position, chunk])
                lanes = pl.ds(pl.multiple_of(chunk * half, half), half)
                pieces[slot, position, 2, :, lanes] = (wave_r * wave_r + wave_i * wave_i).astype(BF)
                return inner

            lax.fori_loop(0, chunks, brighten, 0)
            return carry

        lax.fori_loop(0, hosted, hosted_slice, 0)

    def adjoint(position):
        def hosted_slice(step, carry):
            slot = hosted - 1 - step
            for chunk in range(chunks):
                @pl.when((me < last) & (step == 0))
                def _():
                    adjoint_copy(position, chunk).wait_recv()

                add_product(chunk, cots[position, chunk], adjoint_cols[chunk])

            def produce(chunk, inner):
                result = jnp.dot(adjoint_rows[...], middle[chunk], preferred_element_type=F32)
                real = result[:size, :half] + result[size:, half:]
                imag = result[:size, half:] - result[size:, :half]
                back = both(real, imag).astype(BF)
                backs[chunk] = back

                @pl.when(me > 0)
                def _():
                    back_r, back_i = parts_of(back)
                    win_r, win_i = parts_of(cuts[slot, position, chunk])
                    value = both(win_r * back_r + win_i * back_i, win_r * back_i - win_i * back_r).astype(BF)

                    @pl.when(slot > 0)
                    def _():
                        cots[position, chunk] = value

                    @pl.when(slot == 0)
                    def _():
                        cot_out[position, chunk] = value
                        adjoint_copy(position, chunk).start()

                return inner

            lax.fori_loop(0, chunks, produce, 0)

            def grade(chunk, inner):
                wave_r, wave_i = parts_of(waves[slot, position, chunk])
                back_r, back_i = parts_of(backs[chunk])
                lanes = pl.ds(pl.multiple_of(chunk * half, half), half)
                pieces[slot, position, 0, :, lanes] = (wave_r * back_r + wave_i * back_i).astype(BF)
                pieces[slot, position, 1, :, lanes] = (wave_r * back_i - wave_i * back_r).astype(BF)
                return inner

            lax.fori_loop(0, chunks, grade, 0)
            return carry

        lax.fori_loop(0, hosted, hosted_slice, 0)


    def place(slot, part, position):
        for side in range(2):
            lanes = slice(side * lanes_side, (side + 1) * lanes_side)
            values = jnp.dot(pieces[slot, position, part], wide[position, 1, :, lanes], preferred_element_type=F32)
            values = jnp.dot(tall[position, 0], values.astype(BF), preferred_element_type=F32)

            def put(add):
                for x in range(nx):
                    for y in range(ny):
                        index = x * ny + y
                        major, minor = (x, y) if side == 0 else (y, x)
                        first = MARGIN + index * own
                        second = index * share + (rows if 2 * index >= members else 0)
                        for at, depth, begins in ((0, own, first), (own, share, second)):
                            there = (slot, side, major, part * ny + minor, pl.ds(at, depth))
                            piece = values[begins : begins + depth]
                            if add:
                                piece = piece + grids[there].astype(F32)
                            grids[there] = piece.astype(BF)

            @pl.when(position == 0)
            def _():
                put(False)

            @pl.when(position > 0)
            def _():
                put(True)

    order = (("probe_0", "probe_1"), ("probe_1", "probe_0"))
    parts_in = {LIGHT: (2,), GRADE: (0, 1)}

    def regions(kind, stage):
        parts = parts_in[kind]
        depth = len(parts) * (ny if stage == 0 else 1)
        first = parts[0] * (ny if stage == 0 else 1)
        if depth == 1:
            cut = each // 3 * 2
            return (pl.ds(first, 1), pl.ds(0, cut)), (pl.ds(first, 1), pl.ds(cut, each - cut))
        cut = depth // 2
        return (pl.ds(first, cut), pl.ds(0, each)), (pl.ds(first + cut, depth - cut), pl.ds(0, each))

    def buffers(slot, stage, side):
        if stage == 0:
            return grids.at[slot, side], tuple(ref.at[slot, side] for ref in (pre, staged, got_up, got_down))
        return partial.at[slot, side], tuple(ref.at[slot, side] for ref in (pre2, staged2, got_up2, got_down2))

    def ring(kind, slot, stage, side):
        axis = order[side][stage]
        length = sizes[axis]
        here = where[axis]
        plus, minus = lax.rem(here + 1, length), lax.rem(here + length - 1, length)
        opposite = lax.rem(here + 2, length)
        src, (before, queued, up, down) = buffers(slot, stage, side)
        low, high = regions(kind, stage)

        def copy(index, source_ref, target_ref, to):
            return pltpu.make_async_remote_copy(
                src_ref=source_ref,
                dst_ref=target_ref,
                send_sem=send_r.at[slot, kind, stage, side, index],
                recv_sem=recv_r.at[slot, kind, stage, side, index],
                device_id={axis: to},
                device_id_type=MESH_ID,
            )

        def make(index):
            if index == 0:
                return copy(0, src.at[(opposite, *low)], before.at[low], plus)
            if index == 1:
                return copy(1, src.at[(opposite, *high)], before.at[high], minus)
            if index == 2:
                return copy(2, src.at[(plus, *high)], up.at[high], plus)
            if index == 3:
                return copy(3, src.at[(minus, *low)], down.at[low], minus)
            if index == 4:
                return copy(4, queued.at[low], up.at[low], plus)
            return copy(5, queued.at[high], down.at[high], minus)

        return make, here, plus, minus, low, high

    def begin(kind, slot, stage, side):
        make = ring(kind, slot, stage, side)[0]
        for index in range(4):
            make(index).start()

    def relay(kind, slot, stage, side):
        make, _, plus, minus, low, high = ring(kind, slot, stage, side)
        src, (before, queued, _, _) = buffers(slot, stage, side)
        make(0).wait_recv()
        queued[low] = (before[low].astype(F32) + src[(plus, *low)].astype(F32)).astype(BF)
        make(4).start()
        make(1).wait_recv()
        queued[high] = (before[high].astype(F32) + src[(minus, *high)].astype(F32)).astype(BF)
        make(5).start()

    def settle(kind, slot, stage, side):
        make, here, _, _, _, _ = ring(kind, slot, stage, side)
        src, (_, _, up, down) = buffers(slot, stage, side)
        for index in range(2, 6):
            make(index).wait_recv()
        for part in parts_in[kind]:
            if stage == 0:
                for minor in range(ny):
                    index = part * ny + minor
                    summed = src[here, index].astype(F32) + up[index].astype(F32) + down[index].astype(F32)
                    partial[slot, side, minor, part] = summed.astype(BF)
            else:
                summed = src[here, part].astype(F32) + up[part].astype(F32) + down[part].astype(F32)
                final[slot, side, part] = summed.astype(BF)

    def drain(kind, slot, stage, side):
        make = ring(kind, slot, stage, side)[0]
        for index in range(6):
            make(index).wait_send()

    def both_sides(function, kind, stage):
        def one(slot, carry):
            for side in range(2):
                function(kind, slot, stage, side)
            return carry

        lax.fori_loop(0, slots, one, 0)

    def scatter(kinds):
        for stage in range(2):
            for function in (begin, relay, settle):
                for kind in kinds:
                    both_sides(function, kind, stage)

    early = me < last - 1
    late = me // last

    @pl.when(me <= last)
    def _():
        def phase(step, carry):
            is_back = late * (step % positions) + (1 - late) * (step // positions)
            position = late * (step // positions) + (1 - late) * (step % positions)

            @pl.when(is_back == 0)
            def _():
                forward(position)

            @pl.when(is_back == 1)
            def _():
                adjoint(position)

            @pl.when(early)
            def _():
                def one_part(index, inner):
                    place(0, 2 * (1 - is_back) + index, position)
                    return inner

                lax.fori_loop(0, 1 + is_back, one_part, 0)

            @pl.when(early & (step == positions - 1))
            def _():
                scatter((LIGHT,))

            return carry

        lax.fori_loop(0, 2 * positions, phase, 0)

        @pl.when(early)
        def _():
            scatter((GRADE,))

        @pl.when(me >= last - 1)
        def _():
            def place_one(index, carry):
                rest = lax.rem(index, 3 * positions)
                place(index // (3 * positions), lax.rem(rest, 3), rest // 3)
                return carry

            lax.fori_loop(0, slots * 3 * positions, place_one, 0)
            scatter((LIGHT, GRADE))

    def margin_copy(slot, piece):
        return pltpu.make_async_remote_copy(
            src_ref=final.at[slot, :, :, pl.ds(own, share), :],
            dst_ref=extra.at[slot, piece],
            send_sem=send_m.at[slot],
            recv_sem=recv_m.at[slot, piece],
            device_id=across(target),
            device_id_type=MESH_ID,
        )

    def deliver(slot):
        return pltpu.make_async_remote_copy(
            src_ref=ratio.at[slot],
            dst_ref=incoming,
            send_sem=send_d.at[slot],
            recv_sem=recv_d,
            device_id={"cuts": lax.rem(me + 1 + slot * (me - last + 1), count)},
            device_id_type=MESH_ID,
        )

    def start_margin(slot, carry):
        margin_copy(slot, lax.rem(spot, 2)).start()
        return carry

    lax.fori_loop(0, slots, start_margin, 0)

    def divide(slot, carry):
        @pl.when(outer == 0)
        def _():
            extra[slot] = jnp.zeros(extra.shape[1:], extra.dtype)

        @pl.when(outer == 1)
        def _():
            for piece in range(2):
                margin_copy(slot, piece).wait_recv()

        for side in range(2):
            columns = slice(side * lanes_side, (side + 1) * lanes_side)
            for piece in range(2):
                lines = slice(piece * share, (piece + 1) * share)
                full = final[slot, side, :, lines, :].astype(F32) + extra[slot, piece, side].astype(F32)
                scale = 1.0 / (full[2] + 1.0)
                for part in range(2):
                    ratio[slot, part, lines, columns] = full[part] * scale

        @pl.when((me == last) | (slot > 0))
        def _():
            deliver(slot).start()

        return carry

    lax.fori_loop(0, slots, divide, 0)
    fetch_rows.wait()

    @pl.when(me < last)
    def _():
        out[...] = rows_here[...] - ratio[0]

    @pl.when(me >= last)
    def _():
        deliver(0).wait_recv()
        out[...] = rows_here[...] - incoming[...]

    swap.wait_send()
    for step in range(1, members):
        edge_copy(step, spot).wait_send()

    def finish(index, carry):
        position = index // chunks
        chunk = index % chunks

        @pl.when(me < last)
        def _():
            forward_copy(position, chunk).wait_send()

        @pl.when((me > 0) & (me <= last))
        def _():
            adjoint_copy(position, chunk).wait_send()

        return carry

    lax.fori_loop(0, positions * chunks, finish, 0)

    @pl.when(me >= last)
    def _():
        for position in range(positions):
            window_copy(position, give_slot, give_to).wait_send()

    for kind in (LIGHT, GRADE):
        for stage in range(2):
            both_sides(drain, kind, stage)

    def finish_slot(slot, carry):
        margin_copy(slot, lax.rem(spot, 2)).wait_send()

        @pl.when((me == last) | (slot > 0))
        def _():
            deliver(slot).wait_send()

        return carry

    lax.fori_loop(0, slots, finish_slot, 0)


def shards(probe_wave, fresnel_rows, fresnel_cols, object_slices, offsets, measured):
    owned = object_slices[0]
    starts = offsets[0]
    size = probe_wave.shape[1]
    positions = starts.shape[0]
    rows, width = owned.shape[1:]
    chunks = size // LANES
    pair = 2 * LANES
    nx, ny = lax.axis_size("probe_0"), lax.axis_size("probe_1")
    count = nx * ny
    share = 2 * MARGIN // count
    own = rows // count
    each = own + share
    lanes = width // 2
    dma = pltpu.SemaphoreType.DMA
    stack = (positions, chunks, size, pair)
    block = (HOSTED, 2, 3 * ny, each, lanes)
    small = (HOSTED, 2, 3, each, lanes)
    flags = (positions, chunks)
    anywhere = pl.BlockSpec(memory_space=pl.ANY)
    vmem = pl.BlockSpec(memory_space=pltpu.VMEM)

    updated = pl.pallas_call(
        step_kernel,
        out_shape=jax.ShapeDtypeStruct((2, own, width), F32),
        in_specs=[pl.BlockSpec(memory_space=pltpu.SMEM), anywhere, vmem, vmem, vmem, anywhere],
        out_specs=vmem,
        scratch_shapes=[
            VMEM((2, own, width), F32),
            VMEM((2, share, width), F32),
            VMEM((2, share, width), BF),
            VMEM((2, share, width), BF),
            VMEM((count, 2, share, width), BF),
            VMEM((2, rows + 2 * MARGIN, width), BF),
            VMEM((positions, 2, width, size), BF),
            VMEM((positions, 2, size, width), BF),
            VMEM((positions, size, size), F32),
            VMEM((HOSTED, *stack), BF),
            VMEM((chunks, pair, 2 * size), BF),
            VMEM((chunks, pair, 2 * size), BF),
            VMEM((2 * size, size), BF),
            VMEM((HOSTED, *stack), BF),
            VMEM(stack, BF),
            VMEM(stack, BF),
            VMEM(stack, BF),
            VMEM((size, 2 * size), F32),
            VMEM((chunks, size, pair), BF),
            VMEM((chunks, size, pair), BF),
            VMEM((HOSTED, positions, 3, size, size), BF),
            VMEM((HOSTED, 2, nx, 3 * ny, each, lanes), BF),
            VMEM(block, BF),
            VMEM(block, BF),
            VMEM(block, BF),
            VMEM(block, BF),
            VMEM((HOSTED, 2, ny, 3, each, lanes), BF),
            VMEM(small, BF),
            VMEM(small, BF),
            VMEM(small, BF),
            VMEM(small, BF),
            VMEM(small, BF),
            VMEM((HOSTED, 2, 2, 3, share, lanes), BF),
            VMEM((HOSTED, 2, own, width), F32),
            VMEM((2, own, width), F32),
            dma,
            dma,
            dma((count,)),
            dma((count,)),
            dma(flags),
            dma(flags),
            dma(flags),
            dma(flags),
            dma((positions,)),
            dma((HOSTED, positions)),
            dma((HOSTED, 2, 2, 2, 6)),
            dma((HOSTED, 2, 2, 2, 6)),
            dma((HOSTED,)),
            dma((HOSTED, 2)),
            dma((HOSTED,)),
            dma,
            dma((4,)),
        ],
        compiler_params=pltpu.CompilerParams(collective_id=0, has_side_effects=True, vmem_limit_bytes=67043328),
        name="step",
    )(starts, owned, probe_wave, fresnel_cols, fresnel_rows.reshape(2 * size, size), measured[0])
    return updated[None]


def solution(mesh):
    split = Mesh(
        mesh.devices.reshape(mesh.shape["cuts"], mesh.shape["tile"], 4, 4),
        ("cuts", "tile", "probe_0", "probe_1"),
    )
    return jax.shard_map(
        shards,
        mesh=split,
        in_specs=(
            P(),
            P(),
            P(),
            P("cuts", None, "tile", None),
            P("tile", PROBE, None),
            P("tile", PROBE, None, None),
        ),
        out_specs=P("cuts", None, TILE_PROBE, None),
        check_vma=False,
    )
```

time: 377 us -> 194 us (0.51)
  waiting for transfers between devices: 77.6 us -> 0 us
  local copies, waits for them, and re-layouts: 50.5 us -> 1.62 us
  blocking collectives: 24.2 us -> 0 us
  other arithmetic: 22.5 us -> 0 us
  Pallas kernels: 167 us -> 189 us
  starting transfers between devices: 20.6 us -> 0 us
  between operations: 13.5 us -> 0.01 us
    reduce_scatter x2 -> x0, waiting for transfers between devices: 64.7 us -> none  [shards(): summed = lax.psum_scatter(summed, axis, scatter_dimension=0, tiled=True)]
    another operation x11 -> x0, local copies, waits for them, and re-layouts: 30.5 us -> none  [the longest x4 11.6 us: shards(): jnp.stack([col_r.T, col_i.T])]
    all_gather x1 -> x0, blocking collectives: 24.2 us -> none  [shards(): theirs = lax.all_gather(swapped, PROBE, axis=1, tiled=True)]
    pallas_call x3 -> x1, Pallas kernels: 167 us -> 189 us  [shards(): pl.pallas_call(step_kernel, out_shape=jax.ShapeDtypeStruct((2, own, width...]
    ppermute x3 -> x0, starting transfers between devices: 20.6 us -> none  [the longest x2 13.3 us: shards(): received.append(lax.ppermute(margin, TILE_PROBE, pairs))]
    reshape x5 -> x0, local copies, waits for them, and re-layouts: 13.8 us -> none  [the longest x2 8.9 us: column_blocks(): cut.transpose(2, 0, 3, 4, 1, 5)]
    ppermute x3 -> x0, waiting for transfers between devices: 12.9 us -> none  [the longest x2 12.9 us: shards(): received.append(lax.ppermute(margin, TILE_PROBE, pairs))]
    transpose x2 -> x0, other arithmetic: 10 us -> none  [column_blocks(): cut.transpose(2, 0, 3, 4, 1, 5)]
  transfers between devices with their start and end apart: 5 -> 0, of which waited for: 4 -> 0; matrix products, arithmetic and copies ran while one was open for 17% -> 0% of each run, Pallas kernels for 0% -> 0%
where the time goes in v4:
time: 194 us; the launch traced here: 191 us
  Pallas kernels  189 us (97%)
    pallas_call x1, Pallas kernels, shards(): pl.pallas_call(step_kernel, out_shape=jax.ShapeDtypeStruct((2, own, width...  189 us

profile of v4, /device:TPU:8, one launch (start us, length us, event | category | flops | bytes accessed | tf_op | source)
XLA Modules:
  0.0 190.9 jit_solution(15860848894372235528)
XLA Ops:
  0.0 189.3 %step.1 = f32[2,32,768]{2,1,0:T(8,128)} custom-call(s32[2,2]{1,0:T(2,128)} %bitcast.9, f32[2,512,768]{2,1,0:T(8,128)} %bitcast.5, bf16[2,512,512]{2,1,0:T(8,128)(2,1)} %probe.1, bf16[2,512,512]{2,1,0:T(8,128)(2,1)} %fresnel_cols.1, bf16[1024,512]{1,0:T(8,128)(2,1)} %bitcast.7, f32[2,512,512]{2,1,0:T(8,128)} %bitcast.6), custom_call_target="tpu_custom_call" | custom-call | tf_op jit(solution)/shard_map/step/pallas_call | solution.py:697
  189.3 1.6 copy.8

commit v5 on v4

--- a/solution.py
+++ b/solution.py
@@ -18,10 +18,6 @@
 VMEM = pltpu.VMEM
 
 
-def active_slots(me, count):
-    return (1 + me // (count - 4)) * (1 - me // (count - 2))
-
-
 def step_kernel(
     starts, owned, probe, fresnel_cols, forward_rows, measured,
     out,
@@ -29,10 +25,10 @@
     cuts, forward_cols, adjoint_cols, adjoint_rows,
     waves, cots, wave_out, cot_out, total, middle, backs,
     pieces, grids, pre, staged, got_up, got_down, partial, pre2, staged2, got_up2, got_down2,
-    final, extra, ratio, incoming,
+    final, extra,
     send_z, recv_z, send_e, recv_e,
     send_f, recv_f, send_b, recv_b, send_w, recv_w,
-    send_r, recv_r, send_m, recv_m, send_d, recv_d, local_sem,
+    send_r, recv_r, send_m, recv_m, send_p, recv_p, local_sem,
 ):
     tile = lax.axis_index("tile")
     where = {"probe_0": lax.axis_index("probe_0"), "probe_1": lax.axis_index("probe_1")}
@@ -48,7 +44,7 @@
     _, positions, chunks, size, pair = cuts.shape
     half = pair // 2
     hosted = 1 + me // (last - 1)
-    slots = active_slots(me, count)
+    owner_slot = HOSTED * (me // last)
     _, rows, width = owned.shape
     share = mine.shape[1]
     own = rows // members
@@ -122,7 +118,9 @@
     swap = pltpu.make_async_remote_copy(
         src_ref=mine, dst_ref=swapped, send_sem=send_z, recv_sem=recv_z, device_id={"tile": 1 - tile}, device_id_type=MESH_ID
     )
-    swap.start()
+    @pl.when(me == 0)
+    def _():
+        swap.start()
 
     first_half, second_half = slice(0, half), slice(half, pair)
 
@@ -183,14 +181,6 @@
             device_id_type=MESH_ID,
         )
 
-    swap.wait_recv()
-    for step in range(1, members):
-        edge_copy(step, spot).start()
-    gathered[spot] = swapped[...]
-
-    lax.fori_loop(0, chunks, prepare_forward, 0)
-    lax.fori_loop(0, chunks, prepare_adjoint, 0)
-
     def select(index, carry):
         position, which = index // 2, lax.rem(index, 2)
         start = starts[position, which]
@@ -200,8 +190,28 @@
         wide[position, which] = jnp.where(far == start, 1.0, 0.0).astype(BF)
         return carry
 
+    def share_edges():
+        swap.wait_recv()
+        for step in range(1, members):
+            edge_copy(step, spot).start()
+
+    @pl.when(me > 0)
+    def _():
+        swap.start()
+
+    @pl.when(me == 0)
+    def _():
+        share_edges()
+
     lax.fori_loop(0, 2 * positions, select, 0)
-
+    lax.fori_loop(0, chunks, prepare_forward, 0)
+
+    @pl.when(me > 0)
+    def _():
+        share_edges()
+        lax.fori_loop(0, chunks, prepare_adjoint, 0)
+
+    gathered[spot] = swapped[...]
     for step in range(1, members):
         edge_copy(step, lax.rem(spot + members - step, members)).wait_recv()
     for index in range(members):
@@ -282,6 +292,22 @@
             for other in range(chunks):
                 middle[other] = product[:, other * pair : (other + 1) * pair]
 
+    def owner_copy(kind, slot, position):
+        parts = pl.ds(2, 1) if kind == LIGHT else pl.ds(0, 2)
+        return pltpu.make_async_remote_copy(
+            src_ref=pieces.at[slot, position, parts],
+            dst_ref=pieces.at[HOSTED, position, parts],
+            send_sem=send_p.at[slot, position, kind],
+            recv_sem=recv_p.at[position, kind],
+            device_id={"cuts": lax.rem(me + 1 + slot * (me - last + 1), count)},
+            device_id_type=MESH_ID,
+        )
+
+    def send_to_owner(kind, slot, position):
+        @pl.when((me == last) | (slot > 0))
+        def _():
+            owner_copy(kind, slot, position).start()
+
     def forward(position):
         @pl.when(me < last)
         def _():
@@ -338,6 +364,7 @@
                 return inner
 
             lax.fori_loop(0, chunks, brighten, 0)
+            send_to_owner(LIGHT, slot, position)
             return carry
 
         lax.fori_loop(0, hosted, hosted_slice, 0)
@@ -387,15 +414,16 @@
                 return inner
 
             lax.fori_loop(0, chunks, grade, 0)
+            send_to_owner(GRADE, slot, position)
             return carry
 
         lax.fori_loop(0, hosted, hosted_slice, 0)
 
 
-    def place(slot, part, position):
+    def place(part, position):
         for side in range(2):
             lanes = slice(side * lanes_side, (side + 1) * lanes_side)
-            values = jnp.dot(pieces[slot, position, part], wide[position, 1, :, lanes], preferred_element_type=F32)
+            values = jnp.dot(pieces[owner_slot, position, part], wide[position, 1, :, lanes], preferred_element_type=F32)
             values = jnp.dot(tall[position, 0], values.astype(BF), preferred_element_type=F32)
 
             def put(add):
@@ -406,7 +434,7 @@
                         first = MARGIN + index * own
                         second = index * share + (rows if 2 * index >= members else 0)
                         for at, depth, begins in ((0, own, first), (own, share, second)):
-                            there = (slot, side, major, part * ny + minor, pl.ds(at, depth))
+                            there = (side, major, part * ny + minor, pl.ds(at, depth))
                             piece = values[begins : begins + depth]
                             if add:
                                 piece = piece + grids[there].astype(F32)
@@ -433,26 +461,26 @@
         cut = depth // 2
         return (pl.ds(first, cut), pl.ds(0, each)), (pl.ds(first + cut, depth - cut), pl.ds(0, each))
 
-    def buffers(slot, stage, side):
+    def buffers(stage, side):
         if stage == 0:
-            return grids.at[slot, side], tuple(ref.at[slot, side] for ref in (pre, staged, got_up, got_down))
-        return partial.at[slot, side], tuple(ref.at[slot, side] for ref in (pre2, staged2, got_up2, got_down2))
-
-    def ring(kind, slot, stage, side):
+            return grids.at[side], tuple(ref.at[side] for ref in (pre, staged, got_up, got_down))
+        return partial.at[side], tuple(ref.at[side] for ref in (pre2, staged2, got_up2, got_down2))
+
+    def ring(kind, stage, side):
         axis = order[side][stage]
         length = sizes[axis]
         here = where[axis]
         plus, minus = lax.rem(here + 1, length), lax.rem(here + length - 1, length)
         opposite = lax.rem(here + 2, length)
-        src, (before, queued, up, down) = buffers(slot, stage, side)
+        src, (before, queued, up, down) = buffers(stage, side)
         low, high = regions(kind, stage)
 
         def copy(index, source_ref, target_ref, to):
             return pltpu.make_async_remote_copy(
                 src_ref=source_ref,
                 dst_ref=target_ref,
-                send_sem=send_r.at[slot, kind, stage, side, index],
-                recv_sem=recv_r.at[slot, kind, stage, side, index],
+                send_sem=send_r.at[kind, stage, side, index],
+                recv_sem=recv_r.at[kind, stage, side, index],
                 device_id={axis: to},
                 device_id_type=MESH_ID,
             )
@@ -472,14 +500,14 @@
 
         return make, here, plus, minus, low, high
 
-    def begin(kind, slot, stage, side):
-        make = ring(kind, slot, stage, side)[0]
+    def begin(kind, stage, side):
+        make = ring(kind, stage, side)[0]
         for index in range(4):
             make(index).start()
 
-    def relay(kind, slot, stage, side):
-        make, _, plus, minus, low, high = ring(kind, slot, stage, side)
-        src, (before, queued, _, _) = buffers(slot, stage, side)
+    def relay(kind, stage, side):
+        make, _, plus, minus, low, high = ring(kind, stage, side)
+        src, (before, queued, _, _) = buffers(stage, side)
         make(0).wait_recv()
         queued[low] = (before[low].astype(F32) + src[(plus, *low)].astype(F32)).astype(BF)
         make(4).start()
@@ -487,9 +515,9 @@
         queued[high] = (before[high].astype(F32) + src[(minus, *high)].astype(F32)).astype(BF)
         make(5).start()
 
-    def settle(kind, slot, stage, side):
-        make, here, _, _, _, _ = ring(kind, slot, stage, side)
-        src, (_, _, up, down) = buffers(slot, stage, side)
+    def settle(kind, stage, side):
+        make, here, _, _, _, _ = ring(kind, stage, side)
+        src, (_, _, up, down) = buffers(stage, side)
         for index in range(2, 6):
             make(index).wait_recv()
         for part in parts_in[kind]:
@@ -497,29 +525,24 @@
                 for minor in range(ny):
                     index = part * ny + minor
                     summed = src[here, index].astype(F32) + up[index].astype(F32) + down[index].astype(F32)
-                    partial[slot, side, minor, part] = summed.astype(BF)
+                    partial[side, minor, part] = summed.astype(BF)
             else:
                 summed = src[here, part].astype(F32) + up[part].astype(F32) + down[part].astype(F32)
-                final[slot, side, part] = summed.astype(BF)
-
-    def drain(kind, slot, stage, side):
-        make = ring(kind, slot, stage, side)[0]
+                final[side, part] = summed.astype(BF)
+
+    def drain(kind, stage, side):
+        make = ring(kind, stage, side)[0]
         for index in range(6):
             make(index).wait_send()
 
     def both_sides(function, kind, stage):
-        def one(slot, carry):
-            for side in range(2):
-                function(kind, slot, stage, side)
-            return carry
-
-        lax.fori_loop(0, slots, one, 0)
-
-    def scatter(kinds):
+        for side in range(2):
+            function(kind, stage, side)
+
+    def scatter(kind):
         for stage in range(2):
             for function in (begin, relay, settle):
-                for kind in kinds:
-                    both_sides(function, kind, stage)
+                both_sides(function, kind, stage)
 
     early = me < last - 1
     late = me // last
@@ -530,6 +553,10 @@
             is_back = late * (step % positions) + (1 - late) * (step // positions)
             position = late * (step // positions) + (1 - late) * (step % positions)
 
+            @pl.when((me == 0) & (step == positions))
+            def _():
+                lax.fori_loop(0, chunks, prepare_adjoint, 0)
+
             @pl.when(is_back == 0)
             def _():
                 forward(position)
@@ -541,95 +568,81 @@
             @pl.when(early)
             def _():
                 def one_part(index, inner):
-                    place(0, 2 * (1 - is_back) + index, position)
+                    place(2 * (1 - is_back) + index, position)
                     return inner
 
                 lax.fori_loop(0, 1 + is_back, one_part, 0)
 
             @pl.when(early & (step == positions - 1))
             def _():
-                scatter((LIGHT,))
+                scatter(LIGHT)
 
             return carry
 
         lax.fori_loop(0, 2 * positions, phase, 0)
 
-        @pl.when(early)
+    def landed(kind, position):
+        @pl.when(me >= last)
         def _():
-            scatter((GRADE,))
-
-        @pl.when(me >= last - 1)
-        def _():
-            def place_one(index, carry):
-                rest = lax.rem(index, 3 * positions)
-                place(index // (3 * positions), lax.rem(rest, 3), rest // 3)
-                return carry
-
-            lax.fori_loop(0, slots * 3 * positions, place_one, 0)
-            scatter((LIGHT, GRADE))
-
-    def margin_copy(slot, piece):
+            owner_copy(kind, 0, position).wait_recv()
+
+    @pl.when(me >= last - 1)
+    def _():
+        for position in range(positions):
+            landed(LIGHT, position)
+
+        def lights_in(position, carry):
+            place(2, position)
+            return carry
+
+        lax.fori_loop(0, positions, lights_in, 0)
+        scatter(LIGHT)
+
+        def grades_in(index, carry):
+            position, part = index // 2, lax.rem(index, 2)
+
+            @pl.when(part == 0)
+            def _():
+                landed(GRADE, position)
+
+            place(part, position)
+            return carry
+
+        lax.fori_loop(0, 2 * positions, grades_in, 0)
+
+    scatter(GRADE)
+
+    def margin_copy(piece):
         return pltpu.make_async_remote_copy(
-            src_ref=final.at[slot, :, :, pl.ds(own, share), :],
-            dst_ref=extra.at[slot, piece],
-            send_sem=send_m.at[slot],
-            recv_sem=recv_m.at[slot, piece],
+            src_ref=final.at[:, :, pl.ds(own, share), :],
+            dst_ref=extra.at[piece],
+            send_sem=send_m,
+            recv_sem=recv_m.at[piece],
             device_id=across(target),
             device_id_type=MESH_ID,
         )
 
-    def deliver(slot):
-        return pltpu.make_async_remote_copy(
-            src_ref=ratio.at[slot],
-            dst_ref=incoming,
-            send_sem=send_d.at[slot],
-            recv_sem=recv_d,
-            device_id={"cuts": lax.rem(me + 1 + slot * (me - last + 1), count)},
-            device_id_type=MESH_ID,
-        )
-
-    def start_margin(slot, carry):
-        margin_copy(slot, lax.rem(spot, 2)).start()
-        return carry
-
-    lax.fori_loop(0, slots, start_margin, 0)
-
-    def divide(slot, carry):
-        @pl.when(outer == 0)
-        def _():
-            extra[slot] = jnp.zeros(extra.shape[1:], extra.dtype)
-
-        @pl.when(outer == 1)
-        def _():
-            for piece in range(2):
-                margin_copy(slot, piece).wait_recv()
-
-        for side in range(2):
-            columns = slice(side * lanes_side, (side + 1) * lanes_side)
-            for piece in range(2):
-                lines = slice(piece * share, (piece + 1) * share)
-                full = final[slot, side, :, lines, :].astype(F32) + extra[slot, piece, side].astype(F32)
-                scale = 1.0 / (full[2] + 1.0)
-                for part in range(2):
-                    ratio[slot, part, lines, columns] = full[part] * scale
-
-        @pl.when((me == last) | (slot > 0))
-        def _():
-            deliver(slot).start()
-
-        return carry
-
-    lax.fori_loop(0, slots, divide, 0)
+    margin_copy(lax.rem(spot, 2)).start()
+
+    @pl.when(outer == 0)
+    def _():
+        extra[...] = jnp.zeros(extra.shape, extra.dtype)
+
     fetch_rows.wait()
 
-    @pl.when(me < last)
-    def _():
-        out[...] = rows_here[...] - ratio[0]
-
-    @pl.when(me >= last)
-    def _():
-        deliver(0).wait_recv()
-        out[...] = rows_here[...] - incoming[...]
+    @pl.when(outer == 1)
+    def _():
+        for piece in range(2):
+            margin_copy(piece).wait_recv()
+
+    for side in range(2):
+        columns = slice(side * lanes_side, (side + 1) * lanes_side)
+        for piece in range(2):
+            lines = slice(piece * share, (piece + 1) * share)
+            full = final[side, :, lines, :].astype(F32) + extra[piece, side].astype(F32)
+            scale = 1.0 / (full[2] + 1.0)
+            for part in range(2):
+                out[part, lines, columns] = rows_here[part, lines, columns] - full[part] * scale
 
     swap.wait_send()
     for step in range(1, members):
@@ -660,16 +673,14 @@
         for stage in range(2):
             both_sides(drain, kind, stage)
 
-    def finish_slot(slot, carry):
-        margin_copy(slot, lax.rem(spot, 2)).wait_send()
-
-        @pl.when((me == last) | (slot > 0))
+    margin_copy(lax.rem(spot, 2)).wait_send()
+
+    for slot in range(HOSTED):
+        @pl.when((me == last) | ((me == last - 1) & (slot > 0)))
         def _():
-            deliver(slot).wait_send()
-
-        return carry
-
-    lax.fori_loop(0, slots, finish_slot, 0)
+            for position in range(positions):
+                for kind in (LIGHT, GRADE):
+                    owner_copy(kind, slot, position).wait_send()
 
 
 def shards(probe_wave, fresnel_rows, fresnel_cols, object_slices, offsets, measured):
@@ -688,8 +699,8 @@
     lanes = width // 2
     dma = pltpu.SemaphoreType.DMA
     stack = (positions, chunks, size, pair)
-    block = (HOSTED, 2, 3 * ny, each, lanes)
-    small = (HOSTED, 2, 3, each, lanes)
+    block = (2, 3 * ny, each, lanes)
+    small = (2, 3, each, lanes)
     flags = (positions, chunks)
     anywhere = pl.BlockSpec(memory_space=pl.ANY)
     vmem = pl.BlockSpec(memory_space=pltpu.VMEM)
@@ -720,21 +731,19 @@
             VMEM((size, 2 * size), F32),
             VMEM((chunks, size, pair), BF),
             VMEM((chunks, size, pair), BF),
-            VMEM((HOSTED, positions, 3, size, size), BF),
-            VMEM((HOSTED, 2, nx, 3 * ny, each, lanes), BF),
+            VMEM((HOSTED + 1, positions, 3, size, size), BF),
+            VMEM((2, nx, 3 * ny, each, lanes), BF),
             VMEM(block, BF),
             VMEM(block, BF),
             VMEM(block, BF),
             VMEM(block, BF),
-            VMEM((HOSTED, 2, ny, 3, each, lanes), BF),
+            VMEM((2, ny, 3, each, lanes), BF),
             VMEM(small, BF),
             VMEM(small, BF),
             VMEM(small, BF),
             VMEM(small, BF),
             VMEM(small, BF),
-            VMEM((HOSTED, 2, 2, 3, share, lanes), BF),
-            VMEM((HOSTED, 2, own, width), F32),
-            VMEM((2, own, width), F32),
+            VMEM((2, 2, 3, share, lanes), BF),
             dma,
             dma,
             dma((count,)),
@@ -745,12 +754,12 @@
             dma(flags),
             dma((positions,)),
             dma((HOSTED, positions)),
-            dma((HOSTED, 2, 2, 2, 6)),
-            dma((HOSTED, 2, 2, 2, 6)),
-            dma((HOSTED,)),
-            dma((HOSTED, 2)),
-            dma((HOSTED,)),
+            dma((2, 2, 2, 6)),
+            dma((2, 2, 2, 6)),
             dma,
+            dma((2,)),
+            dma((HOSTED, positions, 2)),
+            dma((positions, 2)),
             dma((4,)),
         ],
         compiler_params=pltpu.CompilerParams(collective_id=0, has_side_effects=True, vmem_limit_bytes=67043328),

time: 194 us -> 194 us (level); the launches traced: 191 us -> 194 us
  Pallas kernels: 189 us -> 192 us
    pallas_call x1, Pallas kernels: 189 us -> 192 us  [shards(): pl.pallas_call(step_kernel, out_shape=jax.ShapeDtypeStruct((2, own, width...]
where the time goes in v5:
time: 194 us
  Pallas kernels  192 us (99%)
    pallas_call x1, Pallas kernels, shards(): pl.pallas_call(step_kernel, out_shape=jax.ShapeDtypeStruct((2, own, width...  192 us

profile of v5, /device:TPU:8, one launch (start us, length us, event | category | flops | bytes accessed | tf_op | source)
XLA Modules:
  0.0 193.6 jit_solution(17460650884603588738)
XLA Ops:
  0.0 192.0 %step.1 = f32[2,32,768]{2,1,0:T(8,128)} custom-call(s32[2,2]{1,0:T(2,128)} %bitcast.9, f32[2,512,768]{2,1,0:T(8,128)} %bitcast.5, bf16[2,512,512]{2,1,0:T(8,128)(2,1)} %probe.1, bf16[2,512,512]{2,1,0:T(8,128)(2,1)} %fresnel_cols.1, bf16[1024,512]{1,0:T(8,128)(2,1)} %bitcast.7, f32[2,512,512]{2,1,0:T(8,128)} %bitcast.6), custom_call_target="tpu_custom_call" | custom-call | tf_op jit(solution)/shard_map/step/pallas_call | solution.py:708
  192.0 1.6 copy.8

commit v6 on v5

--- a/solution.py
+++ b/solution.py
@@ -9,7 +9,7 @@
 MARGIN = 128
 LANES = 128
 HOSTED = 2
-LIGHT, GRADE = 0, 1
+LIGHT, GRADE, BORDER = 0, 1, 2
 PROBE = ("probe_0", "probe_1")
 TILE_PROBE = ("tile", "probe_0", "probe_1")
 MESH_ID = pl.DeviceIdType.MESH
@@ -19,9 +19,9 @@
 
 
 def step_kernel(
-    starts, owned, probe, fresnel_cols, forward_rows, measured,
+    starts, owned, probe_given, cols_given, rows_given, measured,
     out,
-    rows_here, edge_rows, mine, swapped, gathered, slab, tall, wide, amplitude_here,
+    probe, fresnel_cols, forward_rows, rows_here, edge_rows, mine, swapped, gathered, slab, tall, wide, amplitude_here,
     cuts, forward_cols, adjoint_cols, adjoint_rows,
     waves, cots, wave_out, cot_out, total, middle, backs,
     pieces, grids, pre, staged, got_up, got_down, partial, pre2, staged2, got_up2, got_down2,
@@ -104,6 +104,13 @@
 
     fetch_slab(0).start()
 
+    def fetch_given(index):
+        given, here = ((probe_given, probe), (cols_given, fresnel_cols), (rows_given, forward_rows))[index]
+        return pltpu.make_async_copy(given, here, local_sem.at[4 + index])
+
+    for index in range(3):
+        fetch_given(index).start()
+
     def fetch_measured():
         return pltpu.make_async_copy(measured, amplitude_here, local_sem.at[3])
 
@@ -118,11 +125,13 @@
     swap = pltpu.make_async_remote_copy(
         src_ref=mine, dst_ref=swapped, send_sem=send_z, recv_sem=recv_z, device_id={"tile": 1 - tile}, device_id_type=MESH_ID
     )
-    @pl.when(me == 0)
+    @pl.when((me == 0) | (me >= last))
     def _():
         swap.start()
 
     first_half, second_half = slice(0, half), slice(half, pair)
+    for index in range(3):
+        fetch_given(index).wait()
 
     @pl.when(me == 0)
     def _():
@@ -195,20 +204,23 @@
         for step in range(1, members):
             edge_copy(step, spot).start()
 
-    @pl.when(me > 0)
+    @pl.when((me > 0) & (me < last))
     def _():
         swap.start()
 
-    @pl.when(me == 0)
+    @pl.when((me == 0) | (me >= last))
     def _():
         share_edges()
 
     lax.fori_loop(0, 2 * positions, select, 0)
     lax.fori_loop(0, chunks, prepare_forward, 0)
 
+    @pl.when((me > 0) & (me < last))
+    def _():
+        share_edges()
+
     @pl.when(me > 0)
     def _():
-        share_edges()
         lax.fori_loop(0, chunks, prepare_adjoint, 0)
 
     gathered[spot] = swapped[...]
@@ -449,17 +461,20 @@
                 put(True)
 
     order = (("probe_0", "probe_1"), ("probe_1", "probe_0"))
-    parts_in = {LIGHT: (2,), GRADE: (0, 1)}
+    parts_in = {LIGHT: (2,), GRADE: (0, 1), BORDER: (0, 1)}
+    rows_in = {LIGHT: (0, each), GRADE: (0, own), BORDER: (own, share)}
 
     def regions(kind, stage):
         parts = parts_in[kind]
+        start, tall_rows = rows_in[kind]
         depth = len(parts) * (ny if stage == 0 else 1)
         first = parts[0] * (ny if stage == 0 else 1)
         if depth == 1:
-            cut = each // 3 * 2
-            return (pl.ds(first, 1), pl.ds(0, cut)), (pl.ds(first, 1), pl.ds(cut, each - cut))
+            cut = tall_rows // 3 * 2
+            return (pl.ds(first, 1), pl.ds(start, cut)), (pl.ds(first, 1), pl.ds(start + cut, tall_rows - cut))
         cut = depth // 2
-        return (pl.ds(first, cut), pl.ds(0, each)), (pl.ds(first + cut, depth - cut), pl.ds(0, each))
+        lines = pl.ds(start, tall_rows)
+        return (pl.ds(first, cut), lines), (pl.ds(first + cut, depth - cut), lines)
 
     def buffers(stage, side):
         if stage == 0:
@@ -520,15 +535,16 @@
         src, (_, _, up, down) = buffers(stage, side)
         for index in range(2, 6):
             make(index).wait_recv()
+        lines = pl.ds(*rows_in[kind])
         for part in parts_in[kind]:
-            if stage == 0:
-                for minor in range(ny):
-                    index = part * ny + minor
-                    summed = src[here, index].astype(F32) + up[index].astype(F32) + down[index].astype(F32)
-                    partial[side, minor, part] = summed.astype(BF)
-            else:
-                summed = src[here, part].astype(F32) + up[part].astype(F32) + down[part].astype(F32)
-                final[side, part] = summed.astype(BF)
+            for minor in range(ny if stage == 0 else 1):
+                index = part * ny + minor if stage == 0 else part
+                summed = src[here, index, lines].astype(F32) + up[index, lines].astype(F32)
+                summed = (summed + down[index, lines].astype(F32)).astype(BF)
+                if stage == 0:
+                    partial[side, minor, part, lines] = summed
+                else:
+                    final[side, part, lines] = summed
 
     def drain(kind, stage, side):
         make = ring(kind, stage, side)[0]
@@ -609,8 +625,6 @@
             return carry
 
         lax.fori_loop(0, 2 * positions, grades_in, 0)
-
-    scatter(GRADE)
 
     def margin_copy(piece):
         return pltpu.make_async_remote_copy(
@@ -622,7 +636,17 @@
             device_id_type=MESH_ID,
         )
 
+    for function in (begin, relay):
+        for kind in (BORDER, GRADE):
+            both_sides(function, kind, 0)
+    for kind in (BORDER, GRADE):
+        both_sides(settle, kind, 0)
+        both_sides(begin, kind, 1)
+    both_sides(relay, BORDER, 1)
+    both_sides(settle, BORDER, 1)
     margin_copy(lax.rem(spot, 2)).start()
+    both_sides(relay, GRADE, 1)
+    both_sides(settle, GRADE, 1)
 
     @pl.when(outer == 0)
     def _():
@@ -669,7 +693,7 @@
         for position in range(positions):
             window_copy(position, give_slot, give_to).wait_send()
 
-    for kind in (LIGHT, GRADE):
+    for kind in (LIGHT, GRADE, BORDER):
         for stage in range(2):
             both_sides(drain, kind, stage)
 
@@ -708,9 +732,12 @@
     updated = pl.pallas_call(
         step_kernel,
         out_shape=jax.ShapeDtypeStruct((2, own, width), F32),
-        in_specs=[pl.BlockSpec(memory_space=pltpu.SMEM), anywhere, vmem, vmem, vmem, anywhere],
+        in_specs=[pl.BlockSpec(memory_space=pltpu.SMEM)] + [anywhere] * 5,
         out_specs=vmem,
         scratch_shapes=[
+            VMEM((2, size, size), BF),
+            VMEM((2, size, size), BF),
+            VMEM((2 * size, size), BF),
             VMEM((2, own, width), F32),
             VMEM((2, share, width), F32),
             VMEM((2, share, width), BF),
@@ -754,13 +781,13 @@
             dma(flags),
             dma((positions,)),
             dma((HOSTED, positions)),
-            dma((2, 2, 2, 6)),
-            dma((2, 2, 2, 6)),
+            dma((3, 2, 2, 6)),
+            dma((3, 2, 2, 6)),
             dma,
             dma((2,)),
             dma((HOSTED, positions, 2)),
             dma((positions, 2)),
-            dma((4,)),
+            dma((7,)),
         ],
         compiler_params=pltpu.CompilerParams(collective_id=0, has_side_effects=True, vmem_limit_bytes=67043328),
         name="step",

time: 194 us -> 190 us (0.979)
  Pallas kernels: 192 us -> 188 us
    pallas_call x1, Pallas kernels: 192 us -> 188 us  [shards(): pl.pallas_call(step_kernel, out_shape=jax.ShapeDtypeStruct((2, own, width...]
where the time goes in v6:
time: 190 us
  Pallas kernels  188 us (99%)
    pallas_call x1, Pallas kernels, shards(): pl.pallas_call(step_kernel, out_shape=jax.ShapeDtypeStruct((2, own, width...  188 us

profile of v6, /device:TPU:8, one launch (start us, length us, event | category | flops | bytes accessed | tf_op | source)
XLA Modules:
  0.0 189.9 jit_solution(8474143966158929347)
XLA Ops:
  0.0 188.3 %step.1 = f32[2,32,768]{2,1,0:T(8,128)} custom-call(s32[2,2]{1,0:T(2,128)} %bitcast.9, f32[2,512,768]{2,1,0:T(8,128)} %bitcast.5, bf16[2,512,512]{2,1,0:T(8,128)(2,1)} %probe_given.1, bf16[2,512,512]{2,1,0:T(8,128)(2,1)} %cols_given.1, bf16[1024,512]{1,0:T(8,128)(2,1)} %bitcast.7, f32[2,512,512]{2,1,0:T(8,128)} %bitcast.6), custom_call_target="tpu_custom_call" | custom-call | tf_op jit(solution)/shard_map/step/pallas_call | solution.py:732
  188.3 1.6 copy.8

commit v7 on v6

--- a/solution.py
+++ b/solution.py
@@ -21,14 +21,14 @@
 def step_kernel(
     starts, owned, probe_given, cols_given, rows_given, measured,
     out,
-    probe, fresnel_cols, forward_rows, rows_here, edge_rows, mine, swapped, gathered, slab, tall, wide, amplitude_here,
+    fresnel_cols, forward_rows, rows_here, edge_rows, mine, swapped, gathered, slab, tall, wide, amplitude_here,
     cuts, forward_cols, adjoint_cols, adjoint_rows,
-    waves, cots, wave_out, cot_out, total, middle, backs,
+    waves, cots, wave_out, cot_out, total, middle, lent_backs,
     pieces, grids, pre, staged, got_up, got_down, partial, pre2, staged2, got_up2, got_down2,
     final, extra,
     send_z, recv_z, send_e, recv_e,
     send_f, recv_f, send_b, recv_b, send_w, recv_w,
-    send_r, recv_r, send_m, recv_m, send_p, recv_p, local_sem,
+    send_r, recv_r, send_m, recv_m, send_p, recv_p, send_g, recv_g, local_sem,
 ):
     tile = lax.axis_index("tile")
     where = {"probe_0": lax.axis_index("probe_0"), "probe_1": lax.axis_index("probe_1")}
@@ -44,6 +44,10 @@
     _, positions, chunks, size, pair = cuts.shape
     half = pair // 2
     hosted = 1 + me // (last - 1)
+    host = last - 1
+    lender = (me == host - 1) | (me == host - 2)
+    extra_slots = 2 * (me // host) * (1 - me // last)
+    before = left - 2 * (me // host) * (1 - me // last)
     owner_slot = HOSTED * (me // last)
     _, rows, width = owned.shape
     share = mine.shape[1]
@@ -84,6 +88,15 @@
     @pl.when(me == count - 1)
     def _():
         greet({"cuts": last})
+
+    @pl.when((me == host - 2) | (me == host - 3))
+    def _():
+        greet({"cuts": host})
+
+    @pl.when(me == host)
+    def _():
+        for step in (2, 3):
+            greet({"cuts": host - step})
 
     @pl.when(outer == 1)
     def _():
@@ -105,22 +118,30 @@
     fetch_slab(0).start()
 
     def fetch_given(index):
-        given, here = ((probe_given, probe), (cols_given, fresnel_cols), (rows_given, forward_rows))[index]
+        given, here = ((probe_given, pieces.at[0, 0, pl.ds(0, 2)]), (cols_given, fresnel_cols), (rows_given, forward_rows))[index]
         return pltpu.make_async_copy(given, here, local_sem.at[4 + index])
 
     for index in range(3):
         fetch_given(index).start()
 
-    def fetch_measured():
-        return pltpu.make_async_copy(measured, amplitude_here, local_sem.at[3])
-
-    @pl.when(me == last)
-    def _():
-        fetch_measured().start()
+    def fetch_measured(position):
+        return pltpu.make_async_copy(measured.at[position], amplitude_here, local_sem.at[3])
 
     fetch_edge.wait()
     mine[...] = edge_rows[...].astype(BF)
-    pl.semaphore_wait(barrier, members + 3 + (me + 1) // count + (me // last) * (1 - me // (last + 1)))
+    one_more = (me == last) | (me == count - 1) | (me == host - 2) | (me == host - 3)
+
+    @pl.when(me == host)
+    def _():
+        pl.semaphore_wait(barrier, members + 5)
+
+    @pl.when(one_more)
+    def _():
+        pl.semaphore_wait(barrier, members + 4)
+
+    @pl.when((me == 0) | (me == host - 1) | (me == last + 1))
+    def _():
+        pl.semaphore_wait(barrier, members + 3)
 
     swap = pltpu.make_async_remote_copy(
         src_ref=mine, dst_ref=swapped, send_sem=send_z, recv_sem=recv_z, device_id={"tile": 1 - tile}, device_id_type=MESH_ID
@@ -138,8 +159,8 @@
         for position in range(positions):
             for chunk in range(chunks):
                 lanes = slice(chunk * half, (chunk + 1) * half)
-                waves[0, position, chunk, :, first_half] = probe[0, :, lanes]
-                waves[0, position, chunk, :, second_half] = probe[1, :, lanes]
+                waves[0, position, chunk, :, first_half] = pieces[0, 0, 0, :, lanes]
+                waves[0, position, chunk, :, second_half] = pieces[0, 0, 1, :, lanes]
 
     def turned(value):
         return value.astype(F32).T.astype(BF)
@@ -256,15 +277,29 @@
     give_slot = 1 - lax.rem(me + 1, 2) * (me // (last + 1))
     give_to = last - 1 + me // (last + 1)
 
+    def lend(position):
+        slot = HOSTED + lax.rem(me, 2)
+        return pltpu.make_async_remote_copy(
+            src_ref=cuts.at[0, position],
+            dst_ref=cuts.at[slot, position],
+            send_sem=send_w.at[position],
+            recv_sem=recv_w.at[slot, position],
+            device_id={"cuts": host},
+            device_id_type=MESH_ID,
+        )
+
+    @pl.when(lender)
+    def _():
+        for position in range(positions):
+            cut_window(position)
+            cuts[0, position] = wave_out[position]
+        lend(0).start()
+
     @pl.when(me >= last)
     def _():
         for position in range(positions):
             cut_window(position)
             window_copy(position, give_slot, give_to).start()
-
-    @pl.when(me == last)
-    def _():
-        fetch_measured().wait()
 
     def forward_copy(position, chunk):
         return pltpu.make_async_remote_copy(
@@ -282,7 +317,7 @@
             dst_ref=cots.at[position, chunk],
             send_sem=send_b.at[position, chunk],
             recv_sem=recv_b.at[position, chunk],
-            device_id={"cuts": left},
+            device_id={"cuts": before},
             device_id_type=MESH_ID,
         )
 
@@ -321,10 +356,14 @@
             owner_copy(kind, slot, position).start()
 
     def forward(position):
-        @pl.when(me < last)
+        @pl.when((me < host - 2) | (me == host))
         def _():
             cut_window(position)
             cuts[0, position] = wave_out[position]
+
+        @pl.when(me == last)
+        def _():
+            fetch_measured(position).start()
 
         def hosted_slice(slot, carry):
             @pl.when((me >= last) | (slot > 0))
@@ -340,6 +379,10 @@
                 win_r, win_i = parts_of(cuts[slot, position, chunk])
                 out = both(wave_r * win_r - wave_i * win_i, wave_r * win_i + wave_i * win_r).astype(BF)
                 add_product(chunk, out, forward_cols[chunk])
+
+            @pl.when((me == last) & (slot == hosted - 1))
+            def _():
+                fetch_measured(position).wait()
 
             def produce(chunk, inner):
                 result = jnp.dot(forward_rows[...], middle[chunk], preferred_element_type=F32)
@@ -361,7 +404,7 @@
                     @pl.when(me == last)
                     def _():
                         psi_r, psi_i = parts_of(value)
-                        amplitude = amplitude_here[position, :, pl.ds(pl.multiple_of(chunk * half, half), half)]
+                        amplitude = amplitude_here[:, pl.ds(pl.multiple_of(chunk * half, half), half)]
                         factor = 1.0 - amplitude * lax.rsqrt(psi_r * psi_r + psi_i * psi_i + 1.0)
                         cots[position, chunk] = both(psi_r * factor, psi_i * factor).astype(BF)
 
@@ -381,9 +424,43 @@
 
         lax.fori_loop(0, hosted, hosted_slice, 0)
 
+    def grade_all(position, slot):
+        def grade(chunk, inner):
+            wave_r, wave_i = parts_of(waves[slot, position, chunk])
+            back_r, back_i = parts_of(middle[chunk])
+            lanes = pl.ds(pl.multiple_of(chunk * half, half), half)
+            pieces[slot, position, 0, :, lanes] = (wave_r * back_r + wave_i * back_i).astype(BF)
+            pieces[slot, position, 1, :, lanes] = (wave_r * back_i - wave_i * back_r).astype(BF)
+            return inner
+
+        lax.fori_loop(0, chunks, grade, 0)
+
+    def return_back(position, which):
+        return pltpu.make_async_remote_copy(
+            src_ref=lent_backs.at[which, position],
+            dst_ref=cots.at[position],
+            send_sem=send_g.at[which, position],
+            recv_sem=recv_g.at[position],
+            device_id={"cuts": host - 2 + which},
+            device_id_type=MESH_ID,
+        )
+
     def adjoint(position):
         def hosted_slice(step, carry):
-            slot = hosted - 1 - step
+            foreign = step // hosted
+            slot = (hosted - 1 - step) * (1 - foreign) + (2 * HOSTED + 1 - step) * foreign
+
+            @pl.when(foreign > 0)
+            def _():
+                pltpu.make_async_remote_copy(
+                    src_ref=cuts.at[0, position],
+                    dst_ref=cuts.at[slot, position],
+                    send_sem=send_w.at[position],
+                    recv_sem=recv_w.at[slot, position],
+                    device_id={"cuts": host - 1},
+                    device_id_type=MESH_ID,
+                ).wait_recv()
+
             for chunk in range(chunks):
                 @pl.when((me < last) & (step == 0))
                 def _():
@@ -396,7 +473,14 @@
                 real = result[:size, :half] + result[size:, half:]
                 imag = result[:size, half:] - result[size:, :half]
                 back = both(real, imag).astype(BF)
-                backs[chunk] = back
+
+                @pl.when(foreign == 0)
+                def _():
+                    middle[chunk] = back
+
+                @pl.when(foreign > 0)
+                def _():
+                    lent_backs[slot - HOSTED, position, chunk] = back
 
                 @pl.when(me > 0)
                 def _():
@@ -404,11 +488,11 @@
                     win_r, win_i = parts_of(cuts[slot, position, chunk])
                     value = both(win_r * back_r + win_i * back_i, win_r * back_i - win_i * back_r).astype(BF)
 
-                    @pl.when(slot > 0)
+                    @pl.when(step < hosted + extra_slots - 1)
                     def _():
                         cots[position, chunk] = value
 
-                    @pl.when(slot == 0)
+                    @pl.when(step == hosted + extra_slots - 1)
                     def _():
                         cot_out[position, chunk] = value
                         adjoint_copy(position, chunk).start()
@@ -417,19 +501,14 @@
 
             lax.fori_loop(0, chunks, produce, 0)
 
-            def grade(chunk, inner):
-                wave_r, wave_i = parts_of(waves[slot, position, chunk])
-                back_r, back_i = parts_of(backs[chunk])
-                lanes = pl.ds(pl.multiple_of(chunk * half, half), half)
-                pieces[slot, position, 0, :, lanes] = (wave_r * back_r + wave_i * back_i).astype(BF)
-                pieces[slot, position, 1, :, lanes] = (wave_r * back_i - wave_i * back_r).astype(BF)
-                return inner
-
-            lax.fori_loop(0, chunks, grade, 0)
-            send_to_owner(GRADE, slot, position)
+            @pl.when(foreign == 0)
+            def _():
+                grade_all(position, lax.rem(slot, HOSTED))
+                send_to_owner(GRADE, lax.rem(slot, HOSTED), position)
+
             return carry
 
-        lax.fori_loop(0, hosted, hosted_slice, 0)
+        lax.fori_loop(0, hosted + extra_slots, hosted_slice, 0)
 
 
     def place(part, position):
@@ -577,9 +656,16 @@
             def _():
                 forward(position)
 
-            @pl.when(is_back == 1)
+            @pl.when((is_back == 1) & ((me < host - 2) | (me >= host)))
             def _():
                 adjoint(position)
+
+            @pl.when((is_back == 1) & lender)
+            def _():
+                return_back(position, 0).wait_recv()
+                for chunk in range(chunks):
+                    middle[chunk] = cots[position, chunk]
+                grade_all(position, 0)
 
             @pl.when(early)
             def _():
@@ -589,6 +675,11 @@
 
                 lax.fori_loop(0, 1 + is_back, one_part, 0)
 
+            @pl.when(lender & (step == positions - 1))
+            def _():
+                for late_position in range(1, positions):
+                    lend(late_position).start()
+
             @pl.when(early & (step == positions - 1))
             def _():
                 scatter(LIGHT)
@@ -596,6 +687,12 @@
             return carry
 
         lax.fori_loop(0, 2 * positions, phase, 0)
+
+        @pl.when(me == host)
+        def _():
+            for position in range(positions):
+                for which in range(2):
+                    return_back(position, which).start()
 
     def landed(kind, position):
         @pl.when(me >= last)
@@ -680,7 +777,7 @@
         def _():
             forward_copy(position, chunk).wait_send()
 
-        @pl.when((me > 0) & (me <= last))
+        @pl.when((me > 0) & (me <= last) & ((me < host - 2) | (me >= host)))
         def _():
             adjoint_copy(position, chunk).wait_send()
 
@@ -692,6 +789,17 @@
     def _():
         for position in range(positions):
             window_copy(position, give_slot, give_to).wait_send()
+
+    @pl.when(lender)
+    def _():
+        for position in range(positions):
+            lend(position).wait_send()
+
+    @pl.when(me == host)
+    def _():
+        for position in range(positions):
+            for which in range(2):
+                return_back(position, which).wait_send()
 
     for kind in (LIGHT, GRADE, BORDER):
         for stage in range(2):
@@ -736,7 +844,6 @@
         out_specs=vmem,
         scratch_shapes=[
             VMEM((2, size, size), BF),
-            VMEM((2, size, size), BF),
             VMEM((2 * size, size), BF),
             VMEM((2, own, width), F32),
             VMEM((2, share, width), F32),
@@ -746,8 +853,8 @@
             VMEM((2, rows + 2 * MARGIN, width), BF),
             VMEM((positions, 2, width, size), BF),
             VMEM((positions, 2, size, width), BF),
-            VMEM((positions, size, size), F32),
-            VMEM((HOSTED, *stack), BF),
+            VMEM((size, size), F32),
+            VMEM((2 * HOSTED, *stack), BF),
             VMEM((chunks, pair, 2 * size), BF),
             VMEM((chunks, pair, 2 * size), BF),
             VMEM((2 * size, size), BF),
@@ -757,7 +864,7 @@
             VMEM(stack, BF),
             VMEM((size, 2 * size), F32),
             VMEM((chunks, size, pair), BF),
-            VMEM((chunks, size, pair), BF),
+            VMEM((2, *stack), BF),
             VMEM((HOSTED + 1, positions, 3, size, size), BF),
             VMEM((2, nx, 3 * ny, each, lanes), BF),
             VMEM(block, BF),
@@ -780,13 +887,15 @@
             dma(flags),
             dma(flags),
             dma((positions,)),
-            dma((HOSTED, positions)),
+            dma((2 * HOSTED, positions)),
             dma((3, 2, 2, 6)),
             dma((3, 2, 2, 6)),
             dma,
             dma((2,)),
             dma((HOSTED, positions, 2)),
             dma((positions, 2)),
+            dma((2, positions)),
+            dma((positions,)),
             dma((7,)),
         ],
         compiler_params=pltpu.CompilerParams(collective_id=0, has_side_effects=True, vmem_limit_bytes=67043328),

time: 190 us -> 223 us (1.17)
  the two profiles are of different devices: /device:TPU:8 before, /device:TPU:41 now
where the time goes in v7:
time: 223 us
  Pallas kernels  221 us (99%)
    pallas_call x1, Pallas kernels, shards(): pl.pallas_call(step_kernel, out_shape=jax.ShapeDtypeStruct((2, own, width...  221 us

profile of v7, /device:TPU:41, one launch (start us, length us, event | category | flops | bytes accessed | tf_op | source)
XLA Modules:
  0.0 222.6 jit_solution(9202626582791474564)
XLA Ops:
  0.0 221.0 %step.1 = f32[2,32,768]{2,1,0:T(8,128)} custom-call(s32[2,2]{1,0:T(2,128)} %bitcast.9, f32[2,512,768]{2,1,0:T(8,128)} %bitcast.5, bf16[2,512,512]{2,1,0:T(8,128)(2,1)} %probe_given.1, bf16[2,512,512]{2,1,0:T(8,128)(2,1)} %cols_given.1, bf16[1024,512]{1,0:T(8,128)(2,1)} %bitcast.7, f32[2,512,512]{2,1,0:T(8,128)} %bitcast.6), custom_call_target="tpu_custom_call" | custom-call | tf_op jit(solution)/shard_map/step/pallas_call | solution.py:840
  221.0 1.6 copy.8
